TPU v7x, 32 devices: a whole 2x2x4 slice. The times are simulated.
32 devices in a mesh: dp: 2 (over x), tp: 4 (over z), pp: 4 (over y, core).
Axes of the slice: x: 2, y: 2, z: 4, core: 2. Of those that a mesh axis runs over, the one named last changes fastest.
Arguments:
- x_in: bfloat16 [2, 2, 2048, 512], P(None, 'dp'), parts along dimension 1
- dy_out: bfloat16 [2, 2, 2048, 512], P(None, 'dp'), parts along dimension 1
- w_qkv: bfloat16 [4, 3, 512, 8, 64], P('pp', None, None, 'tp')
- b_qkv: bfloat16 [4, 3, 8, 64], P('pp', None, 'tp')
- w_out: bfloat16 [4, 8, 64, 512], P('pp', 'tp')
- b_out: bfloat16 [4, 512], P('pp')
- ln_par: bfloat16 [4, 4, 512], P('pp')
- w_fc1: bfloat16 [4, 512, 2048], P('pp', None, 'tp')
- b_fc1: bfloat16 [4, 2048], P('pp', 'tp')
- w_fc2: bfloat16 [4, 2048, 512], P('pp', 'tp')
- b_fc2: bfloat16 [4, 512], P('pp')
Outputs:
- output 1: bfloat16 [4, 2, 2, 2048, 512], P('pp', None, 'dp'), parts along dimension 2
- output 2: bfloat16 [4, 2, 2, 2048, 512], P('pp', None, 'dp'), parts along dimension 2
- output 3: float32 [8, 3, 512, 8, 64], P(('dp', 'pp'), None, None, 'tp'), parts along dimension 0
- output 4: float32 [8, 3, 8, 64], P(('dp', 'pp'), None, 'tp'), parts along dimension 0
- output 5: float32 [8, 8, 64, 512], P(('dp', 'pp'), 'tp'), parts along dimension 0
- output 6: float32 [8, 512], P(('dp', 'pp')), parts along dimension 0
- output 7: float32 [8, 4, 512], P(('dp', 'pp')), parts along dimension 0
- output 8: float32 [8, 512, 2048], P(('dp', 'pp'), None, 'tp'), parts along dimension 0
- output 9: float32 [8, 2048], P(('dp', 'pp'), 'tp'), parts along dimension 0
- output 10: float32 [8, 2048, 512], P(('dp', 'pp'), 'tp'), parts along dimension 0
- output 11: float32 [8, 512], P(('dp', 'pp')), parts along dimension 0
There are 2 independent parts. A program takes and returns all parts, laid end to end along the dimension named above; an argument that names none is the same for every part.
All inputs are finite; a program needn't handle non-finite values.
Results may differ from a plain program's by a relative error of at most 0.02.
Values are sent between devices in bfloat16 or wider.
A program may use at most 1 GiB of HBM per device.

v0:
```python
import jax
import jax.numpy as jnp
from jax import lax
from jax.sharding import PartitionSpec as P

LN_EPS = 1e-5


def layer_norm(x_act, ln_gain, ln_shift):
    x_wide = x_act.astype(jnp.float32)
    row_mean = jnp.mean(x_wide, axis=-1, keepdims=True)
    centered = x_wide - row_mean
    row_var = jnp.mean(centered * centered, axis=-1, keepdims=True)
    normed = centered * lax.rsqrt(row_var + LN_EPS)
    return (normed * ln_gain + ln_shift).astype(jnp.bfloat16)


def causal_attention(q_heads, k_heads, v_heads):
    head_dim = q_heads.shape[-1]
    seq_len = q_heads.shape[1]
    scores = jnp.einsum("bqhe,bkhe->bhqk", q_heads, k_heads, preferred_element_type=jnp.float32) * (head_dim ** -0.5)
    row_pos = lax.broadcasted_iota(jnp.int32, (seq_len, seq_len), 0)
    col_pos = lax.broadcasted_iota(jnp.int32, (seq_len, seq_len), 1)
    scores = jnp.where(row_pos >= col_pos, scores, -1e30)
    attn_probs = jax.nn.softmax(scores, axis=-1).astype(jnp.bfloat16)
    attn_mix = jnp.einsum("bhqk,bkhe->bqhe", attn_probs, v_heads, preferred_element_type=jnp.float32)
    return attn_mix.astype(jnp.bfloat16)


def gelu_tanh(pre_act):
    return jax.nn.gelu(pre_act, approximate=True)


def layer_forward(x_act, layer_w):
    w_qkv, b_qkv, w_out, b_out, ln_par, w_fc1, b_fc1, w_fc2, b_fc2 = layer_w
    ln_wide = ln_par.astype(jnp.float32)
    h_one = layer_norm(x_act, ln_wide[0], ln_wide[1])
    qkv_all = (jnp.einsum("bsd,cdhe->bsche", h_one, w_qkv, preferred_element_type=jnp.float32) + b_qkv.astype(jnp.float32)).astype(jnp.bfloat16)
    attn_mix = causal_attention(qkv_all[:, :, 0], qkv_all[:, :, 1], qkv_all[:, :, 2])
    attn_part = jnp.einsum("bshe,hed->bsd", attn_mix, w_out, preferred_element_type=jnp.float32).astype(jnp.bfloat16)
    attn_sum = lax.psum(attn_part, "tp")
    x_mid = (x_act.astype(jnp.float32) + attn_sum.astype(jnp.float32) + b_out.astype(jnp.float32)).astype(jnp.bfloat16)
    h_two = layer_norm(x_mid, ln_wide[2], ln_wide[3])
    pre_act = jnp.einsum("bsd,df->bsf", h_two, w_fc1, preferred_element_type=jnp.float32) + b_fc1.astype(jnp.float32)
    gelu_out = gelu_tanh(pre_act).astype(jnp.bfloat16)
    mlp_part = jnp.einsum("bsf,fd->bsd", gelu_out, w_fc2, preferred_element_type=jnp.float32).astype(jnp.bfloat16)
    mlp_sum = lax.psum(mlp_part, "tp")
    y_act = (x_mid.astype(jnp.float32) + mlp_sum.astype(jnp.float32) + b_fc2.astype(jnp.float32)).astype(jnp.bfloat16)
    return y_act, qkv_all, x_mid, pre_act


def layer_backward(grad_out, x_act, qkv_all, x_mid, pre_act, layer_w):
    w_qkv = layer_w[0]
    w_out = layer_w[2]
    ln_wide = layer_w[4].astype(jnp.float32)
    w_fc1 = layer_w[5]
    w_fc2 = layer_w[7]
    grad_wide = grad_out.astype(jnp.float32)
    g_b_fc2 = jnp.sum(grad_wide, axis=(0, 1))
    gelu_wide, gelu_pull = jax.vjp(gelu_tanh, pre_act)
    gelu_out = gelu_wide.astype(jnp.bfloat16)
    g_w_fc2 = jnp.einsum("bsf,bsd->fd", gelu_out, grad_out, preferred_element_type=jnp.float32)
    g_gelu = jnp.einsum("bsd,fd->bsf", grad_out, w_fc2, preferred_element_type=jnp.float32).astype(jnp.bfloat16)
    g_pre = gelu_pull(g_gelu.astype(jnp.float32))[0]
    g_b_fc1 = jnp.sum(g_pre, axis=(0, 1))
    g_pre_half = g_pre.astype(jnp.bfloat16)
    h_two, ln_two_pull = jax.vjp(layer_norm, x_mid, ln_wide[2], ln_wide[3])
    g_w_fc1 = jnp.einsum("bsd,bsf->df", h_two, g_pre_half, preferred_element_type=jnp.float32)
    g_h_two = lax.psum(jnp.einsum("bsf,df->bsd", g_pre_half, w_fc1, preferred_element_type=jnp.float32).astype(jnp.bfloat16), "tp")
    g_mid_ln, g_gain_two, g_shift_two = ln_two_pull(g_h_two)
    g_mid_wide = grad_wide + g_mid_ln.astype(jnp.float32)
    g_mid = g_mid_wide.astype(jnp.bfloat16)
    g_b_out = jnp.sum(g_mid_wide, axis=(0, 1))
    attn_mix, attn_pull = jax.vjp(causal_attention, qkv_all[:, :, 0], qkv_all[:, :, 1], qkv_all[:, :, 2])
    g_w_out = jnp.einsum("bshe,bsd->hed", attn_mix, g_mid, preferred_element_type=jnp.float32)
    g_mix = jnp.einsum("bsd,hed->bshe", g_mid, w_out, preferred_element_type=jnp.float32).astype(jnp.bfloat16)
    g_query, g_key, g_value = attn_pull(g_mix)
    g_qkv = jnp.stack([g_query, g_key, g_value], axis=2)
    g_b_qkv = jnp.sum(g_qkv.astype(jnp.float32), axis=(0, 1))
    h_one, ln_one_pull = jax.vjp(layer_norm, x_act, ln_wide[0], ln_wide[1])
    g_w_qkv = jnp.einsum("bsd,bsche->cdhe", h_one, g_qkv, preferred_element_type=jnp.float32)
    g_h_one = lax.psum(jnp.einsum("bsche,cdhe->bsd", g_qkv, w_qkv, preferred_element_type=jnp.float32).astype(jnp.bfloat16), "tp")
    g_in_ln, g_gain_one, g_shift_one = ln_one_pull(g_h_one)
    grad_in = (g_mid_wide + g_in_ln.astype(jnp.float32)).astype(jnp.bfloat16)
    g_ln = jnp.stack([g_gain_one, g_shift_one, g_gain_two, g_shift_two])
    return grad_in, (g_w_qkv, g_b_qkv, g_w_out, g_b_out, g_ln, g_w_fc1, g_b_fc1, g_w_fc2, g_b_fc2)


def solution(mesh):
    stages = mesh.shape["pp"]
    tp_size = mesh.shape["tp"]
    fwd_pairs = [(src_idx, src_idx + 1) for src_idx in range(stages - 1)]
    back_pairs = [(src_idx + 1, src_idx) for src_idx in range(stages - 1)]

    def pass_on(boundary, stage_pairs):
        seq_part = boundary.shape[1] // tp_size
        own_part = lax.dynamic_slice_in_dim(boundary, lax.axis_index("tp") * seq_part, seq_part, axis=1)
        moved_part = lax.ppermute(own_part, "pp", stage_pairs)
        return lax.all_gather(moved_part, "tp", axis=1, tiled=True)

    def stage_program(x_in, dy_out, w_qkv, b_qkv, w_out, b_out, ln_par, w_fc1, b_fc1, w_fc2, b_fc2):
        layer_w = (w_qkv[0], b_qkv[0], w_out[0], b_out[0], ln_par[0], w_fc1[0], b_fc1[0], w_fc2[0], b_fc2[0])
        micro_count, batch_rows, seq_len, d_model = x_in.shape
        local_heads = w_qkv.shape[3]
        head_dim = w_qkv.shape[4]
        ff_local = w_fc1.shape[2]
        stage_idx = lax.axis_index("pp")
        last_stage = stages - 1
        step_count = micro_count + stages - 1
        act_shape = (batch_rows, seq_len, d_model)
        buf_len = micro_count + 1

        def fwd_step(fwd_carry, step_idx):
            received, x_buf, qkv_buf, mid_buf, pre_buf, out_buf = fwd_carry
            micro_idx = step_idx - stage_idx
            is_valid = (micro_idx >= 0) & (micro_idx < micro_count)
            read_idx = jnp.clip(micro_idx, 0, micro_count - 1)
            write_idx = jnp.where(is_valid, micro_idx, micro_count)
            x_first = lax.dynamic_index_in_dim(x_in, read_idx, 0, keepdims=False)
            x_act = jnp.where(stage_idx == 0, x_first, received)
            y_act, qkv_all, x_mid, pre_act = layer_forward(x_act, layer_w)
            x_buf = lax.dynamic_update_index_in_dim(x_buf, x_act, write_idx, 0)
            qkv_buf = lax.dynamic_update_index_in_dim(qkv_buf, qkv_all, write_idx, 0)
            mid_buf = lax.dynamic_update_index_in_dim(mid_buf, x_mid, write_idx, 0)
            pre_buf = lax.dynamic_update_index_in_dim(pre_buf, pre_act, write_idx, 0)
            out_buf = lax.dynamic_update_index_in_dim(out_buf, y_act, write_idx, 0)
            received = pass_on(y_act, fwd_pairs)
            return (received, x_buf, qkv_buf, mid_buf, pre_buf, out_buf), None

        fwd_init = (jnp.zeros(act_shape, jnp.bfloat16),
                    jnp.zeros((buf_len,) + act_shape, jnp.bfloat16),
                    jnp.zeros((buf_len, batch_rows, seq_len, 3, local_heads, head_dim), jnp.bfloat16),
                    jnp.zeros((buf_len,) + act_shape, jnp.bfloat16),
                    jnp.zeros((buf_len, batch_rows, seq_len, ff_local), jnp.float32),
                    jnp.zeros((buf_len,) + act_shape, jnp.bfloat16))
        fwd_final, _ = lax.scan(fwd_step, fwd_init, jnp.arange(step_count))
        _, x_buf, qkv_buf, mid_buf, pre_buf, out_buf = fwd_final

        def bwd_step(bwd_carry, step_idx):
            received, grad_acc, grad_buf = bwd_carry
            micro_idx = micro_count + last_stage - 1 - stage_idx - step_idx
            is_valid = (micro_idx >= 0) & (micro_idx < micro_count)
            read_idx = jnp.clip(micro_idx, 0, micro_count - 1)
            write_idx = jnp.where(is_valid, micro_idx, micro_count)
            dy_last = lax.dynamic_index_in_dim(dy_out, read_idx, 0, keepdims=False)
            grad_out = jnp.where(stage_idx == last_stage, dy_last, received)
            grad_out = jnp.where(is_valid, grad_out, jnp.zeros_like(grad_out))
            x_act = lax.dynamic_index_in_dim(x_buf, read_idx, 0, keepdims=False)
            qkv_all = lax.dynamic_index_in_dim(qkv_buf, read_idx, 0, keepdims=False)
            x_mid = lax.dynamic_index_in_dim(mid_buf, read_idx, 0, keepdims=False)
            pre_act = lax.dynamic_index_in_dim(pre_buf, read_idx, 0, keepdims=False)
            grad_in, layer_grads = layer_backward(grad_out, x_act, qkv_all, x_mid, pre_act, layer_w)
            grad_acc = tuple(acc_item + new_item for acc_item, new_item in zip(grad_acc, layer_grads))
            grad_buf = lax.dynamic_update_index_in_dim(grad_buf, grad_in, write_idx, 0)
            received = pass_on(grad_in, back_pairs)
            return (received, grad_acc, grad_buf), None

        grad_init = tuple(jnp.zeros(w_item.shape, jnp.float32) for w_item in layer_w)
        bwd_init = (jnp.zeros(act_shape, jnp.bfloat16), grad_init, jnp.zeros((buf_len,) + act_shape, jnp.bfloat16))
        bwd_final, _ = lax.scan(bwd_step, bwd_init, jnp.arange(step_count))
        _, grad_sum, grad_buf = bwd_final
        return (out_buf[:micro_count][None], grad_buf[:micro_count][None]) + tuple(g_item[None] for g_item in grad_sum)

    act_spec = P(None, "dp", None, None)
    arg_specs = (act_spec, act_spec,
                 P("pp", None, None, "tp", None), P("pp", None, "tp", None), P("pp", "tp", None, None),
                 P("pp", None), P("pp", None, None), P("pp", None, "tp"), P("pp", "tp"),
                 P("pp", "tp", None), P("pp", None))
    stage_spec = P("pp", None, "dp", None, None)
    grad_axes = ("dp", "pp")
    result_specs = (stage_spec, stage_spec,
                    P(grad_axes, None, None, "tp", None), P(grad_axes, None, "tp", None), P(grad_axes, "tp", None, None),
                    P(grad_axes, None), P(grad_axes, None, None), P(grad_axes, None, "tp"), P(grad_axes, "tp"),
                    P(grad_axes, "tp", None), P(grad_axes, None))
    return jax.shard_map(stage_program, mesh=mesh, in_specs=arg_specs, out_specs=result_specs, check_vma=False)
```

profile of v0, /device:TPU:0, one launch (start us, length us, event | category | flops | bytes accessed | tf_op | source)
XLA Modules:
  0.0 3231.6 jit_solution(2748766742047812934)
XLA Ops:
  29.8 1466.2 %while.54 = (s32[]{:T(128)}, bf16[1,2048,512]{2,1,0:T(8,128)(2,1)}, bf16[3,1,2048,512]{3,2,1,0:T(8,128)(2,1)}, bf16[3,1,2048,3,2,64]{2,5,4,3,1,0:T(8,128)(2,1)},...) while((s32[]{:T(128)}, bf16[1,2048,512]{2,1,0:T(8,128)(2,1)}, ...), condition=%wide.region_9.10_spmd, body=%wide.region_0.9_spmd.sunk | while | flops 5479079936 | bytes 206274000 | solution.py:136
  44.6 18.7 fusion.282
  63.3 12.2 fusion.283
  78.5 89.0 %all-reduce.5.cloned.1.call-done = bf16[1,2048,512]{2,1,0:T(8,128)(2,1)} async-done(((bf16[1,2048,512]{2,1,0:T(8,128)(2,1)}), bf16[1,2048,512]{2,1,0:T(8,128)(2,1)}) %all-reduce.5.cloned.1.call-update) | async-done | bytes 2097168 | tf_op jit(solution)/shard_map/while/body/eval_jaxpr/psum | solution.py:41
  181.4 85.0 %all-reduce.7.cloned.1.call-done = bf16[1,2048,512]{2,1,0:T(8,128)(2,1)} async-done(((bf16[1,2048,512]{2,1,0:T(8,128)(2,1)}), bf16[1,2048,512]{2,1,0:T(8,128)(2,1)}) %all-reduce.7.cloned.1.call-update) | async-done | bytes 2097168 | tf_op jit(solution)/shard_map/while/body/eval_jaxpr/psum | solution.py:47
  276.9 49.3 %all-gather.3.cloned.1.call-done = bf16[1,2048,512]{2,1,0:T(8,128)(2,1)} async-done(((bf16[1,512,512]{2,1,0:T(8,128)(2,1)}), bf16[1,2048,512]{2,1,0:T(8,128)(2,1)}) %all-gather.3.cloned.1.call-update) | async-done | bytes 2097168 | tf_op jit(solution)/shard_map/while/body/eval_jaxpr/all_gather | solution.py:99
  340.6 18.7 fusion.282
  359.3 12.2 fusion.283
  374.6 85.4 %all-reduce.5.cloned.1.call-done = bf16[1,2048,512]{2,1,0:T(8,128)(2,1)} async-done(((bf16[1,2048,512]{2,1,0:T(8,128)(2,1)}), bf16[1,2048,512]{2,1,0:T(8,128)(2,1)}) %all-reduce.5.cloned.1.call-update) | async-done | bytes 2097168 | tf_op jit(solution)/shard_map/while/body/eval_jaxpr/psum | solution.py:41
  473.8 85.1 %all-reduce.7.cloned.1.call-done = bf16[1,2048,512]{2,1,0:T(8,128)(2,1)} async-done(((bf16[1,2048,512]{2,1,0:T(8,128)(2,1)}), bf16[1,2048,512]{2,1,0:T(8,128)(2,1)}) %all-reduce.7.cloned.1.call-update) | async-done | bytes 2097168 | tf_op jit(solution)/shard_map/while/body/eval_jaxpr/psum | solution.py:47
  569.3 49.3 %all-gather.3.cloned.1.call-done = bf16[1,2048,512]{2,1,0:T(8,128)(2,1)} async-done(((bf16[1,512,512]{2,1,0:T(8,128)(2,1)}), bf16[1,2048,512]{2,1,0:T(8,128)(2,1)}) %all-gather.3.cloned.1.call-update) | async-done | bytes 2097168 | tf_op jit(solution)/shard_map/while/body/eval_jaxpr/all_gather | solution.py:99
  633.1 18.7 fusion.282
  651.8 12.2 fusion.283
  667.1 85.4 %all-reduce.5.cloned.1.call-done = bf16[1,2048,512]{2,1,0:T(8,128)(2,1)} async-done(((bf16[1,2048,512]{2,1,0:T(8,128)(2,1)}), bf16[1,2048,512]{2,1,0:T(8,128)(2,1)}) %all-reduce.5.cloned.1.call-update) | async-done | bytes 2097168 | tf_op jit(solution)/shard_map/while/body/eval_jaxpr/psum | solution.py:41
  766.3 85.2 %all-reduce.7.cloned.1.call-done = bf16[1,2048,512]{2,1,0:T(8,128)(2,1)} async-done(((bf16[1,2048,512]{2,1,0:T(8,128)(2,1)}), bf16[1,2048,512]{2,1,0:T(8,128)(2,1)}) %all-reduce.7.cloned.1.call-update) | async-done | bytes 2097168 | tf_op jit(solution)/shard_map/while/body/eval_jaxpr/psum | solution.py:47
  862.0 49.2 %all-gather.3.cloned.1.call-done = bf16[1,2048,512]{2,1,0:T(8,128)(2,1)} async-done(((bf16[1,512,512]{2,1,0:T(8,128)(2,1)}), bf16[1,2048,512]{2,1,0:T(8,128)(2,1)}) %all-gather.3.cloned.1.call-update) | async-done | bytes 2097168 | tf_op jit(solution)/shard_map/while/body/eval_jaxpr/all_gather | solution.py:99
  925.7 18.7 fusion.282
  944.4 12.2 fusion.283
  959.6 85.3 %all-reduce.5.cloned.1.call-done = bf16[1,2048,512]{2,1,0:T(8,128)(2,1)} async-done(((bf16[1,2048,512]{2,1,0:T(8,128)(2,1)}), bf16[1,2048,512]{2,1,0:T(8,128)(2,1)}) %all-reduce.5.cloned.1.call-update) | async-done | bytes 2097168 | tf_op jit(solution)/shard_map/while/body/eval_jaxpr/psum | solution.py:41
  1058.7 85.1 %all-reduce.7.cloned.1.call-done = bf16[1,2048,512]{2,1,0:T(8,128)(2,1)} async-done(((bf16[1,2048,512]{2,1,0:T(8,128)(2,1)}), bf16[1,2048,512]{2,1,0:T(8,128)(2,1)}) %all-reduce.7.cloned.1.call-update) | async-done | bytes 2097168 | tf_op jit(solution)/shard_map/while/body/eval_jaxpr/psum | solution.py:47
  1154.4 49.1 %all-gather.3.cloned.1.call-done = bf16[1,2048,512]{2,1,0:T(8,128)(2,1)} async-done(((bf16[1,512,512]{2,1,0:T(8,128)(2,1)}), bf16[1,2048,512]{2,1,0:T(8,128)(2,1)}) %all-gather.3.cloned.1.call-update) | async-done | bytes 2097168 | tf_op jit(solution)/shard_map/while/body/eval_jaxpr/all_gather | solution.py:99
  1218.0 18.7 fusion.282
  1236.7 12.2 fusion.283
  1252.0 85.3 %all-reduce.5.cloned.1.call-done = bf16[1,2048,512]{2,1,0:T(8,128)(2,1)} async-done(((bf16[1,2048,512]{2,1,0:T(8,128)(2,1)}), bf16[1,2048,512]{2,1,0:T(8,128)(2,1)}) %all-reduce.5.cloned.1.call-update) | async-done | bytes 2097168 | tf_op jit(solution)/shard_map/while/body/eval_jaxpr/psum | solution.py:41
  1351.1 85.1 %all-reduce.7.cloned.1.call-done = bf16[1,2048,512]{2,1,0:T(8,128)(2,1)} async-done(((bf16[1,2048,512]{2,1,0:T(8,128)(2,1)}), bf16[1,2048,512]{2,1,0:T(8,128)(2,1)}) %all-reduce.7.cloned.1.call-update) | async-done | bytes 2097168 | tf_op jit(solution)/shard_map/while/body/eval_jaxpr/psum | solution.py:47
  1446.8 49.2 %all-gather.3.cloned.1.call-done = bf16[1,2048,512]{2,1,0:T(8,128)(2,1)} async-done(((bf16[1,512,512]{2,1,0:T(8,128)(2,1)}), bf16[1,2048,512]{2,1,0:T(8,128)(2,1)}) %all-gather.3.cloned.1.call-update) | async-done | bytes 2097168 | tf_op jit(solution)/shard_map/while/body/eval_jaxpr/all_gather | solution.py:99
  1500.6 1718.2 %while.55 = (s32[]{:T(128)}, bf16[1,2048,512]{2,1,0:T(8,128)(2,1)}, f32[3,512,2,64]{1,3,2,0:T(8,128)}, f32[3,2,64]{2,1,0:T(2,128)}, f32[2,64,512]{2,1,0:T(8,128)...) while((s32[]{:T(128)}, bf16[1,2048,512]{2,1,0:T(8,128)(2,1)}, ...), condition=%wide.region_32.33_spmd.clone, body=%wide.region_10.32_spmd.clone.sunk | while | flops 13232809984 | bytes 488587200 | solution.py:160
  1526.6 20.2 fusion.314
  1546.8 54.2 %all-reduce.9.cloned.1.call-done = bf16[1,2048,512]{2,1,0:T(8,128)(2,1)} async-done(((bf16[1,2048,512]{2,1,0:T(8,128)(2,1)}), bf16[1,2048,512]{2,1,0:T(8,128)(2,1)}) %all-reduce.9.cloned.1.call-update) | async-done | bytes 2097168 | tf_op jit(solution)/shard_map/while/body/eval_jaxpr/psum | solution.py:69
  1616.6 22.2 fusion.315
  1638.8 18.7 fusion.318
  1657.5 18.8 fusion.317
  1676.4 11.1 fusion.316
  1692.2 83.2 %all-reduce.11.cloned.1.call-done = bf16[1,2048,512]{2,1,0:T(8,128)(2,1)} async-done(((bf16[1,2048,512]{2,1,0:T(8,128)(2,1)}), bf16[1,2048,512]{2,1,0:T(8,128)(2,1)}) %all-reduce.11.cloned.1.call-update) | async-done | bytes 2097168 | tf_op jit(solution)/shard_map/while/body/eval_jaxpr/psum | solution.py:82
  1819.6 24.0 all-gather.5.cloned.1.call-done
  1870.0 19.8 fusion.314
  1889.9 54.6 %all-reduce.9.cloned.1.call-done = bf16[1,2048,512]{2,1,0:T(8,128)(2,1)} async-done(((bf16[1,2048,512]{2,1,0:T(8,128)(2,1)}), bf16[1,2048,512]{2,1,0:T(8,128)(2,1)}) %all-reduce.9.cloned.1.call-update) | async-done | bytes 2097168 | tf_op jit(solution)/shard_map/while/body/eval_jaxpr/psum | solution.py:69
  1960.1 22.2 fusion.315
  1982.3 18.7 fusion.318
  2001.0 18.8 fusion.317
  2035.7 83.1 %all-reduce.11.cloned.1.call-done = bf16[1,2048,512]{2,1,0:T(8,128)(2,1)} async-done(((bf16[1,2048,512]{2,1,0:T(8,128)(2,1)}), bf16[1,2048,512]{2,1,0:T(8,128)(2,1)}) %all-reduce.11.cloned.1.call-update) | async-done | bytes 2097168 | tf_op jit(solution)/shard_map/while/body/eval_jaxpr/psum | solution.py:82
  2164.0 23.2 all-gather.5.cloned.1.call-done
  2213.4 19.9 fusion.314
  2233.3 54.5 %all-reduce.9.cloned.1.call-done = bf16[1,2048,512]{2,1,0:T(8,128)(2,1)} async-done(((bf16[1,2048,512]{2,1,0:T(8,128)(2,1)}), bf16[1,2048,512]{2,1,0:T(8,128)(2,1)}) %all-reduce.9.cloned.1.call-update) | async-done | bytes 2097168 | tf_op jit(solution)/shard_map/while/body/eval_jaxpr/psum | solution.py:69
  2303.5 22.2 fusion.315
  2325.7 18.9 fusion.318
  2344.6 18.8 fusion.317
  2379.3 83.1 %all-reduce.11.cloned.1.call-done = bf16[1,2048,512]{2,1,0:T(8,128)(2,1)} async-done(((bf16[1,2048,512]{2,1,0:T(8,128)(2,1)}), bf16[1,2048,512]{2,1,0:T(8,128)(2,1)}) %all-reduce.11.cloned.1.call-update) | async-done | bytes 2097168 | tf_op jit(solution)/shard_map/while/body/eval_jaxpr/psum | solution.py:82
  2507.3 23.3 all-gather.5.cloned.1.call-done
  2556.8 20.1 fusion.314
  2576.9 54.3 %all-reduce.9.cloned.1.call-done = bf16[1,2048,512]{2,1,0:T(8,128)(2,1)} async-done(((bf16[1,2048,512]{2,1,0:T(8,128)(2,1)}), bf16[1,2048,512]{2,1,0:T(8,128)(2,1)}) %all-reduce.9.cloned.1.call-update) | async-done | bytes 2097168 | tf_op jit(solution)/shard_map/while/body/eval_jaxpr/psum | solution.py:69
  2646.9 22.2 fusion.315
  2669.1 18.7 fusion.318
  2687.8 18.8 fusion.317
  2722.5 83.1 %all-reduce.11.cloned.1.call-done = bf16[1,2048,512]{2,1,0:T(8,128)(2,1)} async-done(((bf16[1,2048,512]{2,1,0:T(8,128)(2,1)}), bf16[1,2048,512]{2,1,0:T(8,128)(2,1)}) %all-reduce.11.cloned.1.call-update) | async-done | bytes 2097168 | tf_op jit(solution)/shard_map/while/body/eval_jaxpr/psum | solution.py:82
  2850.5 23.4 all-gather.5.cloned.1.call-done
  2900.3 19.8 fusion.314
  2920.1 54.6 %all-reduce.9.cloned.1.call-done = bf16[1,2048,512]{2,1,0:T(8,128)(2,1)} async-done(((bf16[1,2048,512]{2,1,0:T(8,128)(2,1)}), bf16[1,2048,512]{2,1,0:T(8,128)(2,1)}) %all-reduce.9.cloned.1.call-update) | async-done | bytes 2097168 | tf_op jit(solution)/shard_map/while/body/eval_jaxpr/psum | solution.py:69
  2990.3 22.2 fusion.315
  3012.5 18.7 fusion.318
  3031.2 18.8 fusion.317
  3050.1 11.1 fusion.316
  3065.9 83.2 %all-reduce.11.cloned.1.call-done = bf16[1,2048,512]{2,1,0:T(8,128)(2,1)} async-done(((bf16[1,2048,512]{2,1,0:T(8,128)(2,1)}), bf16[1,2048,512]{2,1,0:T(8,128)(2,1)}) %all-reduce.11.cloned.1.call-update) | async-done | bytes 2097168 | tf_op jit(solution)/shard_map/while/body/eval_jaxpr/psum | solution.py:82
  3194.2 23.3 all-gather.5.cloned.1.call-done
  (852 shorter events, 721.6 us)
Async XLA Ops:
  30.0 137.6 %all-reduce.5.cloned.1.call-start = ((), (), s32[]{:S(2)}) async-start(), calls=%async_computation | async-start | bytes 4194304 | tf_op jit(solution)/shard_map/while/body/eval_jaxpr/psum | solution.py:41
  78.5 187.9 %all-reduce.7.cloned.1.call-start = ((), (), s32[]{:S(2)}) async-start(), calls=%async_computation.1 | async-start | bytes 4194304 | tf_op jit(solution)/shard_map/while/body/eval_jaxpr/psum | solution.py:47
  181.3 144.9 %all-gather.3.cloned.1.call-start = ((), (), s32[]{:S(2)}) async-start(), calls=%async_computation.2 | async-start | bytes 2621440 | tf_op jit(solution)/shard_map/while/body/eval_jaxpr/all_gather | solution.py:99
  270.0 2.8 collective-permute-start
  326.2 133.8 %all-reduce.5.cloned.1.call-start = ((), (), s32[]{:S(2)}) async-start(), calls=%async_computation | async-start | bytes 4194304 | tf_op jit(solution)/shard_map/while/body/eval_jaxpr/psum | solution.py:41
  374.5 184.3 %all-reduce.7.cloned.1.call-start = ((), (), s32[]{:S(2)}) async-start(), calls=%async_computation.1 | async-start | bytes 4194304 | tf_op jit(solution)/shard_map/while/body/eval_jaxpr/psum | solution.py:47
  473.7 144.9 %all-gather.3.cloned.1.call-start = ((), (), s32[]{:S(2)}) async-start(), calls=%async_computation.2 | async-start | bytes 2621440 | tf_op jit(solution)/shard_map/while/body/eval_jaxpr/all_gather | solution.py:99
  562.4 2.8 collective-permute-start
  618.7 133.8 %all-reduce.5.cloned.1.call-start = ((), (), s32[]{:S(2)}) async-start(), calls=%async_computation | async-start | bytes 4194304 | tf_op jit(solution)/shard_map/while/body/eval_jaxpr/psum | solution.py:41
  667.0 184.4 %all-reduce.7.cloned.1.call-start = ((), (), s32[]{:S(2)}) async-start(), calls=%async_computation.1 | async-start | bytes 4194304 | tf_op jit(solution)/shard_map/while/body/eval_jaxpr/psum | solution.py:47
  766.2 145.0 %all-gather.3.cloned.1.call-start = ((), (), s32[]{:S(2)}) async-start(), calls=%async_computation.2 | async-start | bytes 2621440 | tf_op jit(solution)/shard_map/while/body/eval_jaxpr/all_gather | solution.py:99
  855.1 2.8 collective-permute-start
  911.2 133.8 %all-reduce.5.cloned.1.call-start = ((), (), s32[]{:S(2)}) async-start(), calls=%async_computation | async-start | bytes 4194304 | tf_op jit(solution)/shard_map/while/body/eval_jaxpr/psum | solution.py:41
  959.6 184.3 %all-reduce.7.cloned.1.call-start = ((), (), s32[]{:S(2)}) async-start(), calls=%async_computation.1 | async-start | bytes 4194304 | tf_op jit(solution)/shard_map/while/body/eval_jaxpr/psum | solution.py:47
  1058.7 144.9 %all-gather.3.cloned.1.call-start = ((), (), s32[]{:S(2)}) async-start(), calls=%async_computation.2 | async-start | bytes 2621440 | tf_op jit(solution)/shard_map/while/body/eval_jaxpr/all_gather | solution.py:99
  1147.5 2.8 collective-permute-start
  1203.6 133.8 %all-reduce.5.cloned.1.call-start = ((), (), s32[]{:S(2)}) async-start(), calls=%async_computation | async-start | bytes 4194304 | tf_op jit(solution)/shard_map/while/body/eval_jaxpr/psum | solution.py:41
  1251.9 184.3 %all-reduce.7.cloned.1.call-start = ((), (), s32[]{:S(2)}) async-start(), calls=%async_computation.1 | async-start | bytes 4194304 | tf_op jit(solution)/shard_map/while/body/eval_jaxpr/psum | solution.py:47
  1351.1 145.0 %all-gather.3.cloned.1.call-start = ((), (), s32[]{:S(2)}) async-start(), calls=%async_computation.2 | async-start | bytes 2621440 | tf_op jit(solution)/shard_map/while/body/eval_jaxpr/all_gather | solution.py:99
  1439.9 2.8 collective-permute-start
  1500.6 100.4 %all-reduce.9.cloned.1.call-start = ((), (), s32[]{:S(2)}) async-start(), calls=%async_computation.3 | async-start | bytes 4194304 | tf_op jit(solution)/shard_map/while/body/eval_jaxpr/psum | solution.py:69
  1504.3 110.2 %copy-start.1 = (bf16[1,2048,512]{2,1,0:T(8,128)(2,1)}, bf16[1,2048,512]{2,1,0:T(8,128)(2,1)S(1)}, u32[]{:S(2)}) copy-start(bf16[1,2048,512]{2,1,0:T(8,128)(2,1)S(1)} %fusion.307) | copy-start | bytes 6291460 | tf_op jit(solution)/shard_map/while
  1516.2 259.2 %all-reduce.11.cloned.1.call-start = ((), (), s32[]{:S(2)}) async-start(), calls=%async_computation.4 | async-start | bytes 4194304 | tf_op jit(solution)/shard_map/while/body/eval_jaxpr/psum | solution.py:82
  1522.4 87.5 %copy-start.17 = (f32[2048]{0:T(1024)}, f32[2048]{0:T(1024)S(1)}, u32[]{:S(2)}) copy-start(f32[2048]{0:T(1024)S(1)} %broadcast_multiply_fusion.10) | copy-start | bytes 24580 | tf_op jit(solution)/shard_map/while
  1523.8 86.1 %copy-start.21 = (f32[1,512]{1,0:T(1,128)}, f32[1,512]{1,0:T(1,128)S(1)}, u32[]{:S(2)}) copy-start(f32[1,512]{1,0:T(1,128)S(1)} %get-tuple-element.1068) | copy-start | bytes 6148 | tf_op jit(solution)/shard_map/while
  1657.5 30.0 copy-start.10
  1690.2 85.2 %copy-start.23 = (f32[1,512]{1,0:T(1,128)S(1)}, f32[1,512]{1,0:T(1,128)}, u32[]{:S(2)}) copy-start(f32[1,512]{1,0:T(1,128)} %get-tuple-element.1080) | copy-start | bytes 6148 | tf_op jit(solution)/shard_map/while
  1690.2 153.3 %all-gather.5.cloned.1.call-start = ((), (), s32[]{:S(2)}) async-start(), calls=%async_computation.5 | async-start | bytes 2621440 | tf_op jit(solution)/shard_map/while/body/eval_jaxpr/all_gather | solution.py:99
  1788.8 3.8 collective-permute-start.1
  1843.9 100.5 %all-reduce.9.cloned.1.call-start = ((), (), s32[]{:S(2)}) async-start(), calls=%async_computation.3 | async-start | bytes 4194304 | tf_op jit(solution)/shard_map/while/body/eval_jaxpr/psum | solution.py:69
  1847.7 110.2 %copy-start.1 = (bf16[1,2048,512]{2,1,0:T(8,128)(2,1)}, bf16[1,2048,512]{2,1,0:T(8,128)(2,1)S(1)}, u32[]{:S(2)}) copy-start(bf16[1,2048,512]{2,1,0:T(8,128)(2,1)S(1)} %fusion.307) | copy-start | bytes 6291460 | tf_op jit(solution)/shard_map/while
  1859.7 259.2 %all-reduce.11.cloned.1.call-start = ((), (), s32[]{:S(2)}) async-start(), calls=%async_computation.4 | async-start | bytes 4194304 | tf_op jit(solution)/shard_map/while/body/eval_jaxpr/psum | solution.py:82
  1865.8 87.5 %copy-start.17 = (f32[2048]{0:T(1024)}, f32[2048]{0:T(1024)S(1)}, u32[]{:S(2)}) copy-start(f32[2048]{0:T(1024)S(1)} %broadcast_multiply_fusion.10) | copy-start | bytes 24580 | tf_op jit(solution)/shard_map/while
  1867.2 86.1 %copy-start.21 = (f32[1,512]{1,0:T(1,128)}, f32[1,512]{1,0:T(1,128)S(1)}, u32[]{:S(2)}) copy-start(f32[1,512]{1,0:T(1,128)S(1)} %get-tuple-element.1068) | copy-start | bytes 6148 | tf_op jit(solution)/shard_map/while
  2001.0 30.0 copy-start.10
  2033.7 85.2 %copy-start.23 = (f32[1,512]{1,0:T(1,128)S(1)}, f32[1,512]{1,0:T(1,128)}, u32[]{:S(2)}) copy-start(f32[1,512]{1,0:T(1,128)} %get-tuple-element.1080) | copy-start | bytes 6148 | tf_op jit(solution)/shard_map/while
  2033.7 153.5 %all-gather.5.cloned.1.call-start = ((), (), s32[]{:S(2)}) async-start(), calls=%async_computation.5 | async-start | bytes 2621440 | tf_op jit(solution)/shard_map/while/body/eval_jaxpr/all_gather | solution.py:99
  2132.5 3.8 collective-permute-start.1
  2187.4 100.5 %all-reduce.9.cloned.1.call-start = ((), (), s32[]{:S(2)}) async-start(), calls=%async_computation.3 | async-start | bytes 4194304 | tf_op jit(solution)/shard_map/while/body/eval_jaxpr/psum | solution.py:69
  2191.1 110.2 %copy-start.1 = (bf16[1,2048,512]{2,1,0:T(8,128)(2,1)}, bf16[1,2048,512]{2,1,0:T(8,128)(2,1)S(1)}, u32[]{:S(2)}) copy-start(bf16[1,2048,512]{2,1,0:T(8,128)(2,1)S(1)} %fusion.307) | copy-start | bytes 6291460 | tf_op jit(solution)/shard_map/while
  2203.1 259.3 %all-reduce.11.cloned.1.call-start = ((), (), s32[]{:S(2)}) async-start(), calls=%async_computation.4 | async-start | bytes 4194304 | tf_op jit(solution)/shard_map/while/body/eval_jaxpr/psum | solution.py:82
  2209.2 87.5 %copy-start.17 = (f32[2048]{0:T(1024)}, f32[2048]{0:T(1024)S(1)}, u32[]{:S(2)}) copy-start(f32[2048]{0:T(1024)S(1)} %broadcast_multiply_fusion.10) | copy-start | bytes 24580 | tf_op jit(solution)/shard_map/while
  2210.6 86.1 %copy-start.21 = (f32[1,512]{1,0:T(1,128)}, f32[1,512]{1,0:T(1,128)S(1)}, u32[]{:S(2)}) copy-start(f32[1,512]{1,0:T(1,128)S(1)} %get-tuple-element.1068) | copy-start | bytes 6148 | tf_op jit(solution)/shard_map/while
  2377.3 85.1 %copy-start.23 = (f32[1,512]{1,0:T(1,128)S(1)}, f32[1,512]{1,0:T(1,128)}, u32[]{:S(2)}) copy-start(f32[1,512]{1,0:T(1,128)} %get-tuple-element.1080) | copy-start | bytes 6148 | tf_op jit(solution)/shard_map/while
  2377.3 153.3 %all-gather.5.cloned.1.call-start = ((), (), s32[]{:S(2)}) async-start(), calls=%async_computation.5 | async-start | bytes 2621440 | tf_op jit(solution)/shard_map/while/body/eval_jaxpr/all_gather | solution.py:99
  2475.8 3.8 collective-permute-start.1
  2530.8 100.5 %all-reduce.9.cloned.1.call-start = ((), (), s32[]{:S(2)}) async-start(), calls=%async_computation.3 | async-start | bytes 4194304 | tf_op jit(solution)/shard_map/while/body/eval_jaxpr/psum | solution.py:69
  2534.5 110.2 %copy-start.1 = (bf16[1,2048,512]{2,1,0:T(8,128)(2,1)}, bf16[1,2048,512]{2,1,0:T(8,128)(2,1)S(1)}, u32[]{:S(2)}) copy-start(bf16[1,2048,512]{2,1,0:T(8,128)(2,1)S(1)} %fusion.307) | copy-start | bytes 6291460 | tf_op jit(solution)/shard_map/while
  2546.5 259.1 %all-reduce.11.cloned.1.call-start = ((), (), s32[]{:S(2)}) async-start(), calls=%async_computation.4 | async-start | bytes 4194304 | tf_op jit(solution)/shard_map/while/body/eval_jaxpr/psum | solution.py:82
  2552.6 87.5 %copy-start.17 = (f32[2048]{0:T(1024)}, f32[2048]{0:T(1024)S(1)}, u32[]{:S(2)}) copy-start(f32[2048]{0:T(1024)S(1)} %broadcast_multiply_fusion.10) | copy-start | bytes 24580 | tf_op jit(solution)/shard_map/while
  2554.1 86.1 %copy-start.21 = (f32[1,512]{1,0:T(1,128)}, f32[1,512]{1,0:T(1,128)S(1)}, u32[]{:S(2)}) copy-start(f32[1,512]{1,0:T(1,128)S(1)} %get-tuple-element.1068) | copy-start | bytes 6148 | tf_op jit(solution)/shard_map/while
  2687.8 30.0 copy-start.10
  2720.5 85.1 %copy-start.23 = (f32[1,512]{1,0:T(1,128)S(1)}, f32[1,512]{1,0:T(1,128)}, u32[]{:S(2)}) copy-start(f32[1,512]{1,0:T(1,128)} %get-tuple-element.1080) | copy-start | bytes 6148 | tf_op jit(solution)/shard_map/while
  2720.5 153.3 %all-gather.5.cloned.1.call-start = ((), (), s32[]{:S(2)}) async-start(), calls=%async_computation.5 | async-start | bytes 2621440 | tf_op jit(solution)/shard_map/while/body/eval_jaxpr/all_gather | solution.py:99
  2819.0 3.8 collective-permute-start.1
  2874.2 100.5 %all-reduce.9.cloned.1.call-start = ((), (), s32[]{:S(2)}) async-start(), calls=%async_computation.3 | async-start | bytes 4194304 | tf_op jit(solution)/shard_map/while/body/eval_jaxpr/psum | solution.py:69
  2878.0 110.1 %copy-start.1 = (bf16[1,2048,512]{2,1,0:T(8,128)(2,1)}, bf16[1,2048,512]{2,1,0:T(8,128)(2,1)S(1)}, u32[]{:S(2)}) copy-start(bf16[1,2048,512]{2,1,0:T(8,128)(2,1)S(1)} %fusion.307) | copy-start | bytes 6291460 | tf_op jit(solution)/shard_map/while
  2889.9 259.1 %all-reduce.11.cloned.1.call-start = ((), (), s32[]{:S(2)}) async-start(), calls=%async_computation.4 | async-start | bytes 4194304 | tf_op jit(solution)/shard_map/while/body/eval_jaxpr/psum | solution.py:82
  2896.1 87.5 %copy-start.17 = (f32[2048]{0:T(1024)}, f32[2048]{0:T(1024)S(1)}, u32[]{:S(2)}) copy-start(f32[2048]{0:T(1024)S(1)} %broadcast_multiply_fusion.10) | copy-start | bytes 24580 | tf_op jit(solution)/shard_map/while
  2897.5 86.0 %copy-start.21 = (f32[1,512]{1,0:T(1,128)}, f32[1,512]{1,0:T(1,128)S(1)}, u32[]{:S(2)}) copy-start(f32[1,512]{1,0:T(1,128)S(1)} %get-tuple-element.1068) | copy-start | bytes 6148 | tf_op jit(solution)/shard_map/while
  3031.2 30.0 copy-start.10
  3063.9 85.2 %copy-start.23 = (f32[1,512]{1,0:T(1,128)S(1)}, f32[1,512]{1,0:T(1,128)}, u32[]{:S(2)}) copy-start(f32[1,512]{1,0:T(1,128)} %get-tuple-element.1080) | copy-start | bytes 6148 | tf_op jit(solution)/shard_map/while
  3063.9 153.6 %all-gather.5.cloned.1.call-start = ((), (), s32[]{:S(2)}) async-start(), calls=%async_computation.5 | async-start | bytes 2621440 | tf_op jit(solution)/shard_map/while/body/eval_jaxpr/all_gather | solution.py:99
  3162.7 3.8 collective-permute-start.1
  (199 other events, 1405.9 us)
Sparse Core Ops, SparseCore 0:
  78.6 88.9 all-reduce.4
  181.4 84.9 all-reduce.6
  273.8 52.3 all-gather.2
  374.7 85.2 all-reduce.4
  473.9 84.9 all-reduce.6
  566.2 52.4 all-gather.2
  667.1 85.3 all-reduce.4
  766.3 85.0 all-reduce.6
  858.8 52.3 all-gather.2
  959.7 85.2 all-reduce.4
  1058.8 85.0 all-reduce.6
  1151.2 52.2 all-gather.2
  1252.1 85.2 all-reduce.4
  1351.2 84.9 all-reduce.6
  1443.6 52.3 all-gather.2
  1516.3 84.6 all-reduce.8
  1690.3 85.0 all-reduce.10
  1793.6 49.9 all-gather.4
  1859.8 84.6 all-reduce.8
  2033.8 84.9 all-reduce.10
  2137.2 49.9 all-gather.4
  2203.2 84.6 all-reduce.8
  2377.4 84.9 all-reduce.10
  2480.5 50.0 all-gather.4
  2546.6 84.6 all-reduce.8
  2720.6 84.9 all-reduce.10
  2823.7 50.0 all-gather.4
  2890.0 84.6 all-reduce.8
  3064.0 85.0 all-reduce.10
  3167.5 49.9 all-gather.4
where the time goes:
time: 3240 us; the launch traced here: 3230 us
  waiting for transfers between devices  1930 us (60%)
  matrix products  872 us (27%)
  other arithmetic  300 us (9%)
  local copies, waits for them, and re-layouts  90.9 us (3%)
    psum x5, waiting for transfers between devices, layer_forward(): attn_sum = lax.psum(attn_part, 'tp')  430 us
    psum x5, waiting for transfers between devices, layer_forward(): mlp_sum = lax.psum(mlp_part, 'tp')  425 us
    psum x5, waiting for transfers between devices, layer_backward(): lax.psum(jnp.einsum('bsche,cdhe->bsd', g_qkv, w_qkv, preferred_element_ty...  416 us
    all_gather x10, waiting for transfers between devices, pass_on(): return lax.all_gather(moved_part, 'tp', axis=1, tiled=True)  363 us
    psum x5, waiting for transfers between devices, layer_backward(): lax.psum(jnp.einsum('bsf,df->bsd', g_pre_half, w_fc1, preferred_element_t...  272 us
    dot_general x15, matrix products, causal_attention(): jnp.einsum('bhqk,bkhe->bqhe', attn_probs, v_heads, preferred_element_type...  228 us
    sub x10, matrix products, causal_attention(): attn_probs = jax.nn.softmax(scores, axis=-1).astype(jnp.bfloat16)  193 us
    dot_general x10, matrix products, causal_attention(): jnp.einsum('bqhe,bkhe->bhqk', q_heads, k_heads, preferred_element_type=jn...  188 us
  transfers between devices with their start and end apart: 40, of which 40 were waited for; matrix products, arithmetic and copies ran while one was open for 10% of the time, Pallas kernels for 0%

commit v1 on v0

v1 whole, which is shorter than its diff:
```python
import functools

import jax
import jax.numpy as jnp
from jax import lax
from jax.experimental import pallas as pl
from jax.experimental.pallas import tpu as pltpu
from jax.sharding import PartitionSpec as P

LN_EPS = 1e-5
BF = jnp.bfloat16
F32 = jnp.float32
MESH = pl.DeviceIdType.MESH

LAYERS = 4
SEQ = 2048
D = 512
CH = 128
NJ = 8
ROWS = CH * NJ
SLOTS = 2 * NJ
GELU_C = 0.7978845608028654
GELU_A = 0.044715
W = 128
KB = 256
NO = None


def nn(a, b):
    return lax.dot_general(a, b, (((1,), (0,)), ((), ())), preferred_element_type=F32)


def nt(a, b):
    return lax.dot_general(a, b, (((1,), (1,)), ((), ())), preferred_element_type=F32)


def tn(a, b):
    return lax.dot_general(a, b, (((0,), (0,)), ((), ())), preferred_element_type=F32)


def ln_stats(x_wide):
    mean = jnp.mean(x_wide, axis=-1, keepdims=True)
    cent = x_wide - mean
    var = jnp.mean(cent * cent, axis=-1, keepdims=True)
    rstd = lax.rsqrt(var + LN_EPS)
    return cent * rstd, rstd


def ln_back(dy, xhat, rstd, gain):
    dxhat = dy * gain
    m1 = jnp.mean(dxhat, axis=-1, keepdims=True)
    m2 = jnp.mean(dxhat * xhat, axis=-1, keepdims=True)
    return rstd * (dxhat - m1 - xhat * m2)


def colsum(v):
    return jnp.sum(v, axis=0, keepdims=True)


def when(cond):
    return pl.when(cond)


def wait_dma(ref, sem):
    pltpu.make_async_copy(ref, ref, sem).wait()


class Place:
    def __init__(self):
        self.z = lax.axis_index("tp")
        self.p = lax.axis_index("pp")
        self.y = self.p // 2
        self.c = self.p % 2
        self.hub = (self.z == 1) | (self.z == 2)
        self.leaf = jnp.logical_not(self.hub)
        self.my_hub = jnp.where(self.z == 0, 1, 2)
        self.my_leaf = jnp.where(self.z == 1, 0, 3)
        self.other_hub = 3 - self.z
        self.mate = self.p + 1 - 2 * self.c
        self.across = 2 * (1 - self.y) + self.c

    def tile(self, j):
        return 2 * j + (self.c + j) % 2

    def tile_rows(self, j):
        return pl.ds(pl.multiple_of(self.tile(j) * CH, CH), CH)

    def mate_rows(self, j):
        return pl.ds(pl.multiple_of((2 * j + (self.c + j + 1) % 2) * CH, CH), CH)

    def enter(self):
        bar = pltpu.get_barrier_semaphore()
        for k in range(1, 4):
            pl.semaphore_signal(bar, inc=1, device_id={"pp": (self.p + k) % 4}, device_id_type=MESH)

        @when(self.z > 0)
        def _():
            pl.semaphore_signal(bar, inc=1, device_id={"tp": self.z - 1}, device_id_type=MESH)

        @when(self.z < 3)
        def _():
            pl.semaphore_signal(bar, inc=1, device_id={"tp": self.z + 1}, device_id_type=MESH)

        @when(self.hub)
        def _():
            pl.semaphore_wait(bar, 5)

        @when(self.leaf)
        def _():
            pl.semaphore_wait(bar, 4)


def chunk_rows(j):
    return pl.ds(pl.multiple_of(j * CH, CH), CH)


def send(src, dst, ssem, rsem, dev):
    pltpu.make_async_remote_copy(src, dst, ssem, rsem, device_id=dev, device_id_type=MESH).start()


class LineSum:
    def __init__(self, at, part, lbuf, hbuf, sbuf, fin, s1, s2, r_l, r_h, r_f):
        self.at, self.part, self.lbuf, self.hbuf, self.sbuf, self.fin = at, part, lbuf, hbuf, sbuf, fin
        self.s1, self.s2, self.r_l, self.r_h, self.r_f = s1, s2, r_l, r_h, r_f

    def emit(self, e, value):
        slot = e % SLOTS
        at = self.at

        @when(at.leaf & (e >= SLOTS))
        def _():
            wait_dma(self.part.at[slot], self.s1.at[slot])

        self.part[slot] = value.astype(BF)

        @when(at.leaf)
        def _():
            send(self.part.at[slot], self.lbuf.at[slot], self.s1.at[slot], self.r_l.at[slot], {"tp": at.my_hub})

        self.serve_first(e - 2)
        self.serve_second(e - 4)

    def serve_first(self, e):
        slot = (e + SLOTS) % SLOTS
        at = self.at

        @when(at.hub & (e >= 0))
        def _():
            wait_dma(self.lbuf.at[slot], self.r_l.at[slot])

            @when(e >= SLOTS)
            def _():
                wait_dma(self.sbuf.at[slot], self.s1.at[slot])

            self.sbuf[slot] = (self.part[slot].astype(F32) + self.lbuf[slot].astype(F32)).astype(BF)
            send(self.sbuf.at[slot], self.hbuf.at[slot], self.s1.at[slot], self.r_h.at[slot], {"tp": at.other_hub})

    def serve_second(self, e):
        slot = (e + SLOTS) % SLOTS
        at = self.at

        @when(at.hub & (e >= 0))
        def _():
            wait_dma(self.hbuf.at[slot], self.r_h.at[slot])

            @when(e >= SLOTS)
            def _():
                wait_dma(self.fin.at[slot], self.s2.at[slot])

            self.fin[slot] = (self.sbuf[slot].astype(F32) + self.hbuf[slot].astype(F32)).astype(BF)
            send(self.fin.at[slot], self.fin.at[slot], self.s2.at[slot], self.r_f.at[slot], {"tp": at.my_leaf})

    def get(self, slot):
        @when(self.at.leaf)
        def _():
            wait_dma(self.fin.at[slot], self.r_f.at[slot])

        return self.fin[slot].astype(F32)

    def drain(self, total):
        self.serve_first(total - 2)
        self.serve_first(total - 1)
        for k in range(4):
            self.serve_second(total - 4 + k)

    def close(self):
        def body(slot, carry):
            wait_dma(self.part.at[slot], self.s1.at[slot])

            @when(self.at.hub)
            def _():
                wait_dma(self.fin.at[slot], self.s2.at[slot])

            return carry

        lax.fori_loop(0, SLOTS, body, 0)


LINE_SCRATCH = [pltpu.VMEM((SLOTS, CH, D), BF)] * 5 + [pltpu.SemaphoreType.DMA((SLOTS,))] * 5


def head_stack(v):
    lane = lax.broadcasted_iota(jnp.int32, v.shape, 1)
    zero = jnp.zeros_like(v)
    return jnp.concatenate([jnp.where(lane < 64, v, zero), jnp.where(lane < 64, zero, v)], axis=0)


def head_merge(v):
    lane = lax.broadcasted_iota(jnp.int32, (CH, W), 1)
    return jnp.where(lane < 64, v[:CH], v[CH:])


def forward_kernel(x_in, wq, wo, w1, w2, ws,
                   h_out, xs, xm, kvs, qs, os_, lses, wqa, woa, w1a, w2a, wsa,
                   wqv, wov, w1v, w2v, wsv, kv, xcur, xmid, q_all, o_all, lse_all, scores, acc, lsum,
                   part, lbuf, hbuf, sbuf, fin, s1, s2, r_l, r_h, r_f,
                   x_sem, w_local, w_send, w_recv, w_fwd, kv_s, kv_r, ho_s, ho_r, save):
    at = Place()
    line = LineSum(at, part, lbuf, hbuf, sbuf, fin, s1, s2, r_l, r_h, r_f)
    y, c, p = at.y, at.c, at.p
    w_hbm = (wq, wo, ws, w1, w2)
    w_vm = (wqv, wov, wsv, w1v, w2v)
    group_a, group_m = (0, 1, 2), (3, 4)

    for j in range(NJ):
        pltpu.make_async_copy(x_in.at[y, at.tile_rows(j)], xcur.at[chunk_rows(j)], x_sem.at[j]).start()
    for k in range(5):
        pltpu.make_async_copy(w_hbm[k], w_vm[k].at[p], w_local.at[k]).start()

    at.enter()

    def send_across():
        for k in range(5):
            send(w_hbm[k], w_vm[k].at[p], w_send.at[1, k], w_recv.at[p, k], {"pp": at.across})

    @when(c == 0)
    def _():
        send_across()

    for k in range(5):
        send(w_hbm[k], w_vm[k].at[p], w_send.at[0, k], w_recv.at[p, k], {"pp": at.mate})

    def weights_ready(s, group):
        @when(p == s)
        def _():
            for k in group:
                wait_dma(w_vm[k].at[p], w_local.at[k])

        @when(p != s)
        def _():
            for k in group:
                wait_dma(w_vm[k].at[s], w_recv.at[s, k])

        @when((y != s // 2) & (c == s % 2))
        def _():
            for k in group:
                send(w_vm[k].at[s], w_vm[k].at[s], w_fwd.at[k], w_recv.at[s, k], {"pp": at.mate})

    weights_ready(0, group_a)

    def finish_y(l, j):
        rows = chunk_rows(j)
        total = line.get(NJ + j)
        b2 = wsv[l, 5:6, :].astype(F32)
        out = (xmid[rows, :].astype(F32) + total + b2).astype(BF)

        @when(l > 0)
        def _():
            wait_dma(xcur.at[rows], ho_s.at[j])

        xcur[rows, :] = out
        dst = h_out.at[y, at.tile_rows(j)]

        @when(p == l)
        def _():
            pltpu.make_async_copy(xcur.at[rows], dst, ho_s.at[j]).start()

        @when(p != l)
        def _():
            send(xcur.at[rows], dst, ho_s.at[j], ho_r.at[p], {"pp": l})

    def attn_op(l, j):
        rows = chunk_rows(j)
        par = l % 2

        @when(l == 0)
        def _():
            wait_dma(xcur.at[rows], x_sem.at[j])

        @when(l > 0)
        def _():
            finish_y(l - 1, j)

        small = wsv[l].astype(F32)
        xhat, _ = ln_stats(xcur[rows, :].astype(F32))
        h1 = (xhat * small[0:1] + small[1:2]).astype(BF)
        qkv = (nn(h1, wqv[l]) + small[7:8, :384]).astype(BF)
        q = qkv[:, :W]
        mine = at.tile_rows(j)
        kv[par, mine, :] = qkv[:, W:384]
        send(kv.at[par, mine], kv.at[par, mine], kv_s.at[j], kv_r.at[j], {"pp": at.mate})
        q_all[rows, :] = q
        q2 = head_stack(q * jnp.asarray(0.125, BF))

        def score(kb):
            return nt(q2, kv[par, pl.ds(pl.multiple_of(kb * KB, KB), KB), 0:W])

        def pass_one(kb, best):
            s = score(kb)
            scores[kb] = s
            return jnp.maximum(best, jnp.maximum(s[:, :W], s[:, W:]))

        best = lax.fori_loop(0, j, pass_one, jnp.full((KB, W), -1e30, F32))
        wait_dma(kv.at[par, mine], kv_r.at[j])
        s = score(j)
        row = lax.broadcasted_iota(jnp.int32, (KB, KB), 0) % CH + CH * ((c + j) % 2)
        col = lax.broadcasted_iota(jnp.int32, (KB, KB), 1)
        s = jnp.where(row >= col, s, -1e30)
        scores[j] = s
        best = jnp.maximum(best, jnp.maximum(s[:, :W], s[:, W:]))
        top = jnp.max(best, axis=-1, keepdims=True)
        acc[...] = jnp.zeros_like(acc)
        lsum[...] = jnp.zeros_like(lsum)

        def pass_two(kb, carry):
            e = jnp.exp(scores[kb] - top)
            lsum[...] += e[:, :W] + e[:, W:]
            acc[...] += nn(e.astype(BF), kv[par, pl.ds(pl.multiple_of(kb * KB, KB), KB), W:KB])
            return carry

        lax.fori_loop(0, j + 1, pass_two, 0)
        den = jnp.sum(lsum[...], axis=-1, keepdims=True)
        o = head_merge(acc[...] / den).astype(BF)
        o_all[rows, :] = o
        lse = jnp.broadcast_to(top + jnp.log(den), (KB, W))
        lse_all[pl.ds(pl.multiple_of(j * 8, 8), 8), :] = lse.T[:8]
        line.emit(2 * NJ * l + j, nn(o, wov[l]))

    def mlp_op(l, j):
        rows = chunk_rows(j)
        small = wsv[l].astype(F32)
        xm_new = (xcur[rows, :].astype(F32) + line.get(j) + small[4:5]).astype(BF)
        xmid[rows, :] = xm_new
        xhat, _ = ln_stats(xm_new.astype(F32))
        h2 = (xhat * small[2:3] + small[3:4]).astype(BF)
        u = nn(h2, w1v[l]) + small[6:7]
        a = 0.5 * u * (1.0 + jnp.tanh(GELU_C * (u + GELU_A * u * u * u)))
        line.emit(2 * NJ * l + NJ + j, nn(a.astype(BF), w2v[l]))

    a_saves = ((xcur, xs), (kv, kvs), (q_all, qs), (o_all, os_), (lse_all, lses))

    def layer(l, carry):
        @when(l > 0)
        def _():
            for k in (2, 3, 4):
                wait_dma(a_saves[k][0], save.at[k])
            wait_dma(kv.at[0], save.at[1])
            wait_dma(xcur, save.at[0])

        def attn_step(j, carry):
            attn_op(l, j)
            return carry

        lax.fori_loop(0, NJ, attn_step, 0)
        par = l % 2
        for k in (0, 2, 3, 4):
            pltpu.make_async_copy(a_saves[k][0], a_saves[k][1].at[l], save.at[k]).start()
        pltpu.make_async_copy(kv.at[par], kvs.at[l], save.at[1]).start()

        @when(l == 0)
        def _():
            @when(c == 1)
            def _():
                send_across()

            weights_ready(0, group_m)

        @when(l > 0)
        def _():
            wait_dma(xmid, save.at[5])

        def mlp_step(j, carry):
            mlp_op(l, j)

            @when((j == 6) & (l < LAYERS - 1))
            def _():
                weights_ready(l + 1, group_a + group_m)

            return carry

        lax.fori_loop(0, NJ, mlp_step, 0)
        pltpu.make_async_copy(xmid, xm.at[l], save.at[5]).start()

        def kv_sent(j, carry):
            wait_dma(kv.at[0, pl.ds(0, CH)], kv_s.at[j])
            return carry

        lax.fori_loop(0, NJ, kv_sent, 0)
        return carry

    lax.fori_loop(0, LAYERS, layer, 0)
    outs_w = (wqa, woa, wsa, w1a, w2a)
    for k in range(5):
        pltpu.make_async_copy(w_vm[k], outs_w[k], w_local.at[k]).start()
    line.drain(LAYERS * SLOTS)
    wait_dma(xcur, save.at[0])

    def last(j, carry):
        finish_y(LAYERS - 1, j)
        return carry

    lax.fori_loop(0, NJ, last, 0)

    def ho_done(j, carry):
        wait_dma(xcur.at[pl.ds(0, CH)], ho_s.at[j])
        return carry

    lax.fori_loop(0, NJ, ho_done, 0)
    for k in range(1, 4):
        wait_dma(h_out.at[0, pl.ds(0, ROWS)], ho_r.at[(p + k) % 4])
    wait_dma(kv.at[0], save.at[1])
    for k in (2, 3, 4):
        wait_dma(a_saves[k][0], save.at[k])
    wait_dma(xmid, save.at[5])
    for k in range(5):
        wait_dma(w_vm[k], w_local.at[k])
        wait_dma(w_vm[k].at[0], w_send.at[0, k])
        wait_dma(w_vm[k].at[0], w_send.at[1, k])
        wait_dma(w_vm[k].at[0], w_fwd.at[k])
    line.close()


def run_forward(x_in, wq, wo, w1, w2, ws):
    hbm = pl.BlockSpec(memory_space=pl.ANY)
    sds = jax.ShapeDtypeStruct
    dma = pltpu.SemaphoreType.DMA
    return pl.pallas_call(
        forward_kernel,
        out_shape=(sds((2, SEQ, D), BF), sds((LAYERS, ROWS, D), BF), sds((LAYERS, ROWS, D), BF),
                   sds((LAYERS, SEQ, KB), BF), sds((LAYERS, ROWS, W), BF), sds((LAYERS, ROWS, W), BF),
                   sds((LAYERS, 8 * NJ, KB), F32),
                   sds((LAYERS, D, 384), BF), sds((LAYERS, W, D), BF), sds((LAYERS, D, D), BF),
                   sds((LAYERS, D, D), BF), sds((LAYERS, 16, D), BF)),
        in_specs=[hbm] * 6,
        out_specs=[hbm] * 12,
        scratch_shapes=[
            pltpu.VMEM((LAYERS, D, 384), BF), pltpu.VMEM((LAYERS, W, D), BF), pltpu.VMEM((LAYERS, D, D), BF),
            pltpu.VMEM((LAYERS, D, D), BF), pltpu.VMEM((LAYERS, 16, D), BF),
            pltpu.VMEM((2, SEQ, KB), BF), pltpu.VMEM((ROWS, D), BF), pltpu.VMEM((ROWS, D), BF),
            pltpu.VMEM((ROWS, W), BF), pltpu.VMEM((ROWS, W), BF), pltpu.VMEM((8 * NJ, KB), F32),
            pltpu.VMEM((NJ, KB, KB), F32), pltpu.VMEM((KB, W), F32), pltpu.VMEM((KB, W), F32),
            *LINE_SCRATCH,
            dma((NJ,)), dma((5,)), dma((2, 5)), dma((LAYERS, 5)), dma((5,)), dma((NJ,)), dma((NJ,)), dma((NJ,)), dma((4,)), dma((6,)),
        ],
        compiler_params=pltpu.CompilerParams(collective_id=0, has_side_effects=True, vmem_limit_bytes=60 * 2**20),
        name="forward_layers",
    )(x_in, wq, wo, w1, w2, ws)


def backward_kernel(dy, xs, xm, kvs, qs, os_, lses, wqa, woa, w1a, w2a, wsa,
                    g_in, o_mlp, o_q, o_o, o_sm,
                    wqv, wov, w1v, w2v, wsv, xsv, xmv, kvv, qv, ov, lsev,
                    gcur, gm, dkv, pk, dqs, dq_acc, a_mlp, a_q, a_o, sm, rd_mlp, rd_q, rd_o, ry_mlp, ry_q, ry_o, rsm,
                    part, lbuf, hbuf, sbuf, fin, s1, s2, r_l, r_h, r_f,
                    load, dy_sem, dk_s, dk_r, gi_s, gi_r, d_s, d_r, y_s, y_r, o_sem, sm_s, sm_r):
    at = Place()
    line = LineSum(at, part, lbuf, hbuf, sbuf, fin, s1, s2, r_l, r_h, r_f)
    y, c, p = at.y, at.c, at.p
    loads = ((wsa, wsv), (xm, xmv), (w1a, w1v), (w2a, w2v), (xs, xsv), (kvs, kvv), (qs, qv), (os_, ov), (lses, lsev),
             (wqa, wqv), (woa, wov))

    for j in range(NJ):
        pltpu.make_async_copy(dy.at[y, at.tile_rows(j)], gcur.at[chunk_rows(j)], dy_sem.at[j]).start()
    for l in reversed(range(LAYERS)):
        for k, (src, dst) in enumerate(loads):
            pltpu.make_async_copy(src.at[l], dst.at[l], load.at[l, k]).start()
    at.enter()

    groups = {0: ((a_mlp, rd_mlp, ry_mlp, o_mlp),), 1: ((a_q, rd_q, ry_q, o_q), (a_o, rd_o, ry_o, o_o))}

    def add_into(dst, src):
        n = dst.shape[0]

        def body(i, carry):
            rows = pl.ds(pl.multiple_of(i * 64, 64), 64)
            dst[rows, :] += src[rows, :]
            return carry

        lax.fori_loop(0, n // 64, body, 0)

    def clear(dst):
        n = dst.shape[0]

        def body(i, carry):
            rows = pl.ds(pl.multiple_of(i * 64, 64), 64)
            dst[rows, :] = jnp.zeros((64, dst.shape[1]), F32)
            return carry

        lax.fori_loop(0, n // 64, body, 0)

    def grad_to_mate(l, g):
        @when(c != l % 2)
        def _():
            for k, (acc, rd, _, _) in enumerate(groups[g]):
                send(acc, rd, d_s.at[g, k], d_r.at[g, k], {"pp": at.mate})

    def grad_across(l, g):
        @when(c != l % 2)
        def _():
            for k, (acc, rd, _, _) in enumerate(groups[g]):
                wait_dma(acc, d_s.at[g, k])

        @when(c == l % 2)
        def _():
            for k, (acc, rd, ry, _) in enumerate(groups[g]):
                wait_dma(rd, d_r.at[g, k])
                add_into(rd, acc)

                @when(y != l // 2)
                def _():
                    send(rd, ry, y_s.at[g, k], y_r.at[g, k], {"pp": at.across})

    def grad_home(l, g):
        @when((c == l % 2) & (y != l // 2))
        def _():
            for k, (_, rd, _, _) in enumerate(groups[g]):
                wait_dma(rd, y_s.at[g, k])

        @when(p == l)
        def _():
            for k, (_, rd, ry, out) in enumerate(groups[g]):
                wait_dma(ry, y_r.at[g, k])
                add_into(ry, rd)
                pltpu.make_async_copy(ry, out, o_sem.at[g, k]).start()

    def add_small(l, r, value):
        sm[l, r:r + 1, :] += value

    for l in range(LAYERS):
        sm[l] = jnp.zeros((16, D), F32)

    def finish_layer(l, j):
        rows = chunk_rows(j)
        dh1 = line.get(NJ + (NJ - 1 - j))
        small = wsv[l].astype(F32)
        xhat, rstd = ln_stats(xsv[l, rows, :].astype(F32))
        add_small(l, 0, colsum(dh1 * xhat))
        add_small(l, 1, colsum(dh1))
        out = (gm[rows, :] + ln_back(dh1, xhat, rstd, small[0:1])).astype(BF)

        @when(l < LAYERS - 1)
        def _():
            wait_dma(gcur.at[rows], gi_s.at[j])

        gcur[rows, :] = out
        dst = g_in.at[y, at.tile_rows(j)]

        @when(p == l)
        def _():
            pltpu.make_async_copy(gcur.at[rows], dst, gi_s.at[j]).start()

        @when(p != l)
        def _():
            send(gcur.at[rows], dst, gi_s.at[j], gi_r.at[p], {"pp": l})

    def mlp_back(l, i):
        j = NJ - 1 - i
        rows = chunk_rows(j)

        @when(l == LAYERS - 1)
        def _():
            wait_dma(gcur.at[rows], dy_sem.at[j])

        @when(l < LAYERS - 1)
        def _():
            finish_layer(l + 1, j)

        small = wsv[l].astype(F32)
        g = gcur[rows, :]
        xhat, _ = ln_stats(xmv[l, rows, :].astype(F32))
        h2 = (xhat * small[2:3] + small[3:4]).astype(BF)
        u = nn(h2, w1v[l]) + small[6:7]
        t = jnp.tanh(GELU_C * (u + GELU_A * u * u * u))
        half = 0.5 * (1.0 + t)
        a = (u * half).astype(BF)
        slope = half + 0.5 * u * (1.0 - t * t) * (GELU_C * (1.0 + 3.0 * GELU_A * u * u))
        dpre = nt(g, w2v[l]) * slope
        add_small(l, 5, colsum(g.astype(F32)))
        add_small(l, 6, colsum(dpre))
        dpre = dpre.astype(BF)
        line.emit(2 * NJ * (LAYERS - 1 - l) + i, nt(dpre, w1v[l]))
        a_mlp[0:D, :] += tn(h2, dpre)
        a_mlp[D:2 * D, :] += tn(a, g)

    def attn_back(l, i):
        j = NJ - 1 - i
        rows = chunk_rows(j)
        small = wsv[l].astype(F32)
        dh2 = line.get(i)
        xhat, rstd = ln_stats(xmv[l, rows, :].astype(F32))
        add_small(l, 2, colsum(dh2 * xhat))
        add_small(l, 3, colsum(dh2))
        wide = gcur[rows, :].astype(F32) + ln_back(dh2, xhat, rstd, small[2:3])
        gm[rows, :] = wide
        add_small(l, 4, colsum(wide))
        gmid = wide.astype(BF)
        o = ov[l, rows, :]
        a_o[...] += tn(o, gmid)
        do = nt(gmid, wov[l]).astype(BF)
        prod = do.astype(F32) * o.astype(F32)
        delta = jnp.sum(head_stack(prod), axis=-1, keepdims=True)
        delta = jnp.broadcast_to(delta, (KB, W)).T[0:1]
        lse = lsev[l, pl.ds(pl.multiple_of(j * 8, 8), 8), :][0:1]
        q2 = head_stack(qv[l, rows, :] * jnp.asarray(0.125, BF))
        do2 = head_stack(do)
        dq_acc[...] = jnp.zeros_like(dq_acc)

        def block(kb, masked):
            krows = pl.ds(pl.multiple_of(kb * KB, KB), KB)
            k = kvv[l, krows, 0:W]
            v = kvv[l, krows, W:KB]
            st = nt(k, q2)
            if masked:
                row = lax.broadcasted_iota(jnp.int32, (KB, KB), 0)
                col = lax.broadcasted_iota(jnp.int32, (KB, KB), 1) % CH + CH * ((c + j) % 2)
                st = jnp.where(col >= row, st, -1e30)
            pt = jnp.exp(st - lse)
            dpt = nt(v, do2)
            dst = (pt * (dpt - delta)).astype(BF)
            dkv[krows, 0:W] += nn(dst, q2)
            dkv[krows, W:KB] += nn(pt.astype(BF), do2)
            dq_acc[...] += tn(dst, k)

        def body(kb, carry):
            block(kb, False)
            return carry

        lax.fori_loop(0, j, body, 0)
        block(j, True)
        dqs[rows, :] = (head_merge(dq_acc[...]) * 0.125).astype(BF)
        theirs = at.mate_rows(j)
        send(dkv.at[theirs], pk.at[j], dk_s.at[j], dk_r.at[j], {"pp": at.mate})

    def qkv_back(l, i):
        j = NJ - 1 - i
        rows = chunk_rows(j)
        small = wsv[l].astype(F32)
        wait_dma(pk.at[j], dk_r.at[j])
        dkv_own = (dkv[at.tile_rows(j), :] + pk[j]).astype(BF)
        dqkv = jnp.concatenate([dqs[rows, :], dkv_own], axis=1)
        sm[l, 7:8, 0:384] += colsum(dqkv.astype(F32))
        line.emit(2 * NJ * (LAYERS - 1 - l) + NJ + i, nt(dqkv, wqv[l]))
        xhat, _ = ln_stats(xsv[l, rows, :].astype(F32))
        h1 = (xhat * small[0:1] + small[1:2]).astype(BF)
        a_q[...] += tn(h1, dqkv)

    def layer(n, carry):
        l = LAYERS - 1 - n
        for k, (_, dst) in enumerate(loads):
            wait_dma(dst.at[l], load.at[l, k])
        clear(a_mlp)

        def first_half(i, carry):
            @when((i == 4) & (l < LAYERS - 2))
            def _():
                grad_home(l + 2, 1)

            @when((i == 4) & (l < LAYERS - 1))
            def _():
                grad_across(l + 1, 1)

            mlp_back(l, i)
            return carry

        lax.fori_loop(0, NJ, first_half, 0)
        grad_to_mate(l, 0)
        clear(a_q)
        clear(a_o)
        clear(dkv)

        def second_half(i, carry):
            @when((i == 4) & (l < LAYERS - 1))
            def _():
                grad_home(l + 1, 0)

            @when(i == 4)
            def _():
                grad_across(l, 0)

            @when(i < NJ)
            def _():
                attn_back(l, i)

            @when(i > 0)
            def _():
                qkv_back(l, i - 1)

            return carry

        lax.fori_loop(0, NJ + 1, second_half, 0)
        grad_to_mate(l, 1)

        def dk_sent(j, carry):
            wait_dma(pk.at[j], dk_s.at[j])
            return carry

        lax.fori_loop(0, NJ, dk_sent, 0)
        return carry

    lax.fori_loop(0, LAYERS, layer, 0)
    grad_home(1, 1)
    grad_across(0, 1)
    line.drain(LAYERS * SLOTS)

    def last(i, carry):
        finish_layer(0, NJ - 1 - i)
        return carry

    lax.fori_loop(0, NJ, last, 0)
    for s in range(LAYERS):
        @when(p != s)
        def _():
            send(sm.at[s], rsm.at[p], sm_s.at[s], sm_r.at[p], {"pp": s})
    grad_home(0, 0)
    grad_home(0, 1)

    def gi_done(j, carry):
        wait_dma(gcur.at[pl.ds(0, CH)], gi_s.at[j])
        return carry

    lax.fori_loop(0, NJ, gi_done, 0)
    for s in range(LAYERS):
        @when(p != s)
        def _():
            wait_dma(sm.at[s], sm_s.at[s])
            wait_dma(rsm.at[s], sm_r.at[s])
    rsm[p] = sm[p]
    o_sm[...] = (rsm[0] + rsm[1]) + (rsm[2] + rsm[3])
    for k in range(1, 4):
        wait_dma(g_in.at[0, pl.ds(0, ROWS)], gi_r.at[(p + k) % 4])
    for g, items in groups.items():
        for k, (_, _, ry, _) in enumerate(items):
            wait_dma(ry, o_sem.at[g, k])
    line.close()


def run_backward(*args):
    hbm = pl.BlockSpec(memory_space=pl.ANY)
    sds = jax.ShapeDtypeStruct
    dma = pltpu.SemaphoreType.DMA
    grads = [pltpu.VMEM((2 * D, D), F32), pltpu.VMEM((D, 384), F32), pltpu.VMEM((W, D), F32)]
    return pl.pallas_call(
        backward_kernel,
        out_shape=(sds((2, SEQ, D), BF), sds((2 * D, D), F32), sds((D, 384), F32), sds((W, D), F32), sds((16, D), F32)),
        in_specs=[hbm] * 12,
        out_specs=[hbm] * 4 + [pl.BlockSpec(memory_space=pltpu.VMEM)],
        scratch_shapes=[
            pltpu.VMEM((LAYERS, D, 384), BF), pltpu.VMEM((LAYERS, W, D), BF), pltpu.VMEM((LAYERS, D, D), BF),
            pltpu.VMEM((LAYERS, D, D), BF), pltpu.VMEM((LAYERS, 16, D), BF),
            pltpu.VMEM((LAYERS, ROWS, D), BF), pltpu.VMEM((LAYERS, ROWS, D), BF), pltpu.VMEM((LAYERS, SEQ, KB), BF),
            pltpu.VMEM((LAYERS, ROWS, W), BF), pltpu.VMEM((LAYERS, ROWS, W), BF), pltpu.VMEM((LAYERS, 8 * NJ, KB), F32),
            pltpu.VMEM((ROWS, D), BF), pltpu.VMEM((ROWS, D), F32), pltpu.VMEM((SEQ, KB), F32), pltpu.VMEM((NJ, CH, KB), F32),
            pltpu.VMEM((ROWS, W), BF), pltpu.VMEM((KB, W), F32),
            *grads, pltpu.VMEM((LAYERS, 16, D), F32), *grads, *grads, pltpu.VMEM((LAYERS, 16, D), F32),
            *LINE_SCRATCH,
            dma((LAYERS, 11)), dma((NJ,)), dma((NJ,)), dma((NJ,)), dma((NJ,)), dma((4,)),
            dma((2, 2)), dma((2, 2)), dma((2, 2)), dma((2, 2)), dma((2, 2)), dma((4,)), dma((4,)),
        ],
        compiler_params=pltpu.CompilerParams(collective_id=1, has_side_effects=True, vmem_limit_bytes=63 * 2**20),
        name="backward_layers",
    )(*args)


def solution(mesh):
    def program(x_in, dy_out, w_qkv, b_qkv, w_out, b_out, ln_par, w_fc1, b_fc1, w_fc2, b_fc2):
        wq = w_qkv[0].transpose(1, 0, 2, 3).reshape(D, 384)
        wo = w_out[0].reshape(W, D)
        bq = jnp.pad(b_qkv[0].reshape(1, 384), ((0, 0), (0, D - 384)))
        ws = jnp.concatenate([ln_par[0], b_out, b_fc2, b_fc1, bq, jnp.zeros((8, D), BF)], axis=0)
        fwd = run_forward(x_in.reshape(2, SEQ, D), wq, wo, w_fc1[0], w_fc2[0], ws)
        g_in, d_mlp, d_q, d_o, d_sm = run_backward(dy_out.reshape(2, SEQ, D), *fwd[1:])
        return (fwd[0].reshape(1, 2, 1, SEQ, D), g_in.reshape(1, 2, 1, SEQ, D),
                d_q.reshape(D, 3, 2, 64).transpose(1, 0, 2, 3)[None], d_sm[7, :384].reshape(1, 3, 2, 64),
                d_o.reshape(1, 2, 64, D), d_sm[4:5], d_sm[None, 0:4],
                d_mlp[None, :D], d_sm[6:7], d_mlp[None, D:], d_sm[5:6])

    act_spec = P(NO, "dp", NO, NO)
    arg_specs = (act_spec, act_spec,
                 P("pp", NO, NO, "tp", NO), P("pp", NO, "tp", NO), P("pp", "tp", NO, NO),
                 P("pp", NO), P("pp", NO, NO), P("pp", NO, "tp"), P("pp", "tp"),
                 P("pp", "tp", NO), P("pp", NO))
    stage_spec = P("pp", NO, "dp", NO, NO)
    grad_axes = ("dp", "pp")
    result_specs = (stage_spec, stage_spec,
                    P(grad_axes, NO, NO, "tp", NO), P(grad_axes, NO, "tp", NO), P(grad_axes, "tp", NO, NO),
                    P(grad_axes, NO), P(grad_axes, NO, NO), P(grad_axes, NO, "tp"), P(grad_axes, "tp"),
                    P(grad_axes, "tp", NO), P(grad_axes, NO))
    return jax.shard_map(program, mesh=mesh, in_specs=arg_specs, out_specs=result_specs, check_vma=False)
```

time: 3240 us -> 518 us (0.16)
  waiting for transfers between devices: 1930 us -> 0 us
  matrix products: 872 us -> 0 us
  Pallas kernels: 0 us -> 494 us
  other arithmetic: 300 us -> 0 us
  local copies, waits for them, and re-layouts: 90.9 us -> 20.7 us
    psum x20 -> x0, waiting for transfers between devices: 1540 us -> none  [the longest x5 430 us: layer_forward(): attn_sum = lax.psum(attn_part, 'tp')]
    dot_general x80 -> x0, matrix products: 671 us -> none  [the longest x15 228 us: causal_attention(): jnp.einsum('bhqk,bkhe->bqhe', attn_probs, v_heads, preferred_element_type...]
    pallas_call x0 -> x2, Pallas kernels: none -> 494 us  [the longest x1 280 us: run_backward(): pl.pallas_call(backward_kernel, out_shape=(sds((2, SEQ, D), BF), sds((2 *...]
    all_gather x10 -> x0, waiting for transfers between devices: 363 us -> none  [pass_on(): return lax.all_gather(moved_part, 'tp', axis=1, tiled=True)]
    sub x10 -> x0, matrix products: 193 us -> none  [causal_attention(): attn_probs = jax.nn.softmax(scores, axis=-1).astype(jnp.bfloat16)]
    reduce_sum x60 -> x0, other arithmetic: 146 us -> none  [the longest x20 54.5 us: layer_norm(): row_var = jnp.mean(centered * centered, axis=-1, keepdims=True)]
    dynamic_update_slice x25 -> x0, other arithmetic: 96.9 us -> none  [the longest x5 24 us: bwd_step(): grad_buf = lax.dynamic_update_index_in_dim(grad_buf, grad_in, write_idx, 0)]
    ge x10 -> x0, other arithmetic: 41.4 us -> none  [causal_attention(): scores = jnp.where(row_pos >= col_pos, scores, -1e+30)]
  transfers between devices with their start and end apart: 40 -> 0, of which waited for: 40 -> 0; matrix products, arithmetic and copies ran while one was open for 10% -> 0% of each run, Pallas kernels for 0% -> 0%
where the time goes in v1:
time: 518 us; the launch traced here: 516 us
  Pallas kernels  494 us (95%)
  local copies, waits for them, and re-layouts  20.7 us (4%)
    pallas_call x1, Pallas kernels, run_backward(): pl.pallas_call(backward_kernel, out_shape=(sds((2, SEQ, D), BF), sds((2 *...  280 us
    pallas_call x1, Pallas kernels, run_forward(): pl.pallas_call(forward_kernel, out_shape=(sds((2, SEQ, D), BF), sds((LAYE...  214 us

profile of v1, /device:TPU:0, one launch (start us, length us, event | category | flops | bytes accessed | tf_op | source)
XLA Modules:
  0.0 515.6 jit_solution(10756097498483329172)
XLA Ops:
  0.6 0.8 reshape_squeeze.10
  1.4 2.0 concatenate.3.ws
  3.4 1.9 copy.26.wq
  5.3 213.9 %forward_layers.1 = (bf16[2,2048,512]{2,1,0:T(8,128)(2,1)}, bf16[4,1024,512]{2,1,0:T(8,128)(2,1)}, bf16[4,1024,512]{2,1,0:T(8,128)(2,1)}, bf16[4,2048,256]{2,1,0...) custom-call(bf16[2,2048,512]{2,1,0:T(8,128)(2,1)} %bitcast.30, ...), custom_call_target="tpu_custom_call" | custom-call | tf_op jit(solution)/shard_map/forward_layers/pallas_call | solution.py:437
  219.2 280.3 %backward_layers.1 = (bf16[2,2048,512]{2,1,0:T(8,128)(2,1)}, f32[1024,512]{1,0:T(8,128)}, f32[512,384]{1,0:T(8,128)}, f32[128,512]{1,0:T(8,128)}, f32[16,512]{1,0:T(8,128)}) custom-call(bf16[2,2048,512]{2,1,0:T(8,128)(2,1)} %bitcast.29, bf16[4,1024,512]{2,1,0:T(8,128)(2,1)} %get-tuple-element.29.xs, bf16[4,1024,512]{2,1,0:T(8,128)(2,1)} %get-tuple-element.30.xm, ...), custom_call_target="tpu_custom_call" | custom-call | tf_op jit(solution)/shard_map/backward_layers/pallas_call | solution.py:752
  499.6 0.7 slice_reduce_fusion
  500.3 0.7 reshape_squeeze.11
  501.0 1.4 fusion
  502.4 1.3 slice_bitcast_fusion.2
  503.7 2.3 copy.27
  506.0 0.0 copy-start
  506.0 3.2 slice_bitcast_fusion
  509.2 0.0 copy-done
  509.2 0.0 copy-start.1
  509.2 2.1 copy.33
  511.3 1.6 copy-done.1
  512.9 0.0 copy-start.2
  512.9 2.0 copy.34
  514.9 0.0 copy-done.2
  514.9 0.7 copy.35
  (2 shorter events, 0.0 us)
Async XLA Ops:
  506.0 3.2 copy-start
  509.2 3.7 copy-start.1
  512.9 2.0 copy-start.2

commit v2 on v0

v2 whole, which is shorter than its diff:
```python
import jax
import jax.numpy as jnp
from jax import lax
from jax.experimental import pallas as pl
from jax.experimental.pallas import tpu as pltpu
from jax.sharding import PartitionSpec as P

LN_EPS = 1e-5
BF = jnp.bfloat16
F32 = jnp.float32
MESH = pl.DeviceIdType.MESH

LAYERS = 4
SEQ = 2048
D = 512
CH = 128
NJ = 8
PAIRS = NJ // 2
ROWS = CH * NJ
SLOTS = 2 * NJ
FWD = LAYERS * SLOTS
W = 128
QKV = 3 * W
KB = 256
WIDE = 2 * KB
SMALL = 16
GELU_C = 0.7978845608028654
GELU_A = 0.044715
MASKED = -1e30
NO = None
GAIN1, SHIFT1, GAIN2, SHIFT2, BOUT, BFC2, BFC1, BQKV = range(8)


def nn(a, b):
    return lax.dot_general(a, b, (((1,), (0,)), ((), ())), preferred_element_type=F32)


def nt(a, b):
    return lax.dot_general(a, b, (((1,), (1,)), ((), ())), preferred_element_type=F32)


def tn(a, b):
    return lax.dot_general(a, b, (((0,), (0,)), ((), ())), preferred_element_type=F32)


def ln_stats(x_wide):
    mean = jnp.mean(x_wide, axis=-1, keepdims=True)
    cent = x_wide - mean
    var = jnp.mean(cent * cent, axis=-1, keepdims=True)
    rstd = lax.rsqrt(var + LN_EPS)
    return cent * rstd, rstd


def ln_back(dy, xhat, rstd, gain):
    dxhat = dy * gain
    m1 = jnp.mean(dxhat, axis=-1, keepdims=True)
    m2 = jnp.mean(dxhat * xhat, axis=-1, keepdims=True)
    return rstd * (dxhat - m1 - xhat * m2)


def colsum(v):
    return jnp.sum(v, axis=0, keepdims=True)


def row(small, r):
    return small[r:r + 1]


def blk(i, n):
    return pl.ds(pl.multiple_of(i * n, n), n)


def chunk(j):
    return blk(j, CH)


def loop(n, body):
    def step(i, carry):
        body(i)
        return carry

    lax.fori_loop(0, n, step, 0)


when = pl.when


def wait_dma(ref, sem):
    pltpu.make_async_copy(ref, ref, sem).wait()


def local(src, dst, sem):
    pltpu.make_async_copy(src, dst, sem).start()


def send(src, dst, ssem, rsem, dev):
    pltpu.make_async_remote_copy(src, dst, ssem, rsem, device_id=dev, device_id_type=MESH).start()


class Place:
    def __init__(self):
        self.z = lax.axis_index("tp")
        self.p = lax.axis_index("pp")
        self.y = self.p // 2
        self.c = self.p % 2
        self.hub = (self.z == 1) | (self.z == 2)
        self.leaf = jnp.logical_not(self.hub)
        self.my_hub = {"tp": jnp.where(self.z == 0, 1, 2)}
        self.my_leaf = {"tp": jnp.where(self.z == 1, 0, 3)}
        self.other_hub = {"tp": 3 - self.z}
        self.mate = {"pp": self.p + 1 - 2 * self.c}
        self.across = {"pp": 2 * (1 - self.y) + self.c}

    def rows_of(self, j):
        return chunk(2 * j + (self.c + j) % 2)

    def mate_rows(self, j):
        return chunk(2 * j + (self.c + j + 1) % 2)

    def enter(self):
        bar = pltpu.get_barrier_semaphore()

        def greet(dev):
            pl.semaphore_signal(bar, inc=1, device_id=dev, device_id_type=MESH)

        for k in range(1, LAYERS):
            greet({"pp": (self.p + k) % LAYERS})

        @when(self.z > 0)
        def _():
            greet({"tp": self.z - 1})

        @when(self.z < 3)
        def _():
            greet({"tp": self.z + 1})

        @when(self.hub)
        def _():
            pl.semaphore_wait(bar, 5)

        @when(self.leaf)
        def _():
            pl.semaphore_wait(bar, 4)


class LineSum:
    def __init__(self, at, part, lbuf, hbuf, fin, s1, s2, r_l, r_h, r_f):
        self.at, self.part, self.lbuf, self.hbuf, self.fin = at, part, lbuf, hbuf, fin
        self.s1, self.s2, self.r_l, self.r_h, self.r_f = s1, s2, r_l, r_h, r_f

    def emit(self, e, value):
        slot = e % SLOTS

        @when(e >= SLOTS)
        def _():
            wait_dma(self.part.at[slot], self.s1.at[slot])

        self.part[slot] = value.astype(BF)

        @when(self.at.leaf)
        def _():
            send(self.part.at[slot], self.lbuf.at[slot], self.s1.at[slot], self.r_l.at[slot], self.at.my_hub)

        self.serve_first(e - 2)
        self.serve_second(e - 4)

    def serve_first(self, e):
        slot = (e + SLOTS) % SLOTS

        @when(self.at.hub & (e >= 0))
        def _():
            wait_dma(self.lbuf.at[slot], self.r_l.at[slot])
            self.part[slot] = (self.part[slot].astype(F32) + self.lbuf[slot].astype(F32)).astype(BF)
            send(self.part.at[slot], self.hbuf.at[slot], self.s1.at[slot], self.r_h.at[slot], self.at.other_hub)

    def serve_second(self, e):
        slot = (e + SLOTS) % SLOTS

        @when(self.at.hub & (e >= 0))
        def _():
            wait_dma(self.hbuf.at[slot], self.r_h.at[slot])

            @when(e >= SLOTS)
            def _():
                wait_dma(self.fin.at[slot], self.s2.at[slot])

            self.fin[slot] = (self.part[slot].astype(F32) + self.hbuf[slot].astype(F32)).astype(BF)
            send(self.fin.at[slot], self.fin.at[slot], self.s2.at[slot], self.r_f.at[slot], self.at.my_leaf)

    def get(self, slot):
        @when(self.at.leaf)
        def _():
            wait_dma(self.fin.at[slot], self.r_f.at[slot])

        return self.fin[slot].astype(F32)

    def drain(self, total):
        self.serve_first(total - 2)
        self.serve_first(total - 1)
        for k in range(4):
            self.serve_second(total - 4 + k)

    def close(self):
        def body(slot):
            wait_dma(self.part.at[slot], self.s1.at[slot])

            @when(self.at.hub)
            def _():
                wait_dma(self.fin.at[slot], self.s2.at[slot])

        loop(SLOTS, body)


def head_stack(v):
    first = lax.broadcasted_iota(jnp.int32, v.shape, 1) < W // 2
    zero = jnp.zeros_like(v)
    return jnp.concatenate([jnp.where(first, v, zero), jnp.where(first, zero, v)], axis=0)


def head_merge(v):
    first = lax.broadcasted_iota(jnp.int32, (CH, W), 1) < W // 2
    return jnp.where(first, v[:CH], v[CH:])


def fold(v, op):
    out = v[:, :W]
    for k in range(1, v.shape[1] // W):
        out = op(out, v[:, k * W:(k + 1) * W])
    return out


def decoder_kernel(x_in, dy, wq, wo, w1, w2, ws,
                   h_out, g_in, o_w1, o_w2, o_q, o_o, o_sm,
                   wqv, wov, w1v, w2v, wsv, kv, xs, xm, qs, os_, lses, scores, acc, lsum,
                   gcur, gm, dkv, pk, buf_a, buf_b, buf_c, dq_acc,
                   a_w1, a_w2, a_q, a_o, d_w1, d_w2, d_q, d_o, y_w1, y_w2, y_q, y_o, sm, rsm,
                   part, lbuf, hbuf, fin, s1, s2, r_l, r_h, r_f,
                   x_sem, w_local, w_send, w_recv, w_fwd, kv_s, kv_r, ho_s, ho_r,
                   dy_sem, dk_s, dk_r, gi_s, gi_r, d_s, d_r, y_s, y_r, o_sem, sm_s, sm_r):
    at = Place()
    line = LineSum(at, part, lbuf, hbuf, fin, s1, s2, r_l, r_h, r_f)
    y, c, p = at.y, at.c, at.p
    w_hbm = (ws, wq, wo, w1, w2)
    w_vm = (wsv, wqv, wov, w1v, w2v)
    every = range(len(w_hbm))
    group_a, group_m = every[:3], every[3:]

    for j in range(NJ):
        local(x_in.at[y, at.rows_of(j)], xs.at[0, chunk(j)], x_sem.at[j])
    for k in every:
        local(w_hbm[k], w_vm[k].at[p], w_local.at[k])

    at.enter()

    def send_across():
        for k in every:
            send(w_hbm[k], w_vm[k].at[p], w_send.at[1, k], w_recv.at[p, k], at.across)

    @when(c == 0)
    def _():
        send_across()

    for k in every:
        send(w_hbm[k], w_vm[k].at[p], w_send.at[0, k], w_recv.at[p, k], at.mate)
    for j in range(NJ):
        local(dy.at[y, at.rows_of(j)], gcur.at[chunk(j)], dy_sem.at[j])

    def weights_ready(s, group):
        @when(p == s)
        def _():
            for k in group:
                wait_dma(w_vm[k].at[p], w_local.at[k])

        @when(p != s)
        def _():
            for k in group:
                wait_dma(w_vm[k].at[s], w_recv.at[s, k])

        @when((y != s // 2) & (c == s % 2))
        def _():
            for k in group:
                send(w_vm[k].at[s], w_vm[k].at[s], w_fwd.at[k], w_recv.at[s, k], at.mate)

    def send_home(l, src, dst, ssem, rsem):
        @when(p == l)
        def _():
            local(src, dst, ssem)

        @when(p != l)
        def _():
            send(src, dst, ssem, rsem.at[p], {"pp": l})

    weights_ready(0, group_a)

    def finish_y(l, j):
        rows = chunk(j)
        total = line.get(NJ + j)
        out = (xm[l, rows, :].astype(F32) + total + row(wsv[l].astype(F32), BFC2)).astype(BF)

        @when(l > 0)
        def _():
            wait_dma(gcur.at[rows], ho_s.at[j])

        xs[l + 1, rows, :] = out
        send_home(l, xs.at[l + 1, rows], h_out.at[y, at.rows_of(j)], ho_s.at[j], ho_r)

    def attn_op(l, jj, odd):
        j = 2 * jj + odd
        rows = chunk(j)

        @when(l == 0)
        def _():
            wait_dma(xs.at[0, rows], x_sem.at[j])

        @when(l > 0)
        def _():
            finish_y(l - 1, j)

        small = wsv[l].astype(F32)
        xhat, _ = ln_stats(xs[l, rows, :].astype(F32))
        h1 = (xhat * row(small, GAIN1) + row(small, SHIFT1)).astype(BF)
        qkv = (nt(h1, wqv[l]) + row(small, BQKV)[:, :QKV]).astype(BF)
        q = qkv[:, :W]
        mine = at.rows_of(j)
        kv[l, mine, :] = qkv[:, W:]
        send(kv.at[l, mine], kv.at[l, mine], kv_s.at[j], kv_r.at[j], at.mate)
        qs[l, rows, :] = q
        q2 = head_stack(q * jnp.asarray(0.125, BF))

        def pass_one(kb, best):
            s = nt(q2, kv[l, blk(kb, WIDE), 0:W])
            scores[kb] = s
            return jnp.maximum(best, fold(s, jnp.maximum))

        best = lax.fori_loop(0, jj, pass_one, jnp.full((KB, W), MASKED, F32))
        wait_dma(kv.at[l, mine], kv_r.at[j])
        width = KB * (1 + odd)
        tail = pl.ds(pl.multiple_of(jj * WIDE, WIDE), width)
        s = nt(q2, kv[l, tail, 0:W])
        pos = lax.broadcasted_iota(jnp.int32, (KB, width), 0) % CH + (KB * odd + CH * ((c + odd) % 2))
        s = jnp.where(pos >= lax.broadcasted_iota(jnp.int32, (KB, width), 1), s, MASKED)
        scores[jj, :, 0:width] = s
        top = jnp.max(jnp.maximum(best, fold(s, jnp.maximum)), axis=-1, keepdims=True)
        acc[...] = jnp.zeros_like(acc)
        lsum[...] = jnp.zeros_like(lsum)

        def weigh(s, keys):
            e = jnp.exp(s - top)
            lsum[...] += fold(e, jnp.add)
            acc[...] += nn(e.astype(BF), kv[l, keys, W:])

        loop(jj, lambda kb: weigh(scores[kb], blk(kb, WIDE)))
        weigh(scores[jj, :, 0:width], tail)
        den = jnp.sum(lsum[...], axis=-1, keepdims=True)
        o = head_merge(acc[...] / den).astype(BF)
        os_[l, rows, :] = o
        lses[l, blk(j, 8), :] = jnp.broadcast_to(top + jnp.log(den), (KB, W)).T[:8]
        line.emit(SLOTS * l + j, nn(o, wov[l]))

    def mlp_op(l, j):
        rows = chunk(j)
        small = wsv[l].astype(F32)
        mid = (xs[l, rows, :].astype(F32) + line.get(j) + row(small, BOUT)).astype(BF)
        xm[l, rows, :] = mid
        xhat, _ = ln_stats(mid.astype(F32))
        h2 = (xhat * row(small, GAIN2) + row(small, SHIFT2)).astype(BF)
        u = nn(h2, w1v[l]) + row(small, BFC1)
        a = 0.5 * u * (1.0 + jnp.tanh(GELU_C * (u + GELU_A * u * u * u)))
        line.emit(SLOTS * l + NJ + j, nn(a.astype(BF), w2v[l]))

    def forward_layer(l):
        def attn_pair(jj):
            with jax.named_scope("attn"):
                attn_op(l, jj, 0)
            with jax.named_scope("attn"):
                attn_op(l, jj, 1)

            @when((l == 0) & (jj == 0) & (c == 1))
            def _():
                send_across()

        loop(PAIRS, attn_pair)

        @when(l == 0)
        def _():
            weights_ready(0, group_m)

        def mlp_step(j):
            with jax.named_scope("mlp"):
                mlp_op(l, j)

            @when((j == NJ - 2) & (l < LAYERS - 1))
            def _():
                weights_ready(l + 1, every)

        loop(NJ, mlp_step)
        loop(NJ, lambda j: wait_dma(kv.at[0, chunk(0)], kv_s.at[j]))

    for l in range(LAYERS):
        sm[l] = jnp.zeros((SMALL, D), F32)
    loop(LAYERS, forward_layer)

    groups = (((a_w1, d_w1, y_w1, o_w1), (a_w2, d_w2, y_w2, o_w2)), ((a_q, d_q, y_q, o_q), (a_o, d_o, y_o, o_o)))

    def add_into(dst, src):
        def body(i):
            rows = blk(i, 64)
            dst[rows, :] += src[rows, :]

        loop(dst.shape[0] // 64, body)

    def grad_to_mate(l, g):
        @when(c != l % 2)
        def _():
            for k, (own, mid, _, _) in enumerate(groups[g]):
                send(own, mid, d_s.at[g, k], d_r.at[g, k], at.mate)

    def grad_across(l, g):
        @when(c != l % 2)
        def _():
            for k, (own, _, _, _) in enumerate(groups[g]):
                wait_dma(own, d_s.at[g, k])

        @when(c == l % 2)
        def _():
            for k, (own, mid, far, _) in enumerate(groups[g]):
                wait_dma(mid, d_r.at[g, k])
                add_into(mid, own)

                @when(y != l // 2)
                def _():
                    send(mid, far, y_s.at[g, k], y_r.at[g, k], at.across)

    def grad_home(l, g):
        @when((c == l % 2) & (y != l // 2))
        def _():
            for k, (_, mid, _, _) in enumerate(groups[g]):
                wait_dma(mid, y_s.at[g, k])

        @when(p == l)
        def _():
            for k, (_, mid, far, out) in enumerate(groups[g]):
                wait_dma(far, y_r.at[g, k])
                add_into(far, mid)
                local(far, out, o_sem.at[g, k])

    def add_small(l, r, value):
        sm[l, r:r + 1, :] += value

    def finish_layer(l, j):
        rows = chunk(j)
        dh1 = line.get(SLOTS - 1 - j)
        xhat, rstd = ln_stats(xs[l, rows, :].astype(F32))
        add_small(l, GAIN1, colsum(dh1 * xhat))
        add_small(l, SHIFT1, colsum(dh1))
        out = (gm[rows, :] + ln_back(dh1, xhat, rstd, row(wsv[l].astype(F32), GAIN1))).astype(BF)

        @when(l < LAYERS - 1)
        def _():
            wait_dma(gcur.at[rows], gi_s.at[j])

        gcur[rows, :] = out
        send_home(l, gcur.at[rows], g_in.at[y, at.rows_of(j)], gi_s.at[j], gi_r)

    def mlp_back(l, i):
        j = NJ - 1 - i
        rows = chunk(j)

        @when(l == LAYERS - 1)
        def _():
            wait_dma(gcur.at[rows], dy_sem.at[j])
            finish_y(l, i)

        @when(l < LAYERS - 1)
        def _():
            finish_layer(l + 1, j)

        small = wsv[l].astype(F32)
        g = gcur[rows, :]
        xhat, _ = ln_stats(xm[l, rows, :].astype(F32))
        h2 = (xhat * row(small, GAIN2) + row(small, SHIFT2)).astype(BF)
        u = nn(h2, w1v[l]) + row(small, BFC1)
        t = jnp.tanh(GELU_C * (u + GELU_A * u * u * u))
        half = 0.5 * (1.0 + t)
        slope = half + 0.5 * u * (1.0 - t * t) * (GELU_C * (1.0 + 3.0 * GELU_A * u * u))
        dpre = nt(g, w2v[l]) * slope
        add_small(l, BFC2, colsum(g.astype(F32)))
        add_small(l, BFC1, colsum(dpre))
        dpre = dpre.astype(BF)
        buf_a[rows, :] = h2
        buf_b[rows, :] = dpre
        buf_c[rows, :] = (u * half).astype(BF)
        line.emit(FWD + SLOTS * (LAYERS - 1 - l) + i, nt(dpre, w1v[l]))

    def mlp_weight_grads():
        def body(t):
            cols = blk(t, KB)
            a_w1[:, cols] = tn(buf_a[...], buf_b[:, cols])
            a_w2[:, cols] = tn(buf_c[...], gcur[:, cols])

        loop(D // KB, body)

    def attn_back(l, jj, odd):
        j = 2 * jj + odd
        rows = chunk(j)
        small = wsv[l].astype(F32)
        dh2 = line.get(NJ - 1 - j)
        xhat, rstd = ln_stats(xm[l, rows, :].astype(F32))
        add_small(l, GAIN2, colsum(dh2 * xhat))
        add_small(l, SHIFT2, colsum(dh2))
        wide = gcur[rows, :].astype(F32) + ln_back(dh2, xhat, rstd, row(small, GAIN2))
        gm[rows, :] = wide
        add_small(l, BOUT, colsum(wide))
        gmid = wide.astype(BF)
        buf_c[rows, :] = gmid
        do = nt(gmid, wov[l]).astype(BF)
        delta = jnp.sum(head_stack(do.astype(F32) * os_[l, rows, :].astype(F32)), axis=-1, keepdims=True)
        delta = jnp.broadcast_to(delta, (KB, W)).T[0:1]
        lse = lses[l, blk(j, 8), :][0:1]
        q2 = head_stack(qs[l, rows, :] * jnp.asarray(0.125, BF))
        do2 = head_stack(do)
        dq_acc[...] = jnp.zeros_like(dq_acc)

        def block(keys, width, masked):
            k = kv[l, keys, 0:W]
            st = nt(k, q2)
            if masked:
                pos = lax.broadcasted_iota(jnp.int32, (width, KB), 1) % CH + (KB * odd + CH * ((c + odd) % 2))
                st = jnp.where(pos >= lax.broadcasted_iota(jnp.int32, (width, KB), 0), st, MASKED)
            pt = jnp.exp(st - lse)
            dst = (pt * (nt(kv[l, keys, W:], do2) - delta)).astype(BF)
            dk = nn(dst, q2)
            dv = nn(pt.astype(BF), do2)
            dq_acc[...] += tn(dst, k)
            dkv[keys, 0:W] += dk
            dkv[keys, W:] += dv

        loop(jj, lambda kb: block(blk(kb, WIDE), WIDE, False))
        width = KB * (1 + odd)
        block(pl.ds(pl.multiple_of(jj * WIDE, WIDE), width), width, True)
        buf_b[rows, 0:W] = (head_merge(dq_acc[...]) * 0.125).astype(BF)
        send(dkv.at[at.mate_rows(j)], pk.at[j], dk_s.at[j], dk_r.at[j], at.mate)

    def qkv_back(l, j):
        rows = chunk(j)
        small = wsv[l].astype(F32)
        xhat, _ = ln_stats(xs[l, rows, :].astype(F32))
        buf_a[rows, :] = (xhat * row(small, GAIN1) + row(small, SHIFT1)).astype(BF)
        wait_dma(pk.at[j], dk_r.at[j])
        dkv_own = (dkv[at.rows_of(j), :] + pk[j]).astype(BF)
        buf_b[rows, W:QKV] = dkv_own
        dqkv = jnp.concatenate([buf_b[rows, 0:W], dkv_own], axis=1)
        sm[l, BQKV:BQKV + 1, 0:QKV] += colsum(dqkv.astype(F32))
        line.emit(FWD + SLOTS * (LAYERS - l) - 1 - j, nn(dqkv, wqv[l]))

    def backward_layer(n):
        l = LAYERS - 1 - n

        def first_half(i):
            @when(i == 2)
            def _():
                @when(l < LAYERS - 2)
                def _():
                    grad_home(l + 2, 1)

                @when(l < LAYERS - 1)
                def _():
                    grad_across(l + 1, 1)

            with jax.named_scope("B1"):
                mlp_back(l, i)

        loop(NJ, first_half)
        with jax.named_scope("dw1"):
            mlp_weight_grads()
        grad_to_mate(l, 0)

        def clear(i):
            dkv[blk(i, 64), :] = jnp.zeros((64, KB), F32)

        loop(SEQ // 64, clear)

        def second_half(ii):
            jj = PAIRS - 1 - ii

            @when(ii == 1)
            def _():
                @when(l < LAYERS - 1)
                def _():
                    grad_home(l + 1, 0)

                grad_across(l, 0)

            with jax.named_scope("B2"):
                attn_back(l, jj, 1)

            @when(ii > 0)
            def _():
                with jax.named_scope("B3"):
                    qkv_back(l, 2 * jj + 2)

            with jax.named_scope("B2"):
                attn_back(l, jj, 0)
            with jax.named_scope("B3"):
                qkv_back(l, 2 * jj + 1)

        loop(PAIRS, second_half)
        qkv_back(l, 0)
        with jax.named_scope("dw2"):
            a_q[...] = tn(buf_b[:, 0:QKV], buf_a[...])
            a_o[...] = tn(os_[l], buf_c[...])
        grad_to_mate(l, 1)
        loop(NJ, lambda j: wait_dma(pk.at[j], dk_s.at[j]))

    loop(LAYERS, backward_layer)
    line.drain(FWD + LAYERS * SLOTS)
    grad_across(0, 1)
    loop(NJ, lambda i: finish_layer(0, NJ - 1 - i))
    for s in range(LAYERS):
        @when(p != s)
        def _():
            send(sm.at[s], rsm.at[p], sm_s.at[s], sm_r.at[p], {"pp": s})
    grad_home(1, 1)
    grad_home(0, 0)
    grad_home(0, 1)
    for s in range(LAYERS):
        @when(p != s)
        def _():
            wait_dma(sm.at[s], sm_s.at[s])
            wait_dma(rsm.at[s], sm_r.at[s])
    rsm[p] = sm[p]
    o_sm[...] = (rsm[0] + rsm[1]) + (rsm[2] + rsm[3])

    def sent(j):
        wait_dma(gcur.at[chunk(0)], ho_s.at[j])
        wait_dma(gcur.at[chunk(0)], gi_s.at[j])

    loop(NJ, sent)
    for k in range(1, LAYERS):
        wait_dma(h_out.at[0, pl.ds(0, ROWS)], ho_r.at[(p + k) % LAYERS])
        wait_dma(g_in.at[0, pl.ds(0, ROWS)], gi_r.at[(p + k) % LAYERS])
    for g, items in enumerate(groups):
        for k, (_, _, far, _) in enumerate(items):
            wait_dma(far, o_sem.at[g, k])
    for k in every:
        wait_dma(w_vm[k].at[0], w_send.at[0, k])
        wait_dma(w_vm[k].at[0], w_send.at[1, k])
        wait_dma(w_vm[k].at[0], w_fwd.at[k])
    line.close()


def run_layers(*args):
    hbm = pl.BlockSpec(memory_space=pl.ANY)
    dma = pltpu.SemaphoreType.DMA
    slots = pltpu.VMEM((SLOTS, CH, D), BF)
    slot_sem = dma((SLOTS,))
    chunk_sem = dma((NJ,))
    stage_sem = dma((LAYERS,))
    pair_sem = dma((2, 2))

    def bf(*shape):
        return pltpu.VMEM(shape, BF)

    def f32(*shape):
        return pltpu.VMEM(shape, F32)

    grad_shapes = ((D, D), (D, D), (QKV, D), (W, D))
    grads = [f32(*shape) for shape in grad_shapes]
    acts = jax.ShapeDtypeStruct((2, SEQ, D), BF)
    return pl.pallas_call(
        decoder_kernel,
        out_shape=[acts, acts, *(jax.ShapeDtypeStruct(shape, F32) for shape in (*grad_shapes, (SMALL, D)))],
        in_specs=[hbm] * len(args),
        out_specs=[hbm] * 6 + [pl.BlockSpec(memory_space=pltpu.VMEM)],
        scratch_shapes=[
            bf(LAYERS, QKV, D), bf(LAYERS, W, D), bf(LAYERS, D, D), bf(LAYERS, D, D), bf(LAYERS, SMALL, D),
            bf(LAYERS, SEQ, KB), bf(LAYERS + 1, ROWS, D), bf(LAYERS, ROWS, D), bf(LAYERS, ROWS, W), bf(LAYERS, ROWS, W),
            f32(LAYERS, NJ * 8, KB), f32(PAIRS, KB, WIDE), f32(KB, W), f32(KB, W),
            bf(ROWS, D), f32(ROWS, D), f32(SEQ, KB), f32(NJ, CH, KB), bf(ROWS, D), bf(ROWS, D), bf(ROWS, D), f32(KB, W),
            *grads, *grads, *grads, f32(LAYERS, SMALL, D), f32(LAYERS, SMALL, D),
            *[slots] * 4, *[slot_sem] * 5,
            chunk_sem, dma((len(args) - 2,)), dma((2, len(args) - 2)), dma((LAYERS, len(args) - 2)), dma((len(args) - 2,)),
            chunk_sem, chunk_sem, chunk_sem, stage_sem,
            chunk_sem, chunk_sem, chunk_sem, chunk_sem, stage_sem, *[pair_sem] * 5, stage_sem, stage_sem,
        ],
        compiler_params=pltpu.CompilerParams(collective_id=0, has_side_effects=True, vmem_limit_bytes=67043328),
        name="decoder_layers",
    )(*args)


def solution(mesh):
    def program(x_in, dy_out, w_qkv, b_qkv, w_out, b_out, ln_par, w_fc1, b_fc1, w_fc2, b_fc2):
        layers, parts, _, heads, width = w_qkv.shape
        wq = w_qkv.transpose(0, 1, 3, 4, 2).reshape(QKV, D)
        bq = jnp.pad(b_qkv.reshape(1, QKV), ((0, 0), (0, D - QKV)))
        ws = jnp.concatenate([ln_par.reshape(4, D), b_out, b_fc2, b_fc1, bq, jnp.zeros((8, D), BF)], axis=0)
        h_out, g_in, d_w1, d_w2, d_q, d_o, sm = run_layers(
            x_in.reshape(2, SEQ, D), dy_out.reshape(2, SEQ, D), wq, w_out.reshape(W, D), w_fc1.reshape(D, D), w_fc2.reshape(D, D), ws)
        acts = (layers, *x_in.shape)
        return (h_out.reshape(acts), g_in.reshape(acts),
                d_q.reshape(layers, parts, heads, width, D).transpose(0, 1, 4, 2, 3), sm[BQKV, :QKV].reshape(b_qkv.shape),
                d_o.reshape(w_out.shape), row(sm, BOUT), sm[GAIN1:BOUT].reshape(ln_par.shape),
                d_w1.reshape(w_fc1.shape), row(sm, BFC1), d_w2.reshape(w_fc2.shape), row(sm, BFC2))

    act_spec = P(NO, "dp", NO, NO)
    arg_specs = (act_spec, act_spec,
                 P("pp", NO, NO, "tp", NO), P("pp", NO, "tp", NO), P("pp", "tp", NO, NO),
                 P("pp", NO), P("pp", NO, NO), P("pp", NO, "tp"), P("pp", "tp"),
                 P("pp", "tp", NO), P("pp", NO))
    stage_spec = P("pp", NO, "dp", NO, NO)
    grad_axes = ("dp", "pp")
    result_specs = (stage_spec, stage_spec,
                    P(grad_axes, NO, NO, "tp", NO), P(grad_axes, NO, "tp", NO), P(grad_axes, "tp", NO, NO),
                    P(grad_axes, NO), P(grad_axes, NO, NO), P(grad_axes, NO, "tp"), P(grad_axes, "tp"),
                    P(grad_axes, "tp", NO), P(grad_axes, NO))
    return jax.shard_map(program, mesh=mesh, in_specs=arg_specs, out_specs=result_specs, check_vma=False)
```

time: 3240 us -> 457 us (0.14)
  waiting for transfers between devices: 1930 us -> 0 us
  matrix products: 872 us -> 0 us
  Pallas kernels: 0 us -> 435 us
  other arithmetic: 300 us -> 0 us
  local copies, waits for them, and re-layouts: 90.9 us -> 17.2 us
    psum x20 -> x0, waiting for transfers between devices: 1540 us -> none  [the longest x5 430 us: layer_forward(): attn_sum = lax.psum(attn_part, 'tp')]
    dot_general x80 -> x0, matrix products: 671 us -> none  [the longest x15 228 us: causal_attention(): jnp.einsum('bhqk,bkhe->bqhe', attn_probs, v_heads, preferred_element_type...]
    pallas_call x0 -> x1, Pallas kernels: none -> 435 us  [run_layers(): pl.pallas_call(decoder_kernel, out_shape=[acts, acts, *(jax.ShapeDtypeStr...]
    all_gather x10 -> x0, waiting for transfers between devices: 363 us -> none  [pass_on(): return lax.all_gather(moved_part, 'tp', axis=1, tiled=True)]
    sub x10 -> x0, matrix products: 193 us -> none  [causal_attention(): attn_probs = jax.nn.softmax(scores, axis=-1).astype(jnp.bfloat16)]
    reduce_sum x60 -> x0, other arithmetic: 146 us -> none  [the longest x20 54.5 us: layer_norm(): row_var = jnp.mean(centered * centered, axis=-1, keepdims=True)]
    dynamic_update_slice x25 -> x0, other arithmetic: 96.9 us -> none  [the longest x5 24 us: bwd_step(): grad_buf = lax.dynamic_update_index_in_dim(grad_buf, grad_in, write_idx, 0)]
    ge x10 -> x0, other arithmetic: 41.4 us -> none  [causal_attention(): scores = jnp.where(row_pos >= col_pos, scores, -1e+30)]
  transfers between devices with their start and end apart: 40 -> 0, of which waited for: 40 -> 0; matrix products, arithmetic and copies ran while one was open for 10% -> 0% of each run, Pallas kernels for 0% -> 0%
where the time goes in v2:
time: 457 us; the launch traced here: 453 us
  Pallas kernels  435 us (95%)
  local copies, waits for them, and re-layouts  17.2 us (4%)
    pallas_call x1, Pallas kernels, run_layers(): pl.pallas_call(decoder_kernel, out_shape=[acts, acts, *(jax.ShapeDtypeStr...  435 us
    unnamed x16, local copies, waits for them, and re-layouts  10.3 us

profile of v2, /device:TPU:0, one launch (start us, length us, event | category | flops | bytes accessed | tf_op | source)
XLA Modules:
  0.0 453.2 jit_solution(12003003438549616444)
XLA Ops:
  0.6 0.8 reshape.74
  1.4 2.0 concatenate.3.ws
  3.4 435.4 %decoder_layers.1 = (bf16[2,2048,512]{2,1,0:T(8,128)(2,1)}, bf16[2,2048,512]{2,1,0:T(8,128)(2,1)}, f32[512,512]{1,0:T(8,128)}, f32[512,512]{1,0:T(8,128)}, f32[3...) custom-call(bf16[2,2048,512]{2,1,0:T(8,128)(2,1)} %bitcast.23, bf16[2,2048,512]{2,1,0:T(8,128)(2,1)} %bitcast.24, ...), custom_call_target="tpu_custom_call" | custom-call | tf_op jit(solution)/shard_map/decoder_layers/pallas_call | solution.py:670
  438.8 1.4 fusion
  440.2 1.3 slice_bitcast_fusion
  441.5 0.7 slice_reduce_fusion
  442.3 0.7 reshape_squeeze.3
  442.9 0.0 copy-start
  442.9 4.6 %copy.30 = bf16[1,2,1,2048,512]{4,3,2,1,0:T(8,128)(2,1)} copy(bf16[1,2,1,2048,512]{4,3,2,1,0:T(8,128)(2,1)} %bitcast.26) | data formatting | bytes 8388608
  447.6 0.0 copy-done
  447.6 0.0 copy-start.3
  447.6 0.0 copy-start.4
  447.6 0.0 copy-start.2
  447.6 2.1 copy.31
  449.7 0.0 copy-done.3
  449.7 0.0 copy-start.1
  449.7 0.9 copy.32
  450.6 0.0 copy-done.4
  450.6 0.7 copy.33
  451.3 0.0 copy-done.2
  451.3 1.0 copy.34
  452.3 0.0 copy-done.1
  452.3 1.0 copy.35
  (2 shorter events, 0.0 us)
Async XLA Ops:
  442.9 4.6 %copy-start = (bf16[2,2048,512]{2,1,0:T(8,128)(2,1)S(1)}, bf16[2,2048,512]{2,1,0:T(8,128)(2,1)}, u32[]{:S(2)}) copy-start(bf16[2,2048,512]{2,1,0:T(8,128)(2,1)} %get-tuple-element.19) | copy-start | bytes 12582916
  447.6 2.1 copy-start.3
  447.6 3.0 copy-start.4
  447.6 3.7 copy-start.2
  449.7 2.6 copy-start.1

commit v3 on v2

--- a/solution.py
+++ b/solution.py
@@ -123,35 +123,27 @@
         def greet(dev):
             pl.semaphore_signal(bar, inc=1, device_id=dev, device_id_type=MESH)
 
-        for k in range(1, LAYERS):
-            greet({"pp": (self.p + k) % LAYERS})
-
-        @when(self.z > 0)
-        def _():
-            greet({"tp": self.z - 1})
-
-        @when(self.z < 3)
-        def _():
-            greet({"tp": self.z + 1})
-
-        @when(self.hub)
-        def _():
-            pl.semaphore_wait(bar, 5)
-
-        @when(self.leaf)
-        def _():
-            pl.semaphore_wait(bar, 4)
+        for k in range(1, 4):
+            greet({"pp": (self.p + k) % 4})
+            greet({"tp": (self.z + k) % 4})
+
+        pl.semaphore_wait(bar, 6)
+
+
+def is_gather(e):
+    return (e < FWD) & (e % SLOTS < NJ)
 
 
 class LineSum:
-    def __init__(self, at, part, lbuf, hbuf, fin, s1, s2, r_l, r_h, r_f):
+    def __init__(self, at, gather, part, lbuf, hbuf, fin, s1, s2, r_l, r_h, r_f):
+        self.gather = gather
         self.at, self.part, self.lbuf, self.hbuf, self.fin = at, part, lbuf, hbuf, fin
         self.s1, self.s2, self.r_l, self.r_h, self.r_f = s1, s2, r_l, r_h, r_f
 
     def emit(self, e, value):
         slot = e % SLOTS
 
-        @when(e >= SLOTS)
+        @when((e >= SLOTS) & jnp.logical_not(is_gather(e - SLOTS)))
         def _():
             wait_dma(self.part.at[slot], self.s1.at[slot])
 
@@ -161,13 +153,20 @@
         def _():
             send(self.part.at[slot], self.lbuf.at[slot], self.s1.at[slot], self.r_l.at[slot], self.at.my_hub)
 
-        self.serve_first(e - 2)
-        self.serve_second(e - 4)
+        self.serve(e)
+
+    def serve(self, e):
+        for back, mine, other in ((2, self.serve_first, self.gather.serve_first), (4, self.serve_second, self.gather.serve_second)):
+            mine(e - back)
+
+            @when(self.at.hub & (e >= back) & is_gather(e - back))
+            def _():
+                other((e - back + SLOTS) % SLOTS)
 
     def serve_first(self, e):
         slot = (e + SLOTS) % SLOTS
 
-        @when(self.at.hub & (e >= 0))
+        @when(self.at.hub & (e >= 0) & jnp.logical_not(is_gather(e)))
         def _():
             wait_dma(self.lbuf.at[slot], self.r_l.at[slot])
             self.part[slot] = (self.part[slot].astype(F32) + self.lbuf[slot].astype(F32)).astype(BF)
@@ -176,11 +175,11 @@
     def serve_second(self, e):
         slot = (e + SLOTS) % SLOTS
 
-        @when(self.at.hub & (e >= 0))
+        @when(self.at.hub & (e >= 0) & jnp.logical_not(is_gather(e)))
         def _():
             wait_dma(self.hbuf.at[slot], self.r_h.at[slot])
 
-            @when(e >= SLOTS)
+            @when((e >= SLOTS) & jnp.logical_not(is_gather(e - SLOTS)))
             def _():
                 wait_dma(self.fin.at[slot], self.s2.at[slot])
 
@@ -193,12 +192,6 @@
             wait_dma(self.fin.at[slot], self.r_f.at[slot])
 
         return self.fin[slot].astype(F32)
-
-    def drain(self, total):
-        self.serve_first(total - 2)
-        self.serve_first(total - 1)
-        for k in range(4):
-            self.serve_second(total - 4 + k)
 
     def close(self):
         def body(slot):
@@ -209,6 +202,53 @@
                 wait_dma(self.fin.at[slot], self.s2.at[slot])
 
         loop(SLOTS, body)
+
+
+class LineGather:
+    def __init__(self, at, buf, s_a, s_b, s_c, r_a, r_b):
+        self.at, self.buf, self.s_a, self.s_b, self.s_c, self.r_a, self.r_b = at, buf, s_a, s_b, s_c, r_a, r_b
+        side = at.z // 2
+        self.mine, self.theirs = pl.ds(2 * side, 2), pl.ds(2 - 2 * side, 2)
+
+    def sent(self, j):
+        own, pair = self.buf.at[j, 0], self.buf.at[j, pl.ds(0, 2)]
+        wait_dma(own, self.s_a.at[j])
+
+        @when(self.at.hub)
+        def _():
+            wait_dma(pair, self.s_b.at[j])
+            wait_dma(pair, self.s_c.at[j])
+
+    def emit(self, j, value):
+        at = self.at
+        self.buf[j, at.z] = value
+        own = self.buf.at[j, at.z]
+
+        @when(at.leaf)
+        def _():
+            send(own, own, self.s_a.at[j], self.r_a.at[j], at.my_hub)
+
+        @when(at.hub)
+        def _():
+            send(own, own, self.s_a.at[j], self.r_a.at[j], at.my_leaf)
+
+    def serve_first(self, j):
+        wait_dma(self.buf.at[j, 0], self.r_a.at[j])
+        pair = self.buf.at[j, self.mine]
+        send(pair, pair, self.s_b.at[j], self.r_b.at[j], self.at.other_hub)
+
+    def serve_second(self, j):
+        pair = self.buf.at[j, self.theirs]
+        wait_dma(pair, self.r_b.at[j])
+        send(pair, pair, self.s_c.at[j], self.r_b.at[j], self.at.my_leaf)
+
+    def get(self, j):
+        @when(self.at.leaf)
+        def _():
+            wait_dma(self.buf.at[j, 0], self.r_a.at[j])
+            wait_dma(self.buf.at[j, self.theirs], self.r_b.at[j])
+
+        return jnp.concatenate([self.buf[j, k] for k in range(4)], axis=1)
 
 
 def head_stack(v):
@@ -231,37 +271,53 @@
 
 def decoder_kernel(x_in, dy, wq, wo, w1, w2, ws,
                    h_out, g_in, o_w1, o_w2, o_q, o_o, o_sm,
-                   wqv, wov, w1v, w2v, wsv, kv, xs, xm, qs, os_, lses, scores, acc, lsum,
-                   gcur, gm, dkv, pk, buf_a, buf_b, buf_c, dq_acc,
+                   wsv, wqv, w1v, w2v, wov, kv, xs, xm, qs, os_, lses, scores, acc, lsum,
+                   gcur, gm, dkv, pk, h1s, dqkvs, gms, h2p, dprep, ap, dq_acc, xm_far, g_far,
                    a_w1, a_w2, a_q, a_o, d_w1, d_w2, d_q, d_o, y_w1, y_w2, y_q, y_o, sm, rsm,
-                   part, lbuf, hbuf, fin, s1, s2, r_l, r_h, r_f,
-                   x_sem, w_local, w_send, w_recv, w_fwd, kv_s, kv_r, ho_s, ho_r,
-                   dy_sem, dk_s, dk_r, gi_s, gi_r, d_s, d_r, y_s, y_r, o_sem, sm_s, sm_r):
+                   part, lbuf, hbuf, fin, s1, s2, r_l, r_h, r_f, og, gs_a, gs_b, gs_c, gr_a, gr_b,
+                   x_sem, wz_s, wz_r, w_local, w_send, w_recv, w_fwd, kv_s, kv_r, ho_s, ho_r,
+                   dy_sem, dk_s, dk_r, gi_s, gi_r, d_s, d_r, y_s, y_r, o_sem, sm_s, sm_r, xf_s, xf_r, gf_s, gf_r):
     at = Place()
-    line = LineSum(at, part, lbuf, hbuf, fin, s1, s2, r_l, r_h, r_f)
+    gather = LineGather(at, og, gs_a, gs_b, gs_c, gr_a, gr_b)
+    line = LineSum(at, gather, part, lbuf, hbuf, fin, s1, s2, r_l, r_h, r_f)
     y, c, p = at.y, at.c, at.p
-    w_hbm = (ws, wq, wo, w1, w2)
-    w_vm = (wsv, wqv, wov, w1v, w2v)
-    every = range(len(w_hbm))
-    group_a, group_m = every[:3], every[3:]
+    w_hbm = (ws, wq, w1, w2)
+    w_vm = (wsv, wqv, w1v, w2v, wov)
+    every = range(len(w_vm))
+    at_once, group_a, group_m, out_proj = every[:4], every[:2], every[2:], every[4:]
+    wo_mine = wov.at[p, chunk(at.z)]
 
     for j in range(NJ):
         local(x_in.at[y, at.rows_of(j)], xs.at[0, chunk(j)], x_sem.at[j])
-    for k in every:
+    for k in at_once:
         local(w_hbm[k], w_vm[k].at[p], w_local.at[k])
+    local(wo, wo_mine, w_local.at[4])
 
     at.enter()
 
-    def send_across():
-        for k in every:
-            send(w_hbm[k], w_vm[k].at[p], w_send.at[1, k], w_recv.at[p, k], at.across)
+    def spread(group, way, dev):
+        for k in group:
+            src = w_hbm[k] if k < 4 else wov.at[p]
+            send(src, w_vm[k].at[p], w_send.at[way, k], w_recv.at[p, k], dev)
 
     @when(c == 0)
     def _():
-        send_across()
-
-    for k in every:
-        send(w_hbm[k], w_vm[k].at[p], w_send.at[0, k], w_recv.at[p, k], at.mate)
+        spread(at_once, 1, at.across)
+
+    spread(at_once, 0, at.mate)
+    for k in range(1, 4):
+        send(wo, wo_mine, wz_s.at[k], wz_r.at[at.z], {"tp": (at.z + k) % 4})
+
+    def spread_out_proj():
+        wait_dma(wo_mine, w_local.at[4])
+        for k in range(1, 4):
+            wait_dma(wo_mine, wz_r.at[(at.z + k) % 4])
+            wait_dma(wo_mine, wz_s.at[k])
+        spread(out_proj, 0, at.mate)
+
+        @when(c == 0)
+        def _():
+            spread(out_proj, 1, at.across)
     for j in range(NJ):
         local(dy.at[y, at.rows_of(j)], gcur.at[chunk(j)], dy_sem.at[j])
 
@@ -269,7 +325,8 @@
         @when(p == s)
         def _():
             for k in group:
-                wait_dma(w_vm[k].at[p], w_local.at[k])
+                if k < 4:
+                    wait_dma(w_vm[k].at[p], w_local.at[k])
 
         @when(p != s)
         def _():
@@ -355,13 +412,20 @@
         o = head_merge(acc[...] / den).astype(BF)
         os_[l, rows, :] = o
         lses[l, blk(j, 8), :] = jnp.broadcast_to(top + jnp.log(den), (KB, W)).T[:8]
-        line.emit(SLOTS * l + j, nn(o, wov[l]))
+        gather.emit(j, o)
+        line.serve(SLOTS * l + j)
 
     def mlp_op(l, j):
         rows = chunk(j)
         small = wsv[l].astype(F32)
-        mid = (xs[l, rows, :].astype(F32) + line.get(j) + row(small, BOUT)).astype(BF)
+        gather.sent(j)
+        mid = (xs[l, rows, :].astype(F32) + nn(gather.get(j), wov[l]) + row(small, BOUT)).astype(BF)
         xm[l, rows, :] = mid
+
+        @when((l == 0) & (y == 1))
+        def _():
+            send(xm.at[0, rows], xm_far.at[rows], xf_s.at[j], xf_r.at[j], at.across)
+
         xhat, _ = ln_stats(mid.astype(F32))
         h2 = (xhat * row(small, GAIN2) + row(small, SHIFT2)).astype(BF)
         u = nn(h2, w1v[l]) + row(small, BFC1)
@@ -375,9 +439,13 @@
             with jax.named_scope("attn"):
                 attn_op(l, jj, 1)
 
-            @when((l == 0) & (jj == 0) & (c == 1))
-            def _():
-                send_across()
+            @when((l == 0) & (jj == 1))
+            def _():
+                spread_out_proj()
+
+            @when((l == 0) & (jj == PAIRS - 2) & (c == 1))
+            def _():
+                spread(every, 1, at.across)
 
         loop(PAIRS, attn_pair)
 
@@ -460,7 +528,14 @@
             wait_dma(gcur.at[rows], gi_s.at[j])
 
         gcur[rows, :] = out
-        send_home(l, gcur.at[rows], g_in.at[y, at.rows_of(j)], gi_s.at[j], gi_r)
+
+        @when((l == 1) & (y == 1))
+        def _():
+            send(gcur.at[rows], g_far.at[rows], gi_s.at[j], gf_r.at[j], at.across)
+
+        @when((l != 1) | (y == 0))
+        def _():
+            send_home(l, gcur.at[rows], g_in.at[y, at.rows_of(j)], gi_s.at[j], gi_r)
 
     def mlp_back(l, i):
         j = NJ - 1 - i
@@ -475,30 +550,88 @@
         def _():
             finish_layer(l + 1, j)
 
+        g = gcur[rows, :]
+        dpre = mlp_grads(l, j, xm[l, rows, :], g)
+        add_small(l, BFC2, colsum(g.astype(F32)))
+        add_small(l, BFC1, colsum(dpre))
+        line.emit(FWD + SLOTS * (LAYERS - 1 - l) + i, nt(dpre.astype(BF), w1v[l]))
+
+        @when((l > 0) | (y == 0))
+        def _():
+            mlp_weight_grads(i, gcur)
+
+    def mlp_grads(l, j, mid, g):
         small = wsv[l].astype(F32)
-        g = gcur[rows, :]
-        xhat, _ = ln_stats(xm[l, rows, :].astype(F32))
+        xhat, _ = ln_stats(mid.astype(F32))
         h2 = (xhat * row(small, GAIN2) + row(small, SHIFT2)).astype(BF)
         u = nn(h2, w1v[l]) + row(small, BFC1)
         t = jnp.tanh(GELU_C * (u + GELU_A * u * u * u))
         half = 0.5 * (1.0 + t)
         slope = half + 0.5 * u * (1.0 - t * t) * (GELU_C * (1.0 + 3.0 * GELU_A * u * u))
         dpre = nt(g, w2v[l]) * slope
-        add_small(l, BFC2, colsum(g.astype(F32)))
-        add_small(l, BFC1, colsum(dpre))
-        dpre = dpre.astype(BF)
-        buf_a[rows, :] = h2
-        buf_b[rows, :] = dpre
-        buf_c[rows, :] = (u * half).astype(BF)
-        line.emit(FWD + SLOTS * (LAYERS - 1 - l) + i, nt(dpre, w1v[l]))
-
-    def mlp_weight_grads():
-        def body(t):
-            cols = blk(t, KB)
-            a_w1[:, cols] = tn(buf_a[...], buf_b[:, cols])
-            a_w2[:, cols] = tn(buf_c[...], gcur[:, cols])
-
-        loop(D // KB, body)
+        spot = chunk(j % 2)
+        h2p[spot, :] = h2
+        dprep[spot, :] = dpre.astype(BF)
+        ap[spot, :] = (u * half).astype(BF)
+        return dpre
+
+    def mlp_weight_grads(i, g_ref):
+        grads = blk((NJ - 1 - i) // 2, KB)
+
+        @when(i == 1)
+        def _():
+            a_w1[...] = tn(h2p[...], dprep[...])
+            a_w2[...] = tn(ap[...], g_ref[grads, :])
+
+        @when((i > 1) & (i % 2 == 1))
+        def _():
+            a_w1[...] += tn(h2p[...], dprep[...])
+            a_w2[...] += tn(ap[...], g_ref[grads, :])
+
+    def far_mlp_weight_grads():
+        def body(i):
+            j = NJ - 1 - i
+            rows = chunk(j)
+            wait_dma(xm_far.at[rows], xf_r.at[j])
+            wait_dma(g_far.at[rows], gf_r.at[j])
+            dst = g_in.at[1, at.rows_of(j)]
+
+            @when(c == 1)
+            def _():
+                local(g_far.at[rows], dst, gi_r.at[3])
+
+            @when(c == 0)
+            def _():
+                send(g_far.at[rows], dst, gf_s.at[j], gi_r.at[2], at.mate)
+
+            mlp_grads(0, j, xm_far[rows, :], g_far[rows, :])
+
+            @when(i % 2 == 1)
+            def _():
+                a_w1[...] += tn(h2p[...], dprep[...])
+                a_w2[...] += tn(ap[...], g_far[blk(j // 2, KB), :])
+
+        loop(NJ, body)
+
+        @when(c == 1)
+        def _():
+            for k, (own, mid, _, _) in enumerate(groups[0]):
+                send(own, mid, d_s.at[0, k], d_r.at[0, k], at.mate)
+            for k, (own, _, _, _) in enumerate(groups[0]):
+                wait_dma(own, d_s.at[0, k])
+
+        @when(c == 0)
+        def _():
+            for k, (own, mid, _, out) in enumerate(groups[0]):
+                wait_dma(mid, d_r.at[0, k])
+                add_into(mid, own)
+                local(mid, out, o_sem.at[0, k])
+            loop(NJ, lambda j: wait_dma(g_far.at[chunk(j)], gf_s.at[j]))
+
+    def attn_weight_grads(l):
+        a_q[...] = tn(dqkvs[...], h1s[...])
+        a_o[...] = tn(os_[l], gms[...])
+        grad_to_mate(l, 1)
 
     def attn_back(l, jj, odd):
         j = 2 * jj + odd
@@ -512,8 +645,8 @@
         gm[rows, :] = wide
         add_small(l, BOUT, colsum(wide))
         gmid = wide.astype(BF)
-        buf_c[rows, :] = gmid
-        do = nt(gmid, wov[l]).astype(BF)
+        gms[rows, :] = gmid
+        do = nt(gmid, wov[l, chunk(at.z), :]).astype(BF)
         delta = jnp.sum(head_stack(do.astype(F32) * os_[l, rows, :].astype(F32)), axis=-1, keepdims=True)
         delta = jnp.broadcast_to(delta, (KB, W)).T[0:1]
         lse = lses[l, blk(j, 8), :][0:1]
@@ -538,18 +671,18 @@
         loop(jj, lambda kb: block(blk(kb, WIDE), WIDE, False))
         width = KB * (1 + odd)
         block(pl.ds(pl.multiple_of(jj * WIDE, WIDE), width), width, True)
-        buf_b[rows, 0:W] = (head_merge(dq_acc[...]) * 0.125).astype(BF)
+        dqkvs[rows, 0:W] = (head_merge(dq_acc[...]) * 0.125).astype(BF)
         send(dkv.at[at.mate_rows(j)], pk.at[j], dk_s.at[j], dk_r.at[j], at.mate)
 
     def qkv_back(l, j):
         rows = chunk(j)
         small = wsv[l].astype(F32)
         xhat, _ = ln_stats(xs[l, rows, :].astype(F32))
-        buf_a[rows, :] = (xhat * row(small, GAIN1) + row(small, SHIFT1)).astype(BF)
+        h1s[rows, :] = (xhat * row(small, GAIN1) + row(small, SHIFT1)).astype(BF)
         wait_dma(pk.at[j], dk_r.at[j])
         dkv_own = (dkv[at.rows_of(j), :] + pk[j]).astype(BF)
-        buf_b[rows, W:QKV] = dkv_own
-        dqkv = jnp.concatenate([buf_b[rows, 0:W], dkv_own], axis=1)
+        dqkvs[rows, W:] = dkv_own
+        dqkv = jnp.concatenate([dqkvs[rows, 0:W], dkv_own], axis=1)
         sm[l, BQKV:BQKV + 1, 0:QKV] += colsum(dqkv.astype(F32))
         line.emit(FWD + SLOTS * (LAYERS - l) - 1 - j, nn(dqkv, wqv[l]))
 
@@ -557,6 +690,10 @@
         l = LAYERS - 1 - n
 
         def first_half(i):
+            @when((i == 0) & (l < LAYERS - 1))
+            def _():
+                attn_weight_grads(l + 1)
+
             @when(i == 2)
             def _():
                 @when(l < LAYERS - 2)
@@ -571,9 +708,10 @@
                 mlp_back(l, i)
 
         loop(NJ, first_half)
-        with jax.named_scope("dw1"):
-            mlp_weight_grads()
-        grad_to_mate(l, 0)
+
+        @when(l > 0)
+        def _():
+            grad_to_mate(l, 0)
 
         def clear(i):
             dkv[blk(i, 64), :] = jnp.zeros((64, KB), F32)
@@ -583,16 +721,16 @@
         def second_half(ii):
             jj = PAIRS - 1 - ii
 
-            @when(ii == 1)
-            def _():
-                @when(l < LAYERS - 1)
-                def _():
-                    grad_home(l + 1, 0)
-
-                grad_across(l, 0)
+            @when((ii == 1) & (l < LAYERS - 1))
+            def _():
+                grad_home(l + 1, 0)
 
             with jax.named_scope("B2"):
                 attn_back(l, jj, 1)
+
+            @when((ii == 0) & (l > 0))
+            def _():
+                grad_across(l, 0)
 
             @when(ii > 0)
             def _():
@@ -606,22 +744,39 @@
 
         loop(PAIRS, second_half)
         qkv_back(l, 0)
-        with jax.named_scope("dw2"):
-            a_q[...] = tn(buf_b[:, 0:QKV], buf_a[...])
-            a_o[...] = tn(os_[l], buf_c[...])
-        grad_to_mate(l, 1)
         loop(NJ, lambda j: wait_dma(pk.at[j], dk_s.at[j]))
 
     loop(LAYERS, backward_layer)
-    line.drain(FWD + LAYERS * SLOTS)
+    attn_weight_grads(0)
     grad_across(0, 1)
-    loop(NJ, lambda i: finish_layer(0, NJ - 1 - i))
+    last = FWD + LAYERS * SLOTS - 1
+
+    def finish_last(i):
+        @when((i == 1) | (i == 2))
+        def _():
+            line.serve_first(last - 2 + i)
+
+        @when(i > 3)
+        def _():
+            line.serve_second(last - NJ + 1 + i)
+
+        finish_layer(0, NJ - 1 - i)
+
+    loop(NJ, finish_last)
     for s in range(LAYERS):
         @when(p != s)
         def _():
             send(sm.at[s], rsm.at[p], sm_s.at[s], sm_r.at[p], {"pp": s})
+
+    @when(y == 0)
+    def _():
+        far_mlp_weight_grads()
+
+    @when(y == 1)
+    def _():
+        loop(NJ, lambda j: wait_dma(xm.at[0, chunk(j)], xf_s.at[j]))
+
     grad_home(1, 1)
-    grad_home(0, 0)
     grad_home(0, 1)
     for s in range(LAYERS):
         @when(p != s)
@@ -673,15 +828,15 @@
         in_specs=[hbm] * len(args),
         out_specs=[hbm] * 6 + [pl.BlockSpec(memory_space=pltpu.VMEM)],
         scratch_shapes=[
-            bf(LAYERS, QKV, D), bf(LAYERS, W, D), bf(LAYERS, D, D), bf(LAYERS, D, D), bf(LAYERS, SMALL, D),
+            bf(LAYERS, SMALL, D), bf(LAYERS, QKV, D), *[bf(LAYERS, D, D)] * 3,
             bf(LAYERS, SEQ, KB), bf(LAYERS + 1, ROWS, D), bf(LAYERS, ROWS, D), bf(LAYERS, ROWS, W), bf(LAYERS, ROWS, W),
             f32(LAYERS, NJ * 8, KB), f32(PAIRS, KB, WIDE), f32(KB, W), f32(KB, W),
-            bf(ROWS, D), f32(ROWS, D), f32(SEQ, KB), f32(NJ, CH, KB), bf(ROWS, D), bf(ROWS, D), bf(ROWS, D), f32(KB, W),
+            bf(ROWS, D), f32(ROWS, D), f32(SEQ, KB), f32(NJ, CH, KB), bf(ROWS, D), bf(ROWS, QKV), bf(ROWS, D), *[bf(KB, D)] * 3, f32(KB, W), bf(ROWS, D), bf(ROWS, D),
             *grads, *grads, *grads, f32(LAYERS, SMALL, D), f32(LAYERS, SMALL, D),
-            *[slots] * 4, *[slot_sem] * 5,
-            chunk_sem, dma((len(args) - 2,)), dma((2, len(args) - 2)), dma((LAYERS, len(args) - 2)), dma((len(args) - 2,)),
+            *[slots] * 4, *[slot_sem] * 5, bf(NJ, 4, CH, W), *[chunk_sem] * 5,
+            chunk_sem, stage_sem, stage_sem, dma((len(args) - 2,)), dma((2, len(args) - 2)), dma((LAYERS, len(args) - 2)), dma((len(args) - 2,)),
             chunk_sem, chunk_sem, chunk_sem, stage_sem,
-            chunk_sem, chunk_sem, chunk_sem, chunk_sem, stage_sem, *[pair_sem] * 5, stage_sem, stage_sem,
+            chunk_sem, chunk_sem, chunk_sem, chunk_sem, stage_sem, *[pair_sem] * 5, stage_sem, stage_sem, *[chunk_sem] * 4,
         ],
         compiler_params=pltpu.CompilerParams(collective_id=0, has_side_effects=True, vmem_limit_bytes=67043328),
         name="decoder_layers",

time: 457 us -> 439 us (0.961)
  Pallas kernels: 435 us -> 420 us
    pallas_call x1, Pallas kernels: 435 us -> 420 us  [run_layers(): pl.pallas_call(decoder_kernel, out_shape=[acts, acts, *(jax.ShapeDtypeStr...]
where the time goes in v3:
time: 439 us; the launch traced here: 438 us
  Pallas kernels  420 us (96%)
  local copies, waits for them, and re-layouts  17.2 us (4%)
    pallas_call x1, Pallas kernels, run_layers(): pl.pallas_call(decoder_kernel, out_shape=[acts, acts, *(jax.ShapeDtypeStr...  420 us
    unnamed x16, local copies, waits for them, and re-layouts  10.3 us

profile of v3, /device:TPU:0, one launch (start us, length us, event | category | flops | bytes accessed | tf_op | source)
XLA Modules:
  0.0 438.2 jit_solution(18260461389028525561)
XLA Ops:
  0.6 0.8 reshape.74
  1.4 2.0 concatenate.3.ws
  3.4 420.4 %decoder_layers.1 = (bf16[2,2048,512]{2,1,0:T(8,128)(2,1)}, bf16[2,2048,512]{2,1,0:T(8,128)(2,1)}, f32[512,512]{1,0:T(8,128)}, f32[512,512]{1,0:T(8,128)}, f32[3...) custom-call(bf16[2,2048,512]{2,1,0:T(8,128)(2,1)} %bitcast.23, bf16[2,2048,512]{2,1,0:T(8,128)(2,1)} %bitcast.24, ...), custom_call_target="tpu_custom_call" | custom-call | tf_op jit(solution)/shard_map/decoder_layers/pallas_call | solution.py:825
  423.7 1.4 fusion
  425.2 1.3 slice_bitcast_fusion
  426.5 0.7 slice_reduce_fusion
  427.2 0.7 reshape_squeeze.3
  427.9 0.0 copy-start
  427.9 4.6 %copy.30 = bf16[1,2,1,2048,512]{4,3,2,1,0:T(8,128)(2,1)} copy(bf16[1,2,1,2048,512]{4,3,2,1,0:T(8,128)(2,1)} %bitcast.26) | data formatting | bytes 8388608
  432.5 0.0 copy-done
  432.5 0.0 copy-start.3
  432.5 0.0 copy-start.4
  432.5 0.0 copy-start.2
  432.5 2.1 copy.31
  434.7 0.0 copy-done.3
  434.7 0.0 copy-start.1
  434.7 0.9 copy.32
  435.5 0.0 copy-done.4
  435.5 0.7 copy.33
  436.2 0.0 copy-done.2
  436.3 1.0 copy.34
  437.2 0.0 copy-done.1
  437.2 1.0 copy.35
  (2 shorter events, 0.0 us)
Async XLA Ops:
  427.9 4.6 %copy-start = (bf16[2,2048,512]{2,1,0:T(8,128)(2,1)S(1)}, bf16[2,2048,512]{2,1,0:T(8,128)(2,1)}, u32[]{:S(2)}) copy-start(bf16[2,2048,512]{2,1,0:T(8,128)(2,1)} %get-tuple-element.19) | copy-start | bytes 12582916
  432.5 2.1 copy-start.3
  432.5 3.0 copy-start.4
  432.5 3.7 copy-start.2
  434.7 2.6 copy-start.1

commit v4 on v3

--- a/solution.py
+++ b/solution.py
@@ -74,6 +74,10 @@
     return blk(j, CH)
 
 
+def pair(jj):
+    return blk(jj, KB)
+
+
 def loop(n, body):
     def step(i, carry):
         body(i)
@@ -211,13 +215,13 @@
         self.mine, self.theirs = pl.ds(2 * side, 2), pl.ds(2 - 2 * side, 2)
 
     def sent(self, j):
-        own, pair = self.buf.at[j, 0], self.buf.at[j, pl.ds(0, 2)]
+        own, two = self.buf.at[j, 0], self.buf.at[j, pl.ds(0, 2)]
         wait_dma(own, self.s_a.at[j])
 
         @when(self.at.hub)
         def _():
-            wait_dma(pair, self.s_b.at[j])
-            wait_dma(pair, self.s_c.at[j])
+            wait_dma(two, self.s_b.at[j])
+            wait_dma(two, self.s_c.at[j])
 
     def emit(self, j, value):
         at = self.at
@@ -234,13 +238,13 @@
 
     def serve_first(self, j):
         wait_dma(self.buf.at[j, 0], self.r_a.at[j])
-        pair = self.buf.at[j, self.mine]
-        send(pair, pair, self.s_b.at[j], self.r_b.at[j], self.at.other_hub)
+        two = self.buf.at[j, self.mine]
+        send(two, two, self.s_b.at[j], self.r_b.at[j], self.at.other_hub)
 
     def serve_second(self, j):
-        pair = self.buf.at[j, self.theirs]
-        wait_dma(pair, self.r_b.at[j])
-        send(pair, pair, self.s_c.at[j], self.r_b.at[j], self.at.my_leaf)
+        two = self.buf.at[j, self.theirs]
+        wait_dma(two, self.r_b.at[j])
+        send(two, two, self.s_c.at[j], self.r_b.at[j], self.at.my_leaf)
 
     def get(self, j):
         @when(self.at.leaf)
@@ -258,8 +262,13 @@
 
 
 def head_merge(v):
-    first = lax.broadcasted_iota(jnp.int32, (CH, W), 1) < W // 2
-    return jnp.where(first, v[:CH], v[CH:])
+    n = v.shape[0] // 2
+    first = lax.broadcasted_iota(jnp.int32, (n, W), 1) < W // 2
+    return jnp.where(first, v[:n], v[n:])
+
+
+def as_row(v):
+    return jnp.broadcast_to(v, (v.shape[0], W)).T[:8]
 
 
 def fold(v, op):
@@ -272,11 +281,11 @@
 def decoder_kernel(x_in, dy, wq, wo, w1, w2, ws,
                    h_out, g_in, o_w1, o_w2, o_q, o_o, o_sm,
                    wsv, wqv, w1v, w2v, wov, kv, xs, xm, qs, os_, lses, scores, acc, lsum,
-                   gcur, gm, dkv, pk, h1s, dqkvs, gms, h2p, dprep, ap, dq_acc, xm_far, g_far,
+                   gcur, gm, dkv, pk, h1s, dqkvs, gms, h2p, dprep, ap, dq_acc, xm_far, g_far, g_half,
                    a_w1, a_w2, a_q, a_o, d_w1, d_w2, d_q, d_o, y_w1, y_w2, y_q, y_o, sm, rsm,
                    part, lbuf, hbuf, fin, s1, s2, r_l, r_h, r_f, og, gs_a, gs_b, gs_c, gr_a, gr_b,
                    x_sem, wz_s, wz_r, w_local, w_send, w_recv, w_fwd, kv_s, kv_r, ho_s, ho_r,
-                   dy_sem, dk_s, dk_r, gi_s, gi_r, d_s, d_r, y_s, y_r, o_sem, sm_s, sm_r, xf_s, xf_r, gf_s, gf_r):
+                   dy_sem, dk_s, dk_r, gi_s, gi_r, d_s, d_r, y_s, y_r, o_sem, sm_s, sm_r, xf_s, xf_r, gf_s, gf_r, gh_r, gx):
     at = Place()
     gather = LineGather(at, og, gs_a, gs_b, gs_c, gr_a, gr_b)
     line = LineSum(at, gather, part, lbuf, hbuf, fin, s1, s2, r_l, r_h, r_f)
@@ -321,6 +330,13 @@
     for j in range(NJ):
         local(dy.at[y, at.rows_of(j)], gcur.at[chunk(j)], dy_sem.at[j])
 
+    def weights_on(s, group):
+        @when((y != s // 2) & (c == s % 2))
+        def _():
+            for k in group:
+                wait_dma(w_vm[k].at[s], w_recv.at[s, k])
+                send(w_vm[k].at[s], w_vm[k].at[s], w_fwd.at[k], w_recv.at[s, k], at.mate)
+
     def weights_ready(s, group):
         @when(p == s)
         def _():
@@ -328,16 +344,11 @@
                 if k < 4:
                     wait_dma(w_vm[k].at[p], w_local.at[k])
 
-        @when(p != s)
+        @when((p != s) & ((y == s // 2) | (c != s % 2)))
         def _():
             for k in group:
                 wait_dma(w_vm[k].at[s], w_recv.at[s, k])
 
-        @when((y != s // 2) & (c == s % 2))
-        def _():
-            for k in group:
-                send(w_vm[k].at[s], w_vm[k].at[s], w_fwd.at[k], w_recv.at[s, k], at.mate)
-
     def send_home(l, src, dst, ssem, rsem):
         @when(p == l)
         def _():
@@ -347,6 +358,7 @@
         def _():
             send(src, dst, ssem, rsem.at[p], {"pp": l})
 
+    weights_on(0, group_a)
     weights_ready(0, group_a)
 
     def finish_y(l, j):
@@ -361,64 +373,79 @@
         xs[l + 1, rows, :] = out
         send_home(l, xs.at[l + 1, rows], h_out.at[y, at.rows_of(j)], ho_s.at[j], ho_r)
 
-    def attn_op(l, jj, odd):
-        j = 2 * jj + odd
-        rows = chunk(j)
+    def query_places(shape, axis, odd):
+        return lax.broadcasted_iota(jnp.int32, shape, axis) % CH + (KB * odd + CH * ((c + odd) % 2))
+
+    def tail_keys(jj, odd):
+        return pl.ds(pl.multiple_of(jj * WIDE, WIDE), KB * (1 + odd))
+
+    def attn_pair(l, jj):
+        rows = pair(jj)
+        both = (2 * jj, 2 * jj + 1)
 
         @when(l == 0)
         def _():
-            wait_dma(xs.at[0, rows], x_sem.at[j])
+            for j in both:
+                wait_dma(xs.at[0, chunk(j)], x_sem.at[j])
 
         @when(l > 0)
         def _():
-            finish_y(l - 1, j)
+            for j in both:
+                finish_y(l - 1, j)
 
         small = wsv[l].astype(F32)
         xhat, _ = ln_stats(xs[l, rows, :].astype(F32))
         h1 = (xhat * row(small, GAIN1) + row(small, SHIFT1)).astype(BF)
         qkv = (nt(h1, wqv[l]) + row(small, BQKV)[:, :QKV]).astype(BF)
-        q = qkv[:, :W]
-        mine = at.rows_of(j)
-        kv[l, mine, :] = qkv[:, W:]
-        send(kv.at[l, mine], kv.at[l, mine], kv_s.at[j], kv_r.at[j], at.mate)
-        qs[l, rows, :] = q
-        q2 = head_stack(q * jnp.asarray(0.125, BF))
-
-        def pass_one(kb, best):
+        for k, j in enumerate(both):
+            kv[l, at.rows_of(j), :] = qkv[k * CH:(k + 1) * CH, W:]
+        for j in both:
+            mine = kv.at[l, at.rows_of(j)]
+            send(mine, mine, kv_s.at[j], kv_r.at[j], at.mate)
+        qs[l, rows, :] = qkv[:, :W]
+        for odd in range(2):
+            attend(l, jj, odd)
+
+    def attend(l, jj, odd):
+        j = 2 * jj + odd
+        rows = chunk(j)
+        q2 = head_stack(qs[l, rows, :] * jnp.asarray(0.125, BF))
+        lsum[...] = jnp.full_like(lsum, MASKED)
+
+        def pass_one(kb):
             s = nt(q2, kv[l, blk(kb, WIDE), 0:W])
             scores[kb] = s
-            return jnp.maximum(best, fold(s, jnp.maximum))
-
-        best = lax.fori_loop(0, jj, pass_one, jnp.full((KB, W), MASKED, F32))
-        wait_dma(kv.at[l, mine], kv_r.at[j])
-        width = KB * (1 + odd)
-        tail = pl.ds(pl.multiple_of(jj * WIDE, WIDE), width)
+            lsum[...] = jnp.maximum(lsum[...], fold(s, jnp.maximum))
+
+        loop(jj, pass_one)
+        wait_dma(kv.at[l, at.rows_of(j)], kv_r.at[j])
+        tail = tail_keys(jj, odd)
         s = nt(q2, kv[l, tail, 0:W])
-        pos = lax.broadcasted_iota(jnp.int32, (KB, width), 0) % CH + (KB * odd + CH * ((c + odd) % 2))
-        s = jnp.where(pos >= lax.broadcasted_iota(jnp.int32, (KB, width), 1), s, MASKED)
-        scores[jj, :, 0:width] = s
-        top = jnp.max(jnp.maximum(best, fold(s, jnp.maximum)), axis=-1, keepdims=True)
-        acc[...] = jnp.zeros_like(acc)
-        lsum[...] = jnp.zeros_like(lsum)
+        s = jnp.where(query_places(s.shape, 0, odd) >= lax.broadcasted_iota(jnp.int32, s.shape, 1), s, MASKED)
+        top = jnp.max(jnp.maximum(lsum[...], fold(s, jnp.maximum)), axis=-1, keepdims=True)
 
         def weigh(s, keys):
             e = jnp.exp(s - top)
-            lsum[...] += fold(e, jnp.add)
-            acc[...] += nn(e.astype(BF), kv[l, keys, W:])
-
-        loop(jj, lambda kb: weigh(scores[kb], blk(kb, WIDE)))
-        weigh(scores[jj, :, 0:width], tail)
+            return fold(e, jnp.add), nn(e.astype(BF), kv[l, keys, W:])
+
+        lsum[...], acc[...] = weigh(s, tail)
+
+        def pass_two(kb):
+            more, part_o = weigh(scores[kb], blk(kb, WIDE))
+            lsum[...] += more
+            acc[...] += part_o
+
+        loop(jj, pass_two)
         den = jnp.sum(lsum[...], axis=-1, keepdims=True)
         o = head_merge(acc[...] / den).astype(BF)
         os_[l, rows, :] = o
-        lses[l, blk(j, 8), :] = jnp.broadcast_to(top + jnp.log(den), (KB, W)).T[:8]
+        lses[l, blk(j, 8), :] = as_row(top + jnp.log(den))
         gather.emit(j, o)
         line.serve(SLOTS * l + j)
 
     def mlp_op(l, j):
         rows = chunk(j)
         small = wsv[l].astype(F32)
-        gather.sent(j)
         mid = (xs[l, rows, :].astype(F32) + nn(gather.get(j), wov[l]) + row(small, BOUT)).astype(BF)
         xm[l, rows, :] = mid
 
@@ -430,36 +457,45 @@
         h2 = (xhat * row(small, GAIN2) + row(small, SHIFT2)).astype(BF)
         u = nn(h2, w1v[l]) + row(small, BFC1)
         a = 0.5 * u * (1.0 + jnp.tanh(GELU_C * (u + GELU_A * u * u * u)))
+        gather.sent(j)
         line.emit(SLOTS * l + NJ + j, nn(a.astype(BF), w2v[l]))
 
     def forward_layer(l):
-        def attn_pair(jj):
+        def attn_step(jj):
             with jax.named_scope("attn"):
-                attn_op(l, jj, 0)
-            with jax.named_scope("attn"):
-                attn_op(l, jj, 1)
+                attn_pair(l, jj)
 
             @when((l == 0) & (jj == 1))
             def _():
                 spread_out_proj()
 
-            @when((l == 0) & (jj == PAIRS - 2) & (c == 1))
-            def _():
-                spread(every, 1, at.across)
-
-        loop(PAIRS, attn_pair)
-
-        @when(l == 0)
-        def _():
-            weights_ready(0, group_m)
+            @when((l < 2) & (jj == 2))
+            def _():
+                weights_on(l, group_m)
+
+
+        loop(PAIRS, attn_step)
+
+        @when((l == 0) & (c == 1))
+        def _():
+            spread(every, 1, at.across)
+
+        @when(l < 2)
+        def _():
+            weights_ready(l, group_m)
 
         def mlp_step(j):
             with jax.named_scope("mlp"):
                 mlp_op(l, j)
 
-            @when((j == NJ - 2) & (l < LAYERS - 1))
-            def _():
-                weights_ready(l + 1, every)
+            for when_j, step in ((3, weights_on), (NJ - 2, weights_ready)):
+                @when((j == when_j) & (l < LAYERS - 1))
+                def _():
+                    step(l + 1, group_a)
+
+                @when((j == when_j) & (l > 0) & (l < LAYERS - 1))
+                def _():
+                    step(l + 1, group_m)
 
         loop(NJ, mlp_step)
         loop(NJ, lambda j: wait_dma(kv.at[0, chunk(0)], kv_s.at[j]))
@@ -483,7 +519,7 @@
             for k, (own, mid, _, _) in enumerate(groups[g]):
                 send(own, mid, d_s.at[g, k], d_r.at[g, k], at.mate)
 
-    def grad_across(l, g):
+    def grad_across(l, g, whole=True):
         @when(c != l % 2)
         def _():
             for k, (own, _, _, _) in enumerate(groups[g]):
@@ -495,7 +531,7 @@
                 wait_dma(mid, d_r.at[g, k])
                 add_into(mid, own)
 
-                @when(y != l // 2)
+                @when((y != l // 2) & whole)
                 def _():
                     send(mid, far, y_s.at[g, k], y_r.at[g, k], at.across)
 
@@ -533,7 +569,12 @@
         def _():
             send(gcur.at[rows], g_far.at[rows], gi_s.at[j], gf_r.at[j], at.across)
 
-        @when((l != 1) | (y == 0))
+        @when((l == 0) & (y == 1))
+        def _():
+            half = blk(2 * j + at.z % 2, CH // 2)
+            send(gcur.at[half], g_half.at[c, j], gi_s.at[j], gh_r.at[c, j], {"pp": 0})
+
+        @when((l > 1) | (y == 0))
         def _():
             send_home(l, gcur.at[rows], g_in.at[y, at.rows_of(j)], gi_s.at[j], gi_r)
 
@@ -604,6 +645,15 @@
             def _():
                 send(g_far.at[rows], dst, gf_s.at[j], gi_r.at[2], at.mate)
 
+            @when(c == 0)
+            def _():
+                for core in range(2):
+                    piece = g_half.at[core, j]
+                    wait_dma(piece, gh_r.at[core, j])
+                    out = g_in.at[1, blk(4 * j + 2 * ((core + j) % 2) + at.z % 2, CH // 2)]
+                    local(piece, out, gx.at[0])
+                    send(piece, out, gx.at[1], gx.at[2], {"tp": at.z + 1 - 2 * (at.z % 2)})
+
             mlp_grads(0, j, xm_far[rows, :], g_far[rows, :])
 
             @when(i % 2 == 1)
@@ -627,6 +677,8 @@
                 add_into(mid, own)
                 local(mid, out, o_sem.at[0, k])
             loop(NJ, lambda j: wait_dma(g_far.at[chunk(j)], gf_s.at[j]))
+            for k in range(3):
+                wait_dma(g_half, gx.at[k])
 
     def attn_weight_grads(l):
         a_q[...] = tn(dqkvs[...], h1s[...])
@@ -648,31 +700,33 @@
         gms[rows, :] = gmid
         do = nt(gmid, wov[l, chunk(at.z), :]).astype(BF)
         delta = jnp.sum(head_stack(do.astype(F32) * os_[l, rows, :].astype(F32)), axis=-1, keepdims=True)
-        delta = jnp.broadcast_to(delta, (KB, W)).T[0:1]
+        delta = as_row(delta)[0:1]
         lse = lses[l, blk(j, 8), :][0:1]
         q2 = head_stack(qs[l, rows, :] * jnp.asarray(0.125, BF))
         do2 = head_stack(do)
-        dq_acc[...] = jnp.zeros_like(dq_acc)
-
-        def block(keys, width, masked):
+
+        def block(keys, masked):
             k = kv[l, keys, 0:W]
             st = nt(k, q2)
             if masked:
-                pos = lax.broadcasted_iota(jnp.int32, (width, KB), 1) % CH + (KB * odd + CH * ((c + odd) % 2))
-                st = jnp.where(pos >= lax.broadcasted_iota(jnp.int32, (width, KB), 0), st, MASKED)
+                st = jnp.where(query_places(st.shape, 1, odd) >= lax.broadcasted_iota(jnp.int32, st.shape, 0), st, MASKED)
             pt = jnp.exp(st - lse)
             dst = (pt * (nt(kv[l, keys, W:], do2) - delta)).astype(BF)
             dk = nn(dst, q2)
             dv = nn(pt.astype(BF), do2)
-            dq_acc[...] += tn(dst, k)
+            dq = tn(dst, k)
             dkv[keys, 0:W] += dk
             dkv[keys, W:] += dv
-
-        loop(jj, lambda kb: block(blk(kb, WIDE), WIDE, False))
-        width = KB * (1 + odd)
-        block(pl.ds(pl.multiple_of(jj * WIDE, WIDE), width), width, True)
+            return dq
+
+        dq_acc[...] = block(tail_keys(jj, odd), True)
+        send(dkv.at[at.mate_rows(j)], pk.at[j], dk_s.at[j], dk_r.at[j], at.mate)
+
+        def full(kb):
+            dq_acc[...] += block(blk(kb, WIDE), False)
+
+        loop(jj, full)
         dqkvs[rows, 0:W] = (head_merge(dq_acc[...]) * 0.125).astype(BF)
-        send(dkv.at[at.mate_rows(j)], pk.at[j], dk_s.at[j], dk_r.at[j], at.mate)
 
     def qkv_back(l, j):
         rows = chunk(j)
@@ -732,23 +786,18 @@
             def _():
                 grad_across(l, 0)
 
-            @when(ii > 0)
-            def _():
-                with jax.named_scope("B3"):
-                    qkv_back(l, 2 * jj + 2)
-
+            with jax.named_scope("B3"):
+                qkv_back(l, 2 * jj + 1)
             with jax.named_scope("B2"):
                 attn_back(l, jj, 0)
             with jax.named_scope("B3"):
-                qkv_back(l, 2 * jj + 1)
+                qkv_back(l, 2 * jj)
 
         loop(PAIRS, second_half)
-        qkv_back(l, 0)
         loop(NJ, lambda j: wait_dma(pk.at[j], dk_s.at[j]))
 
     loop(LAYERS, backward_layer)
     attn_weight_grads(0)
-    grad_across(0, 1)
     last = FWD + LAYERS * SLOTS - 1
 
     def finish_last(i):
@@ -762,7 +811,21 @@
 
         finish_layer(0, NJ - 1 - i)
 
+        @when(i == 2)
+        def _():
+            grad_across(0, 1, False)
+
+        @when((i > 1) & (p == 2))
+        def _():
+            rows = blk(i - 2, 64)
+            send(d_q.at[rows], y_q.at[rows], y_s.at[1, 0], y_r.at[1, 0], at.across)
+
     loop(NJ, finish_last)
+
+    @when(p == 2)
+    def _():
+        send(d_o, y_o, y_s.at[1, 1], y_r.at[1, 1], at.across)
+
     for s in range(LAYERS):
         @when(p != s)
         def _():
@@ -788,12 +851,25 @@
 
     def sent(j):
         wait_dma(gcur.at[chunk(0)], ho_s.at[j])
-        wait_dma(gcur.at[chunk(0)], gi_s.at[j])
+
+        @when(y == 0)
+        def _():
+            wait_dma(gcur.at[chunk(0)], gi_s.at[j])
+
+        @when(y == 1)
+        def _():
+            wait_dma(g_half.at[0, 0], gi_s.at[j])
 
     loop(NJ, sent)
-    for k in range(1, LAYERS):
-        wait_dma(h_out.at[0, pl.ds(0, ROWS)], ho_r.at[(p + k) % LAYERS])
-        wait_dma(g_in.at[0, pl.ds(0, ROWS)], gi_r.at[(p + k) % LAYERS])
+    for s in range(LAYERS):
+        @when(p != s)
+        def _():
+            wait_dma(h_out.at[0, pl.ds(0, ROWS)], ho_r.at[s])
+
+        @when((p != s) & ((p > 0) | (s == 1)))
+        def _():
+            wait_dma(g_in.at[0, pl.ds(0, ROWS)], gi_r.at[s])
+
     for g, items in enumerate(groups):
         for k, (_, _, far, _) in enumerate(items):
             wait_dma(far, o_sem.at[g, k])
@@ -831,15 +907,53 @@
             bf(LAYERS, SMALL, D), bf(LAYERS, QKV, D), *[bf(LAYERS, D, D)] * 3,
             bf(LAYERS, SEQ, KB), bf(LAYERS + 1, ROWS, D), bf(LAYERS, ROWS, D), bf(LAYERS, ROWS, W), bf(LAYERS, ROWS, W),
             f32(LAYERS, NJ * 8, KB), f32(PAIRS, KB, WIDE), f32(KB, W), f32(KB, W),
-            bf(ROWS, D), f32(ROWS, D), f32(SEQ, KB), f32(NJ, CH, KB), bf(ROWS, D), bf(ROWS, QKV), bf(ROWS, D), *[bf(KB, D)] * 3, f32(KB, W), bf(ROWS, D), bf(ROWS, D),
+            bf(ROWS, D), f32(ROWS, D), f32(SEQ, KB), f32(NJ, CH, KB), bf(ROWS, D), bf(ROWS, QKV), bf(ROWS, D), *[bf(KB, D)] * 3, f32(KB, W), bf(ROWS, D), bf(ROWS, D), bf(2, NJ, CH // 2, D),
             *grads, *grads, *grads, f32(LAYERS, SMALL, D), f32(LAYERS, SMALL, D),
             *[slots] * 4, *[slot_sem] * 5, bf(NJ, 4, CH, W), *[chunk_sem] * 5,
             chunk_sem, stage_sem, stage_sem, dma((len(args) - 2,)), dma((2, len(args) - 2)), dma((LAYERS, len(args) - 2)), dma((len(args) - 2,)),
             chunk_sem, chunk_sem, chunk_sem, stage_sem,
-            chunk_sem, chunk_sem, chunk_sem, chunk_sem, stage_sem, *[pair_sem] * 5, stage_sem, stage_sem, *[chunk_sem] * 4,
+            chunk_sem, chunk_sem, chunk_sem, chunk_sem, stage_sem, *[pair_sem] * 5, stage_sem, stage_sem, *[chunk_sem] * 4, dma((2, NJ)), dma((3,)),
         ],
         compiler_params=pltpu.CompilerParams(collective_id=0, has_side_effects=True, vmem_limit_bytes=67043328),
         name="decoder_layers",
+    )(*args)
+
+
+def collect_kernel(*refs):
+    count = 6
+    srcs, small, outs = refs[:count], refs[count], refs[count + 1:2 * count + 1]
+    ln, bout, bfc1, bfc2, bqkv = refs[2 * count + 1:2 * count + 6]
+    bufs, (sem_in, sem_out) = refs[2 * count + 6:3 * count + 6], refs[3 * count + 6:]
+    parts = []
+    for k, src in enumerate(srcs):
+        n = src.shape[0] // 4 if k < 2 else src.shape[0]
+        parts += [(k, pl.ds(i * n, n)) for i in range(src.shape[0] // n)]
+    for i, (k, rows) in enumerate(parts):
+        local(srcs[k].at[rows], bufs[k].at[rows], sem_in.at[i])
+    ln[...] = small[0:BOUT, :]
+    for r, out in ((BOUT, bout), (BFC1, bfc1), (BFC2, bfc2)):
+        out[...] = small[r:r + 1, :]
+    for i in range(6):
+        bqkv[i // 2, i % 2:i % 2 + 1, :] = small[BQKV:BQKV + 1, i * 64:(i + 1) * 64]
+    for i, (k, rows) in enumerate(parts):
+        wait_dma(bufs[k].at[rows], sem_in.at[i])
+        local(bufs[k].at[rows], outs[k].at[rows], sem_out.at[i])
+    for i, (k, rows) in enumerate(parts):
+        wait_dma(bufs[k].at[rows], sem_out.at[i])
+
+
+def collect(*args):
+    hbm, vmem = pl.BlockSpec(memory_space=pl.ANY), pl.BlockSpec(memory_space=pltpu.VMEM)
+    big = args[:-1]
+    shapes = [(GAIN1 + 4, D), (1, D), (1, D), (1, D), (3, 2, 64)]
+    return pl.pallas_call(
+        collect_kernel,
+        out_shape=[*(jax.ShapeDtypeStruct(a.shape, a.dtype) for a in big), *(jax.ShapeDtypeStruct(shape, F32) for shape in shapes)],
+        in_specs=[hbm] * len(big) + [vmem],
+        out_specs=[hbm] * len(big) + [vmem] * len(shapes),
+        scratch_shapes=[*(pltpu.VMEM(a.shape, a.dtype) for a in big), *[pltpu.SemaphoreType.DMA((2 * len(big),))] * 2],
+        compiler_params=pltpu.CompilerParams(vmem_limit_bytes=67043328),
+        name="collect",
     )(*args)
 
 
@@ -849,13 +963,14 @@
         wq = w_qkv.transpose(0, 1, 3, 4, 2).reshape(QKV, D)
         bq = jnp.pad(b_qkv.reshape(1, QKV), ((0, 0), (0, D - QKV)))
         ws = jnp.concatenate([ln_par.reshape(4, D), b_out, b_fc2, b_fc1, bq, jnp.zeros((8, D), BF)], axis=0)
-        h_out, g_in, d_w1, d_w2, d_q, d_o, sm = run_layers(
+        h_out, g_in, *rest = run_layers(
             x_in.reshape(2, SEQ, D), dy_out.reshape(2, SEQ, D), wq, w_out.reshape(W, D), w_fc1.reshape(D, D), w_fc2.reshape(D, D), ws)
+        h_out, g_in, d_w1, d_w2, d_q, d_o, ln, bout, bfc1, bfc2, bqkv = collect(h_out.reshape(-1, D), g_in.reshape(-1, D), *rest)
         acts = (layers, *x_in.shape)
         return (h_out.reshape(acts), g_in.reshape(acts),
-                d_q.reshape(layers, parts, heads, width, D).transpose(0, 1, 4, 2, 3), sm[BQKV, :QKV].reshape(b_qkv.shape),
-                d_o.reshape(w_out.shape), row(sm, BOUT), sm[GAIN1:BOUT].reshape(ln_par.shape),
-                d_w1.reshape(w_fc1.shape), row(sm, BFC1), d_w2.reshape(w_fc2.shape), row(sm, BFC2))
+                d_q.reshape(layers, parts, heads, width, D).transpose(0, 1, 4, 2, 3), bqkv.reshape(b_qkv.shape),
+                d_o.reshape(w_out.shape), bout, ln.reshape(ln_par.shape),
+                d_w1.reshape(w_fc1.shape), bfc1, d_w2.reshape(w_fc2.shape), bfc2)
 
     act_spec = P(NO, "dp", NO, NO)
     arg_specs = (act_spec, act_spec,

time: 439 us -> 418 us (0.952)
  local copies, waits for them, and re-layouts: 17.2 us -> 2.73 us
  Pallas kernels: 420 us -> 415 us
    pallas_call x1, Pallas kernels: 420 us -> 405 us  [run_layers(): pl.pallas_call(decoder_kernel, out_shape=[acts, acts, *(jax.ShapeDtypeStr...]
    unnamed x16 -> x0, local copies, waits for them, and re-layouts: 10.3 us -> none
    pallas_call x0 -> x1, Pallas kernels: none -> 10.1 us  [collect(): pl.pallas_call(collect_kernel, out_shape=[*(jax.ShapeDtypeStruct(a.shape,...]
where the time goes in v4:
time: 418 us
  Pallas kernels  415 us (99%)
    pallas_call x1, Pallas kernels, run_layers(): pl.pallas_call(decoder_kernel, out_shape=[acts, acts, *(jax.ShapeDtypeStr...  405 us
    pallas_call x1, Pallas kernels, collect(): pl.pallas_call(collect_kernel, out_shape=[*(jax.ShapeDtypeStruct(a.shape,...  10.1 us

profile of v4, /device:TPU:0, one launch (start us, length us, event | category | flops | bytes accessed | tf_op | source)
XLA Modules:
  0.0 418.2 jit_solution(17604171750767403676)
XLA Ops:
  0.6 0.8 reshape.83
  1.4 2.0 concatenate.3.ws
  3.4 404.7 %decoder_layers.1 = (bf16[2,2048,512]{2,1,0:T(8,128)(2,1)}, bf16[2,2048,512]{2,1,0:T(8,128)(2,1)}, f32[512,512]{1,0:T(8,128)}, f32[512,512]{1,0:T(8,128)}, f32[3...) custom-call(bf16[2,2048,512]{2,1,0:T(8,128)(2,1)} %bitcast.25, bf16[2,2048,512]{2,1,0:T(8,128)(2,1)} %bitcast.26, ...), custom_call_target="tpu_custom_call" | custom-call | tf_op jit(solution)/shard_map/decoder_layers/pallas_call | solution.py:901
  408.0 10.1 %collect.1 = (bf16[4096,512]{1,0:T(8,128)(2,1)}, bf16[4096,512]{1,0:T(8,128)(2,1)}, f32[512,512]{1,0:T(8,128)}, f32[512,512]{1,0:T(8,128)}, f32[384,512]{1,0:T(8...) custom-call(bf16[4096,512]{1,0:T(8,128)(2,1)} %bitcast.27, ...), custom_call_target="tpu_custom_call" | custom-call | tf_op jit(solution)/shard_map/collect/pallas_call | solution.py:949
  (2 shorter events, 0.0 us)

commit v5 on v4

--- a/solution.py
+++ b/solution.py
@@ -293,7 +293,7 @@
     w_hbm = (ws, wq, w1, w2)
     w_vm = (wsv, wqv, w1v, w2v, wov)
     every = range(len(w_vm))
-    at_once, group_a, group_m, out_proj = every[:4], every[:2], every[2:], every[4:]
+    at_once, group_a, mlp_w, group_m, out_proj = every[:4], every[:2], every[2:4], every[2:], every[4:]
     wo_mine = wov.at[p, chunk(at.z)]
 
     for j in range(NJ):
@@ -304,18 +304,17 @@
 
     at.enter()
 
+    for k in group_a:
+        wait_dma(w_vm[k].at[p], w_local.at[k])
+
     def spread(group, way, dev):
         for k in group:
-            src = w_hbm[k] if k < 4 else wov.at[p]
+            src = w_hbm[k] if k in mlp_w else w_vm[k].at[p]
             send(src, w_vm[k].at[p], w_send.at[way, k], w_recv.at[p, k], dev)
 
-    @when(c == 0)
-    def _():
-        spread(at_once, 1, at.across)
-
-    spread(at_once, 0, at.mate)
-    for k in range(1, 4):
-        send(wo, wo_mine, wz_s.at[k], wz_r.at[at.z], {"tp": (at.z + k) % 4})
+    def gather_out_proj():
+        for k in range(1, 4):
+            send(wo, wo_mine, wz_s.at[k], wz_r.at[at.z], {"tp": (at.z + k) % 4})
 
     def spread_out_proj():
         wait_dma(wo_mine, w_local.at[4])
@@ -324,9 +323,15 @@
             wait_dma(wo_mine, wz_s.at[k])
         spread(out_proj, 0, at.mate)
 
-        @when(c == 0)
-        def _():
-            spread(out_proj, 1, at.across)
+    @when(c == 0)
+    def _():
+        spread(every[:3], 1, at.across)
+
+    @when(p != 1)
+    def _():
+        gather_out_proj()
+
+    spread(at_once, 0, at.mate)
     for j in range(NJ):
         local(dy.at[y, at.rows_of(j)], gcur.at[chunk(j)], dy_sem.at[j])
 
@@ -341,7 +346,7 @@
         @when(p == s)
         def _():
             for k in group:
-                if k < 4:
+                if k in mlp_w:
                     wait_dma(w_vm[k].at[p], w_local.at[k])
 
         @when((p != s) & ((y == s // 2) | (c != s % 2)))
@@ -402,33 +407,30 @@
         for j in both:
             mine = kv.at[l, at.rows_of(j)]
             send(mine, mine, kv_s.at[j], kv_r.at[j], at.mate)
-        qs[l, rows, :] = qkv[:, :W]
-        for odd in range(2):
-            attend(l, jj, odd)
-
-    def attend(l, jj, odd):
-        j = 2 * jj + odd
-        rows = chunk(j)
-        q2 = head_stack(qs[l, rows, :] * jnp.asarray(0.125, BF))
+        q = qkv[:, :W]
+        qs[l, rows, :] = q
+        q4 = head_stack(q * jnp.asarray(0.125, BF))
         lsum[...] = jnp.full_like(lsum, MASKED)
 
         def pass_one(kb):
-            s = nt(q2, kv[l, blk(kb, WIDE), 0:W])
+            s = nt(q4, kv[l, blk(kb, WIDE), 0:W])
             scores[kb] = s
             lsum[...] = jnp.maximum(lsum[...], fold(s, jnp.maximum))
 
         loop(jj, pass_one)
-        wait_dma(kv.at[l, at.rows_of(j)], kv_r.at[j])
-        tail = tail_keys(jj, odd)
-        s = nt(q2, kv[l, tail, 0:W])
-        s = jnp.where(query_places(s.shape, 0, odd) >= lax.broadcasted_iota(jnp.int32, s.shape, 1), s, MASKED)
+        for j in both:
+            wait_dma(kv.at[l, at.rows_of(j)], kv_r.at[j])
+        s = nt(q4, kv[l, blk(jj, WIDE), 0:W])
+        r = lax.broadcasted_iota(jnp.int32, (WIDE, WIDE), 0) % KB
+        seen = r % CH + jnp.where(r < CH, CH * c, KB + CH * (1 - c)) >= lax.broadcasted_iota(jnp.int32, (WIDE, WIDE), 1)
+        s = jnp.where(seen, s, MASKED)
         top = jnp.max(jnp.maximum(lsum[...], fold(s, jnp.maximum)), axis=-1, keepdims=True)
 
         def weigh(s, keys):
             e = jnp.exp(s - top)
             return fold(e, jnp.add), nn(e.astype(BF), kv[l, keys, W:])
 
-        lsum[...], acc[...] = weigh(s, tail)
+        lsum[...], acc[...] = weigh(s, blk(jj, WIDE))
 
         def pass_two(kb):
             more, part_o = weigh(scores[kb], blk(kb, WIDE))
@@ -439,9 +441,12 @@
         den = jnp.sum(lsum[...], axis=-1, keepdims=True)
         o = head_merge(acc[...] / den).astype(BF)
         os_[l, rows, :] = o
-        lses[l, blk(j, 8), :] = as_row(top + jnp.log(den))
-        gather.emit(j, o)
-        line.serve(SLOTS * l + j)
+        stat = as_row(top + jnp.log(den))
+        for k, j in enumerate(both):
+            lses[l, blk(j, 8), :] = jnp.concatenate([stat[:, k * CH:(k + 1) * CH], stat[:, KB + k * CH:KB + (k + 1) * CH]], axis=1)
+        for k, j in enumerate(both):
+            gather.emit(j, o[k * CH:(k + 1) * CH])
+            line.serve(SLOTS * l + j)
 
     def mlp_op(l, j):
         rows = chunk(j)
@@ -465,20 +470,38 @@
             with jax.named_scope("attn"):
                 attn_pair(l, jj)
 
+            @when((l == 0) & (jj == 0) & (c == 0))
+            def _():
+                spread_out_proj()
+                spread(out_proj, 1, at.across)
+                spread(mlp_w[1:], 1, at.across)
+
             @when((l == 0) & (jj == 1))
             def _():
+                weights_on(0, mlp_w[:1])
+
+                @when(p == 1)
+                def _():
+                    gather_out_proj()
+
+            @when((l == 0) & (jj == 2))
+            def _():
+                weights_on(0, out_proj)
+
+            @when((l == 1) & (jj == 2))
+            def _():
+                weights_on(1, group_m)
+
+        loop(PAIRS, attn_step)
+
+        @when(l == 0)
+        def _():
+            weights_on(0, mlp_w[1:])
+
+            @when(c == 1)
+            def _():
                 spread_out_proj()
-
-            @when((l < 2) & (jj == 2))
-            def _():
-                weights_on(l, group_m)
-
-
-        loop(PAIRS, attn_step)
-
-        @when((l == 0) & (c == 1))
-        def _():
-            spread(every, 1, at.across)
+                spread(every, 1, at.across)
 
         @when(l < 2)
         def _():
@@ -629,56 +652,42 @@
             a_w1[...] += tn(h2p[...], dprep[...])
             a_w2[...] += tn(ap[...], g_ref[grads, :])
 
-    def far_mlp_weight_grads():
-        def body(i):
-            j = NJ - 1 - i
-            rows = chunk(j)
-            wait_dma(xm_far.at[rows], xf_r.at[j])
-            wait_dma(g_far.at[rows], gf_r.at[j])
-            dst = g_in.at[1, at.rows_of(j)]
-
-            @when(c == 1)
-            def _():
-                local(g_far.at[rows], dst, gi_r.at[3])
-
-            @when(c == 0)
-            def _():
-                send(g_far.at[rows], dst, gf_s.at[j], gi_r.at[2], at.mate)
-
-            @when(c == 0)
-            def _():
-                for core in range(2):
-                    piece = g_half.at[core, j]
-                    wait_dma(piece, gh_r.at[core, j])
-                    out = g_in.at[1, blk(4 * j + 2 * ((core + j) % 2) + at.z % 2, CH // 2)]
-                    local(piece, out, gx.at[0])
-                    send(piece, out, gx.at[1], gx.at[2], {"tp": at.z + 1 - 2 * (at.z % 2)})
-
-            mlp_grads(0, j, xm_far[rows, :], g_far[rows, :])
-
-            @when(i % 2 == 1)
-            def _():
-                a_w1[...] += tn(h2p[...], dprep[...])
-                a_w2[...] += tn(ap[...], g_far[blk(j // 2, KB), :])
-
-        loop(NJ, body)
+    def far_mlp_weight_grads(i):
+        j = NJ - 1 - i
+        rows = chunk(j)
+        wait_dma(xm_far.at[rows], xf_r.at[j])
+        wait_dma(g_far.at[rows], gf_r.at[j])
+        dst = g_in.at[1, at.rows_of(j)]
 
         @when(c == 1)
         def _():
-            for k, (own, mid, _, _) in enumerate(groups[0]):
-                send(own, mid, d_s.at[0, k], d_r.at[0, k], at.mate)
-            for k, (own, _, _, _) in enumerate(groups[0]):
-                wait_dma(own, d_s.at[0, k])
+            local(g_far.at[rows], dst, gi_r.at[3])
 
         @when(c == 0)
         def _():
-            for k, (own, mid, _, out) in enumerate(groups[0]):
-                wait_dma(mid, d_r.at[0, k])
-                add_into(mid, own)
-                local(mid, out, o_sem.at[0, k])
-            loop(NJ, lambda j: wait_dma(g_far.at[chunk(j)], gf_s.at[j]))
-            for k in range(3):
-                wait_dma(g_half, gx.at[k])
+            send(g_far.at[rows], dst, gf_s.at[j], gi_r.at[2], at.mate)
+
+        mlp_grads(0, j, xm_far[rows, :], g_far[rows, :])
+
+        @when(i % 2 == 1)
+        def _():
+            a_w1[...] += tn(h2p[...], dprep[...])
+            a_w2[...] += tn(ap[...], g_far[blk(j // 2, KB), :])
+
+    def swap_halves(i):
+        j = NJ - 1 - i
+        for core in range(2):
+            piece = g_half.at[core, j]
+            wait_dma(piece, gh_r.at[core, j])
+            out = g_in.at[1, blk(4 * j + 2 * ((core + j) % 2) + at.z % 2, CH // 2)]
+            local(piece, out, gx.at[0])
+            send(piece, out, gx.at[1], gx.at[2], {"tp": at.z + 1 - 2 * (at.z % 2)})
+
+    def far_sums():
+        for k, (own, mid, _, out) in enumerate(groups[0]):
+            wait_dma(mid, d_r.at[0, k])
+            add_into(mid, own)
+            local(mid, out, o_sem.at[0, k])
 
     def attn_weight_grads(l):
         a_q[...] = tn(dqkvs[...], h1s[...])
@@ -811,16 +820,31 @@
 
         finish_layer(0, NJ - 1 - i)
 
-        @when(i == 2)
+        @when(y == 0)
+        def _():
+            far_mlp_weight_grads(i)
+
+        @when((p == 0) & at.leaf & (i > 2))
+        def _():
+            swap_halves(i - 3)
+
+        first = jnp.where(at.hub, 2, 0)
+
+        @when(i == first)
         def _():
             grad_across(0, 1, False)
 
-        @when((i > 1) & (p == 2))
-        def _():
-            rows = blk(i - 2, 64)
+        @when((i >= first) & (i < first + 6) & (p == 2))
+        def _():
+            rows = blk(i - first, 64)
             send(d_q.at[rows], y_q.at[rows], y_s.at[1, 0], y_r.at[1, 0], at.across)
 
     loop(NJ, finish_last)
+
+    @when(p == 1)
+    def _():
+        for k, (own, mid, _, _) in enumerate(groups[0]):
+            send(own, mid, d_s.at[0, k], d_r.at[0, k], at.mate)
 
     @when(p == 2)
     def _():
@@ -831,53 +855,70 @@
         def _():
             send(sm.at[s], rsm.at[p], sm_s.at[s], sm_r.at[p], {"pp": s})
 
-    @when(y == 0)
+    @when((p == 0) & at.hub)
     def _():
-        far_mlp_weight_grads()
-
-    @when(y == 1)
-    def _():
-        loop(NJ, lambda j: wait_dma(xm.at[0, chunk(j)], xf_s.at[j]))
-
-    grad_home(1, 1)
-    grad_home(0, 1)
-    for s in range(LAYERS):
-        @when(p != s)
-        def _():
-            wait_dma(sm.at[s], sm_s.at[s])
-            wait_dma(rsm.at[s], sm_r.at[s])
-    rsm[p] = sm[p]
-    o_sm[...] = (rsm[0] + rsm[1]) + (rsm[2] + rsm[3])
-
-    def sent(j):
-        wait_dma(gcur.at[chunk(0)], ho_s.at[j])
-
-        @when(y == 0)
-        def _():
-            wait_dma(gcur.at[chunk(0)], gi_s.at[j])
-
-        @when(y == 1)
-        def _():
-            wait_dma(g_half.at[0, 0], gi_s.at[j])
-
-    loop(NJ, sent)
-    for s in range(LAYERS):
-        @when(p != s)
-        def _():
-            wait_dma(h_out.at[0, pl.ds(0, ROWS)], ho_r.at[s])
-
-        @when((p != s) & ((p > 0) | (s == 1)))
-        def _():
-            wait_dma(g_in.at[0, pl.ds(0, ROWS)], gi_r.at[s])
-
-    for g, items in enumerate(groups):
-        for k, (_, _, far, _) in enumerate(items):
-            wait_dma(far, o_sem.at[g, k])
+        loop(NJ - 3, swap_halves)
+
     for k in every:
         wait_dma(w_vm[k].at[0], w_send.at[0, k])
         wait_dma(w_vm[k].at[0], w_send.at[1, k])
         wait_dma(w_vm[k].at[0], w_fwd.at[k])
     line.close()
+    loop(NJ, lambda j: wait_dma(gcur.at[chunk(0)], ho_s.at[j]))
+
+    @when(p == 1)
+    def _():
+        for k, (own, mid, _, _) in enumerate(groups[0]):
+            wait_dma(own, d_s.at[0, k])
+
+    @when(p == 0)
+    def _():
+        swap_halves(NJ - 3)
+        swap_halves(NJ - 2)
+        far_sums()
+        swap_halves(NJ - 1)
+        loop(NJ, lambda j: wait_dma(g_far.at[chunk(j)], gf_s.at[j]))
+        for k in range(3):
+            wait_dma(g_half, gx.at[k])
+
+    @when(y == 1)
+    def _():
+        loop(NJ, lambda j: wait_dma(xm.at[0, chunk(j)], xf_s.at[j]))
+
+    grad_home(1, 1)
+    grad_home(0, 1)
+    for s in range(LAYERS):
+        @when(p != s)
+        def _():
+            wait_dma(sm.at[s], sm_s.at[s])
+            wait_dma(rsm.at[s], sm_r.at[s])
+    rsm[p] = sm[p]
+    sm[0] = (rsm[0] + rsm[1]) + (rsm[2] + rsm[3])
+    local(sm.at[0], o_sm, x_sem.at[0])
+
+    def sent(j):
+        @when(y == 0)
+        def _():
+            wait_dma(gcur.at[chunk(0)], gi_s.at[j])
+
+        @when(y == 1)
+        def _():
+            wait_dma(g_half.at[0, 0], gi_s.at[j])
+
+    loop(NJ, sent)
+    for s in range(LAYERS):
+        @when(p != s)
+        def _():
+            wait_dma(h_out.at[0, pl.ds(0, ROWS)], ho_r.at[s])
+
+        @when((p != s) & ((p > 0) | (s == 1)))
+        def _():
+            wait_dma(g_in.at[0, pl.ds(0, ROWS)], gi_r.at[s])
+
+    for g, items in enumerate(groups):
+        for k, (_, _, far, _) in enumerate(items):
+            wait_dma(far, o_sem.at[g, k])
+    wait_dma(sm.at[0], x_sem.at[0])
 
 
 def run_layers(*args):
@@ -902,11 +943,11 @@
         decoder_kernel,
         out_shape=[acts, acts, *(jax.ShapeDtypeStruct(shape, F32) for shape in (*grad_shapes, (SMALL, D)))],
         in_specs=[hbm] * len(args),
-        out_specs=[hbm] * 6 + [pl.BlockSpec(memory_space=pltpu.VMEM)],
+        out_specs=[hbm] * 7,
         scratch_shapes=[
             bf(LAYERS, SMALL, D), bf(LAYERS, QKV, D), *[bf(LAYERS, D, D)] * 3,
             bf(LAYERS, SEQ, KB), bf(LAYERS + 1, ROWS, D), bf(LAYERS, ROWS, D), bf(LAYERS, ROWS, W), bf(LAYERS, ROWS, W),
-            f32(LAYERS, NJ * 8, KB), f32(PAIRS, KB, WIDE), f32(KB, W), f32(KB, W),
+            f32(LAYERS, NJ * 8, KB), f32(PAIRS, WIDE, WIDE), f32(WIDE, W), f32(WIDE, W),
             bf(ROWS, D), f32(ROWS, D), f32(SEQ, KB), f32(NJ, CH, KB), bf(ROWS, D), bf(ROWS, QKV), bf(ROWS, D), *[bf(KB, D)] * 3, f32(KB, W), bf(ROWS, D), bf(ROWS, D), bf(2, NJ, CH // 2, D),
             *grads, *grads, *grads, f32(LAYERS, SMALL, D), f32(LAYERS, SMALL, D),
             *[slots] * 4, *[slot_sem] * 5, bf(NJ, 4, CH, W), *[chunk_sem] * 5,
@@ -924,22 +965,18 @@
     srcs, small, outs = refs[:count], refs[count], refs[count + 1:2 * count + 1]
     ln, bout, bfc1, bfc2, bqkv = refs[2 * count + 1:2 * count + 6]
     bufs, (sem_in, sem_out) = refs[2 * count + 6:3 * count + 6], refs[3 * count + 6:]
-    parts = []
-    for k, src in enumerate(srcs):
-        n = src.shape[0] // 4 if k < 2 else src.shape[0]
-        parts += [(k, pl.ds(i * n, n)) for i in range(src.shape[0] // n)]
-    for i, (k, rows) in enumerate(parts):
-        local(srcs[k].at[rows], bufs[k].at[rows], sem_in.at[i])
+    for k in range(count):
+        local(srcs[k], bufs[k], sem_in.at[k])
     ln[...] = small[0:BOUT, :]
     for r, out in ((BOUT, bout), (BFC1, bfc1), (BFC2, bfc2)):
         out[...] = small[r:r + 1, :]
     for i in range(6):
         bqkv[i // 2, i % 2:i % 2 + 1, :] = small[BQKV:BQKV + 1, i * 64:(i + 1) * 64]
-    for i, (k, rows) in enumerate(parts):
-        wait_dma(bufs[k].at[rows], sem_in.at[i])
-        local(bufs[k].at[rows], outs[k].at[rows], sem_out.at[i])
-    for i, (k, rows) in enumerate(parts):
-        wait_dma(bufs[k].at[rows], sem_out.at[i])
+    for k in range(count):
+        wait_dma(bufs[k], sem_in.at[k])
+        local(bufs[k], outs[k], sem_out.at[k])
+    for k in range(count):
+        wait_dma(bufs[k], sem_out.at[k])
 
 
 def collect(*args):
@@ -951,7 +988,7 @@
         out_shape=[*(jax.ShapeDtypeStruct(a.shape, a.dtype) for a in big), *(jax.ShapeDtypeStruct(shape, F32) for shape in shapes)],
         in_specs=[hbm] * len(big) + [vmem],
         out_specs=[hbm] * len(big) + [vmem] * len(shapes),
-        scratch_shapes=[*(pltpu.VMEM(a.shape, a.dtype) for a in big), *[pltpu.SemaphoreType.DMA((2 * len(big),))] * 2],
+        scratch_shapes=[*(pltpu.VMEM(a.shape, a.dtype) for a in big), *[pltpu.SemaphoreType.DMA((len(big),))] * 2],
         compiler_params=pltpu.CompilerParams(vmem_limit_bytes=67043328),
         name="collect",
     )(*args)

time: 418 us -> 411 us (0.983)
  Pallas kernels: 415 us -> 407 us
    pallas_call x1, Pallas kernels: 405 us -> 398 us  [run_layers(): pl.pallas_call(decoder_kernel, out_shape=[acts, acts, *(jax.ShapeDtypeStr...]
where the time goes in v5:
time: 411 us
  Pallas kernels  407 us (99%)
    pallas_call x1, Pallas kernels, run_layers(): pl.pallas_call(decoder_kernel, out_shape=[acts, acts, *(jax.ShapeDtypeStr...  398 us
    pallas_call x1, Pallas kernels, collect(): pl.pallas_call(collect_kernel, out_shape=[*(jax.ShapeDtypeStruct(a.shape,...  9.2 us

profile of v5, /device:TPU:0, one launch (start us, length us, event | category | flops | bytes accessed | tf_op | source)
XLA Modules:
  0.0 410.7 jit_solution(9791436135218184942)
XLA Ops:
  0.6 0.8 reshape.83
  1.4 2.0 concatenate.3.ws
  3.4 398.1 %decoder_layers.1 = (bf16[2,2048,512]{2,1,0:T(8,128)(2,1)}, bf16[2,2048,512]{2,1,0:T(8,128)(2,1)}, f32[512,512]{1,0:T(8,128)}, f32[512,512]{1,0:T(8,128)}, f32[3...) custom-call(bf16[2,2048,512]{2,1,0:T(8,128)(2,1)} %bitcast.25, bf16[2,2048,512]{2,1,0:T(8,128)(2,1)} %bitcast.26, ...), custom_call_target="tpu_custom_call" | custom-call | tf_op jit(solution)/shard_map/decoder_layers/pallas_call | solution.py:942
  401.5 9.2 %collect.1 = (bf16[4096,512]{1,0:T(8,128)(2,1)}, bf16[4096,512]{1,0:T(8,128)(2,1)}, f32[512,512]{1,0:T(8,128)}, f32[512,512]{1,0:T(8,128)}, f32[384,512]{1,0:T(8...) custom-call(bf16[4096,512]{1,0:T(8,128)(2,1)} %bitcast.27, ...), custom_call_target="tpu_custom_call" | custom-call | tf_op jit(solution)/shard_map/collect/pallas_call | solution.py:986
  (2 shorter events, 0.0 us)

commit v6 on v5

--- a/solution.py
+++ b/solution.py
@@ -28,6 +28,9 @@
 GELU_A = 0.044715
 MASKED = -1e30
 NO = None
+TP = 4
+HALF = CH // 2
+VMEM_LIMIT = 67043328
 GAIN1, SHIFT1, GAIN2, SHIFT2, BOUT, BFC2, BFC1, BQKV = range(8)
 
 
@@ -127,9 +130,9 @@
         def greet(dev):
             pl.semaphore_signal(bar, inc=1, device_id=dev, device_id_type=MESH)
 
-        for k in range(1, 4):
-            greet({"pp": (self.p + k) % 4})
-            greet({"tp": (self.z + k) % 4})
+        for k in range(1, TP):
+            greet({"pp": (self.p + k) % TP})
+            greet({"tp": (self.z + k) % TP})
 
         pl.semaphore_wait(bar, 6)
 
@@ -252,7 +255,7 @@
             wait_dma(self.buf.at[j, 0], self.r_a.at[j])
             wait_dma(self.buf.at[j, self.theirs], self.r_b.at[j])
 
-        return jnp.concatenate([self.buf[j, k] for k in range(4)], axis=1)
+        return jnp.concatenate([self.buf[j, k] for k in range(TP)], axis=1)
 
 
 def head_stack(v):
@@ -278,19 +281,21 @@
     return out
 
 
-def decoder_kernel(x_in, dy, wq, wo, w1, w2, ws,
+def decoder_kernel(x_in, dy, wq, wo, w1, w2, ln_par, b_out, b_fc2, b_fc1, b_qkv,
                    h_out, g_in, o_w1, o_w2, o_q, o_o, o_sm,
                    wsv, wqv, w1v, w2v, wov, kv, xs, xm, qs, os_, lses, scores, acc, lsum,
                    gcur, gm, dkv, pk, h1s, dqkvs, gms, h2p, dprep, ap, dq_acc, xm_far, g_far, g_half,
                    a_w1, a_w2, a_q, a_o, d_w1, d_w2, d_q, d_o, y_w1, y_w2, y_q, y_o, sm, rsm,
                    part, lbuf, hbuf, fin, s1, s2, r_l, r_h, r_f, og, gs_a, gs_b, gs_c, gr_a, gr_b,
+                   v_ln, v_bout, v_bfc2, v_bfc1, v_bqkv, v_sem,
                    x_sem, wz_s, wz_r, w_local, w_send, w_recv, w_fwd, kv_s, kv_r, ho_s, ho_r,
                    dy_sem, dk_s, dk_r, gi_s, gi_r, d_s, d_r, y_s, y_r, o_sem, sm_s, sm_r, xf_s, xf_r, gf_s, gf_r, gh_r, gx):
     at = Place()
     gather = LineGather(at, og, gs_a, gs_b, gs_c, gr_a, gr_b)
     line = LineSum(at, gather, part, lbuf, hbuf, fin, s1, s2, r_l, r_h, r_f)
     y, c, p = at.y, at.c, at.p
-    w_hbm = (ws, wq, w1, w2)
+    w_hbm = (NO, wq, w1, w2)
+    small_in = ((ln_par, v_ln), (b_out, v_bout), (b_fc2, v_bfc2), (b_fc1, v_bfc1), (b_qkv, v_bqkv))
     w_vm = (wsv, wqv, w1v, w2v, wov)
     every = range(len(w_vm))
     at_once, group_a, mlp_w, group_m, out_proj = every[:4], every[:2], every[2:4], every[2:], every[4:]
@@ -298,14 +303,21 @@
 
     for j in range(NJ):
         local(x_in.at[y, at.rows_of(j)], xs.at[0, chunk(j)], x_sem.at[j])
-    for k in at_once:
+    for k in at_once[1:]:
         local(w_hbm[k], w_vm[k].at[p], w_local.at[k])
+    for k, (src, dst) in enumerate(small_in):
+        local(src, dst, v_sem.at[k])
     local(wo, wo_mine, w_local.at[4])
 
     at.enter()
 
-    for k in group_a:
-        wait_dma(w_vm[k].at[p], w_local.at[k])
+    for k, (_, dst) in enumerate(small_in):
+        wait_dma(dst, v_sem.at[k])
+    pieces = [v_bqkv[i // 2, i % 2:i % 2 + 1, :].astype(F32) for i in range(6)]
+    bias = jnp.concatenate([*pieces, jnp.zeros((1, D - QKV), F32)], axis=1)
+    rows = [v[...].astype(F32) for v in (v_ln, v_bout, v_bfc2, v_bfc1)]
+    wsv[p] = jnp.concatenate([*rows, bias, jnp.zeros((SMALL // 2, D), F32)], axis=0).astype(BF)
+    wait_dma(wqv.at[p], w_local.at[1])
 
     def spread(group, way, dev):
         for k in group:
@@ -313,13 +325,13 @@
             send(src, w_vm[k].at[p], w_send.at[way, k], w_recv.at[p, k], dev)
 
     def gather_out_proj():
-        for k in range(1, 4):
-            send(wo, wo_mine, wz_s.at[k], wz_r.at[at.z], {"tp": (at.z + k) % 4})
+        for k in range(1, TP):
+            send(wo, wo_mine, wz_s.at[k], wz_r.at[at.z], {"tp": (at.z + k) % TP})
 
     def spread_out_proj():
         wait_dma(wo_mine, w_local.at[4])
-        for k in range(1, 4):
-            wait_dma(wo_mine, wz_r.at[(at.z + k) % 4])
+        for k in range(1, TP):
+            wait_dma(wo_mine, wz_r.at[(at.z + k) % TP])
             wait_dma(wo_mine, wz_s.at[k])
         spread(out_proj, 0, at.mate)
 
@@ -531,10 +543,10 @@
 
     def add_into(dst, src):
         def body(i):
-            rows = blk(i, 64)
+            rows = blk(i, HALF)
             dst[rows, :] += src[rows, :]
 
-        loop(dst.shape[0] // 64, body)
+        loop(dst.shape[0] // HALF, body)
 
     def grad_to_mate(l, g):
         @when(c != l % 2)
@@ -594,7 +606,7 @@
 
         @when((l == 0) & (y == 1))
         def _():
-            half = blk(2 * j + at.z % 2, CH // 2)
+            half = blk(2 * j + at.z % 2, HALF)
             send(gcur.at[half], g_half.at[c, j], gi_s.at[j], gh_r.at[c, j], {"pp": 0})
 
         @when((l > 1) | (y == 0))
@@ -679,7 +691,7 @@
         for core in range(2):
             piece = g_half.at[core, j]
             wait_dma(piece, gh_r.at[core, j])
-            out = g_in.at[1, blk(4 * j + 2 * ((core + j) % 2) + at.z % 2, CH // 2)]
+            out = g_in.at[1, blk(4 * j + 2 * ((core + j) % 2) + at.z % 2, HALF)]
             local(piece, out, gx.at[0])
             send(piece, out, gx.at[1], gx.at[2], {"tp": at.z + 1 - 2 * (at.z % 2)})
 
@@ -690,6 +702,13 @@
             local(mid, out, o_sem.at[0, k])
 
     def attn_weight_grads(l):
+        small = wsv[l].astype(F32)
+
+        def normed(jj):
+            xhat, _ = ln_stats(xs[l, pair(jj), :].astype(F32))
+            h1s[pair(jj), :] = (xhat * row(small, GAIN1) + row(small, SHIFT1)).astype(BF)
+
+        loop(PAIRS, normed)
         a_q[...] = tn(dqkvs[...], h1s[...])
         a_o[...] = tn(os_[l], gms[...])
         grad_to_mate(l, 1)
@@ -739,9 +758,6 @@
 
     def qkv_back(l, j):
         rows = chunk(j)
-        small = wsv[l].astype(F32)
-        xhat, _ = ln_stats(xs[l, rows, :].astype(F32))
-        h1s[rows, :] = (xhat * row(small, GAIN1) + row(small, SHIFT1)).astype(BF)
         wait_dma(pk.at[j], dk_r.at[j])
         dkv_own = (dkv[at.rows_of(j), :] + pk[j]).astype(BF)
         dqkvs[rows, W:] = dkv_own
@@ -752,12 +768,15 @@
     def backward_layer(n):
         l = LAYERS - 1 - n
 
+        def clear(i):
+            dkv[blk(i, HALF), :] = jnp.zeros((HALF, KB), F32)
+
         def first_half(i):
-            @when((i == 0) & (l < LAYERS - 1))
+            @when((i == 1) & (l < LAYERS - 1))
             def _():
                 attn_weight_grads(l + 1)
 
-            @when(i == 2)
+            @when(i == 4)
             def _():
                 @when(l < LAYERS - 2)
                 def _():
@@ -767,6 +786,10 @@
                 def _():
                     grad_across(l + 1, 1)
 
+            @when(i == 3)
+            def _():
+                loop(SEQ // HALF, clear)
+
             with jax.named_scope("B1"):
                 mlp_back(l, i)
 
@@ -775,11 +798,6 @@
         @when(l > 0)
         def _():
             grad_to_mate(l, 0)
-
-        def clear(i):
-            dkv[blk(i, 64), :] = jnp.zeros((64, KB), F32)
-
-        loop(SEQ // 64, clear)
 
         def second_half(ii):
             jj = PAIRS - 1 - ii
@@ -836,7 +854,7 @@
 
         @when((i >= first) & (i < first + 6) & (p == 2))
         def _():
-            rows = blk(i - first, 64)
+            rows = blk(i - first, HALF)
             send(d_q.at[rows], y_q.at[rows], y_s.at[1, 0], y_r.at[1, 0], at.across)
 
     loop(NJ, finish_last)
@@ -948,14 +966,15 @@
             bf(LAYERS, SMALL, D), bf(LAYERS, QKV, D), *[bf(LAYERS, D, D)] * 3,
             bf(LAYERS, SEQ, KB), bf(LAYERS + 1, ROWS, D), bf(LAYERS, ROWS, D), bf(LAYERS, ROWS, W), bf(LAYERS, ROWS, W),
             f32(LAYERS, NJ * 8, KB), f32(PAIRS, WIDE, WIDE), f32(WIDE, W), f32(WIDE, W),
-            bf(ROWS, D), f32(ROWS, D), f32(SEQ, KB), f32(NJ, CH, KB), bf(ROWS, D), bf(ROWS, QKV), bf(ROWS, D), *[bf(KB, D)] * 3, f32(KB, W), bf(ROWS, D), bf(ROWS, D), bf(2, NJ, CH // 2, D),
+            bf(ROWS, D), f32(ROWS, D), f32(SEQ, KB), f32(NJ, CH, KB), bf(ROWS, D), bf(ROWS, QKV), bf(ROWS, D), *[bf(KB, D)] * 3, f32(KB, W), bf(ROWS, D), bf(ROWS, D), bf(2, NJ, HALF, D),
             *grads, *grads, *grads, f32(LAYERS, SMALL, D), f32(LAYERS, SMALL, D),
-            *[slots] * 4, *[slot_sem] * 5, bf(NJ, 4, CH, W), *[chunk_sem] * 5,
-            chunk_sem, stage_sem, stage_sem, dma((len(args) - 2,)), dma((2, len(args) - 2)), dma((LAYERS, len(args) - 2)), dma((len(args) - 2,)),
+            *[slots] * 4, *[slot_sem] * 5, bf(NJ, TP, CH, W), *[chunk_sem] * 5,
+            *(pltpu.VMEM(a.shape, BF) for a in args[6:]), dma((len(args) - 6,)),
+            chunk_sem, stage_sem, stage_sem, dma((5,)), dma((2, 5)), dma((LAYERS, 5)), dma((5,)),
             chunk_sem, chunk_sem, chunk_sem, stage_sem,
             chunk_sem, chunk_sem, chunk_sem, chunk_sem, stage_sem, *[pair_sem] * 5, stage_sem, stage_sem, *[chunk_sem] * 4, dma((2, NJ)), dma((3,)),
         ],
-        compiler_params=pltpu.CompilerParams(collective_id=0, has_side_effects=True, vmem_limit_bytes=67043328),
+        compiler_params=pltpu.CompilerParams(collective_id=0, has_side_effects=True, vmem_limit_bytes=VMEM_LIMIT),
         name="decoder_layers",
     )(*args)
 
@@ -971,7 +990,7 @@
     for r, out in ((BOUT, bout), (BFC1, bfc1), (BFC2, bfc2)):
         out[...] = small[r:r + 1, :]
     for i in range(6):
-        bqkv[i // 2, i % 2:i % 2 + 1, :] = small[BQKV:BQKV + 1, i * 64:(i + 1) * 64]
+        bqkv[i // 2, i % 2:i % 2 + 1, :] = small[BQKV:BQKV + 1, i * HALF:(i + 1) * HALF]
     for k in range(count):
         wait_dma(bufs[k], sem_in.at[k])
         local(bufs[k], outs[k], sem_out.at[k])
@@ -989,7 +1008,7 @@
         in_specs=[hbm] * len(big) + [vmem],
         out_specs=[hbm] * len(big) + [vmem] * len(shapes),
         scratch_shapes=[*(pltpu.VMEM(a.shape, a.dtype) for a in big), *[pltpu.SemaphoreType.DMA((len(big),))] * 2],
-        compiler_params=pltpu.CompilerParams(vmem_limit_bytes=67043328),
+        compiler_params=pltpu.CompilerParams(vmem_limit_bytes=VMEM_LIMIT),
         name="collect",
     )(*args)
 
@@ -998,10 +1017,9 @@
     def program(x_in, dy_out, w_qkv, b_qkv, w_out, b_out, ln_par, w_fc1, b_fc1, w_fc2, b_fc2):
         layers, parts, _, heads, width = w_qkv.shape
         wq = w_qkv.transpose(0, 1, 3, 4, 2).reshape(QKV, D)
-        bq = jnp.pad(b_qkv.reshape(1, QKV), ((0, 0), (0, D - QKV)))
-        ws = jnp.concatenate([ln_par.reshape(4, D), b_out, b_fc2, b_fc1, bq, jnp.zeros((8, D), BF)], axis=0)
         h_out, g_in, *rest = run_layers(
-            x_in.reshape(2, SEQ, D), dy_out.reshape(2, SEQ, D), wq, w_out.reshape(W, D), w_fc1.reshape(D, D), w_fc2.reshape(D, D), ws)
+            x_in.reshape(2, SEQ, D), dy_out.reshape(2, SEQ, D), wq, w_out.reshape(W, D), w_fc1.reshape(D, D), w_fc2.reshape(D, D),
+            ln_par.reshape(-1, D), b_out, b_fc2, b_fc1, b_qkv.reshape(b_qkv.shape[1:]))
         h_out, g_in, d_w1, d_w2, d_q, d_o, ln, bout, bfc1, bfc2, bqkv = collect(h_out.reshape(-1, D), g_in.reshape(-1, D), *rest)
         acts = (layers, *x_in.shape)
         return (h_out.reshape(acts), g_in.reshape(acts),

time: 411 us -> 408 us (level)
  no operation moved by 1% of the time
where the time goes in v6:
time: 408 us
  Pallas kernels  407 us (100%)
    pallas_call x1, Pallas kernels, run_layers(): pl.pallas_call(decoder_kernel, out_shape=[acts, acts, *(jax.ShapeDtypeStr...  398 us
    pallas_call x1, Pallas kernels, collect(): pl.pallas_call(collect_kernel, out_shape=[*(jax.ShapeDtypeStruct(a.shape,...  9.2 us

profile of v6, /device:TPU:0, one launch (start us, length us, event | category | flops | bytes accessed | tf_op | source)
XLA Modules:
  0.0 407.7 jit_solution(2966003144310141947)
XLA Ops:
  0.6 397.8 %decoder_layers.1 = (bf16[2,2048,512]{2,1,0:T(8,128)(2,1)}, bf16[2,2048,512]{2,1,0:T(8,128)(2,1)}, f32[512,512]{1,0:T(8,128)}, f32[512,512]{1,0:T(8,128)}, f32[3...) custom-call(bf16[2,2048,512]{2,1,0:T(8,128)(2,1)} %bitcast.26, bf16[2,2048,512]{2,1,0:T(8,128)(2,1)} %bitcast.27, ...), custom_call_target="tpu_custom_call" | custom-call | tf_op jit(solution)/shard_map/decoder_layers/pallas_call | solution.py:960
  398.4 9.2 %collect.1 = (bf16[4096,512]{1,0:T(8,128)(2,1)}, bf16[4096,512]{1,0:T(8,128)(2,1)}, f32[512,512]{1,0:T(8,128)}, f32[512,512]{1,0:T(8,128)}, f32[384,512]{1,0:T(8...) custom-call(bf16[4096,512]{1,0:T(8,128)(2,1)} %bitcast.28, ...), custom_call_target="tpu_custom_call" | custom-call | tf_op jit(solution)/shard_map/collect/pallas_call | solution.py:1005

commit v7 on v6

--- a/solution.py
+++ b/solution.py
@@ -163,7 +163,7 @@
         self.serve(e)
 
     def serve(self, e):
-        for back, mine, other in ((2, self.serve_first, self.gather.serve_first), (4, self.serve_second, self.gather.serve_second)):
+        for back, mine, other in ((1, self.serve_first, self.gather.serve_first), (3, self.serve_second, self.gather.serve_second)):
             mine(e - back)
 
             @when(self.at.hub & (e >= back) & is_gather(e - back))
@@ -828,13 +828,13 @@
     last = FWD + LAYERS * SLOTS - 1
 
     def finish_last(i):
-        @when((i == 1) | (i == 2))
-        def _():
-            line.serve_first(last - 2 + i)
-
-        @when(i > 3)
-        def _():
-            line.serve_second(last - NJ + 1 + i)
+        @when((i >= 1) & (i < 2))
+        def _():
+            line.serve_first(last - 1 + i)
+
+        @when(i >= 5)
+        def _():
+            line.serve_second(last - 7 + i)
 
         finish_layer(0, NJ - 1 - i)
 

time: 408 us -> 407 us (level)
  no operation moved by 1% of the time
where the time goes in v7:
time: 407 us
  Pallas kernels  406 us (100%)
    pallas_call x1, Pallas kernels, run_layers(): pl.pallas_call(decoder_kernel, out_shape=[acts, acts, *(jax.ShapeDtypeStr...  397 us
    pallas_call x1, Pallas kernels, collect(): pl.pallas_call(collect_kernel, out_shape=[*(jax.ShapeDtypeStruct(a.shape,...  9.2 us

profile of v7, /device:TPU:0, one launch (start us, length us, event | category | flops | bytes accessed | tf_op | source)
XLA Modules:
  0.0 406.8 jit_solution(18218142351660809178)
XLA Ops:
  0.6 396.9 %decoder_layers.1 = (bf16[2,2048,512]{2,1,0:T(8,128)(2,1)}, bf16[2,2048,512]{2,1,0:T(8,128)(2,1)}, f32[512,512]{1,0:T(8,128)}, f32[512,512]{1,0:T(8,128)}, f32[3...) custom-call(bf16[2,2048,512]{2,1,0:T(8,128)(2,1)} %bitcast.26, bf16[2,2048,512]{2,1,0:T(8,128)(2,1)} %bitcast.27, ...), custom_call_target="tpu_custom_call" | custom-call | tf_op jit(solution)/shard_map/decoder_layers/pallas_call | solution.py:960
  397.6 9.2 %collect.1 = (bf16[4096,512]{1,0:T(8,128)(2,1)}, bf16[4096,512]{1,0:T(8,128)(2,1)}, f32[512,512]{1,0:T(8,128)}, f32[512,512]{1,0:T(8,128)}, f32[384,512]{1,0:T(8...) custom-call(bf16[4096,512]{1,0:T(8,128)(2,1)} %bitcast.28, ...), custom_call_target="tpu_custom_call" | custom-call | tf_op jit(solution)/shard_map/collect/pallas_call | solution.py:1005
